TPU v7x, 64 devices: a 2x2x8 block of a 4x4x8 slice. The times are simulated.
64 devices in a mesh: dp: 4 (over x, y), sp: 16 (over z, core).
Axes of the slice: x: 2, y: 2, z: 8, core: 2. Of those that a mesh axis runs over, the one named last changes fastest.
The devices are a block of a 4x4x8 slice.
Arguments:
- latent: bfloat16 [64, 32, 32, 1280], P('dp', 'sp'), parts along dimension 0
- time_emb: bfloat16 [64, 1280], P('dp'), parts along dimension 0
- context: bfloat16 [64, 77, 2048], P('dp'), parts along dimension 0
- res_conv: bfloat16 [2, 2, 3, 3, 1280, 1280], replicated
- res_time: bfloat16 [2, 1280, 1280], replicated
- res_norm: bfloat16 [2, 2, 2, 32, 40], replicated
- attn_norm: bfloat16 [2, 32, 40], replicated
- proj_inout: bfloat16 [2, 1280, 1280], replicated
- self_qkv: bfloat16 [3, 1280, 20, 64], replicated
- self_out: bfloat16 [20, 64, 1280], replicated
- cross_q: bfloat16 [1280, 20, 64], replicated
- cross_kv: bfloat16 [2, 2048, 20, 64], replicated
- cross_out: bfloat16 [20, 64, 1280], replicated
- ff_in: bfloat16 [1280, 10240], replicated
- ff_out: bfloat16 [5120, 1280], replicated
Outputs:
- output: bfloat16 [64, 32, 32, 1280], P('dp', 'sp'), parts along dimension 0
There are 4 independent parts. A program takes and returns all parts, laid end to end along the dimension named above; an argument that names none is the same for every part.
All inputs are finite; a program needn't handle non-finite values.
Results may differ from a plain program's by a relative error of at most 0.0133442.
Values are sent between devices in bfloat16 or wider.
A program may use at most 768 MiB of HBM per device.

v0:
```python
import jax
import jax.numpy as jnp
from jax import lax
from jax.sharding import PartitionSpec as P

GN_EPS = 1e-6
LN_EPS = 1e-5


def group_norm(hidden, scale_shift, elem_count):
    groups = scale_shift.shape[1]
    feat_f32 = hidden.astype(jnp.float32).reshape(hidden.shape[:-1] + (groups, -1))
    local_sums = jnp.stack([jnp.sum(feat_f32, axis=(1, 2, 4)), jnp.sum(feat_f32 * feat_f32, axis=(1, 2, 4))])
    stat_sums = lax.psum(local_sums, 'sp')
    grp_mean = stat_sums[0] / elem_count
    grp_rstd = lax.rsqrt(stat_sums[1] / elem_count - grp_mean * grp_mean + GN_EPS)
    normed = (feat_f32 - grp_mean[:, None, None, :, None]) * grp_rstd[:, None, None, :, None]
    normed = normed * scale_shift[0].astype(jnp.float32) + scale_shift[1].astype(jnp.float32)
    return normed.reshape(hidden.shape)


def conv_band(act_in, kernel, num_bands):
    to_next = [(source, source + 1) for source in range(num_bands - 1)]
    to_prev = [(source + 1, source) for source in range(num_bands - 1)]
    top_halo = lax.ppermute(act_in[:, -1:], 'sp', to_next)
    bottom_halo = lax.ppermute(act_in[:, :1], 'sp', to_prev)
    padded = jnp.concatenate([top_halo, act_in, bottom_halo], axis=1)
    return lax.conv_general_dilated(padded, kernel, (1, 1), ((0, 0), (1, 1)), dimension_numbers=('NHWC', 'HWIO', 'NHWC'), preferred_element_type=jnp.float32)


def time_project(time_emb, weight):
    time_act = jax.nn.silu(time_emb.astype(jnp.float32)).astype(jnp.bfloat16)
    return jnp.dot(time_act, weight, preferred_element_type=jnp.float32)


def res_block(hidden, time_proj, kernels, norm_pair, elem_count, num_bands):
    act_one = jax.nn.silu(group_norm(hidden, norm_pair[0], elem_count)).astype(jnp.bfloat16)
    mid_act = (conv_band(act_one, kernels[0], num_bands) + time_proj[:, None, None, :]).astype(jnp.bfloat16)
    act_two = jax.nn.silu(group_norm(mid_act, norm_pair[1], elem_count)).astype(jnp.bfloat16)
    return (hidden.astype(jnp.float32) + conv_band(act_two, kernels[1], num_bands)).astype(jnp.bfloat16)


def layer_norm(tokens):
    feat_f32 = tokens.astype(jnp.float32)
    centred = feat_f32 - jnp.mean(feat_f32, axis=-1, keepdims=True)
    return (centred * lax.rsqrt(jnp.mean(centred * centred, axis=-1, keepdims=True) + LN_EPS)).astype(jnp.bfloat16)


def project(rows_flat, weight):
    return jnp.einsum('tc,chd->thd', rows_flat, weight, preferred_element_type=jnp.float32).astype(jnp.bfloat16)


def attend(queries, key_all, val_all):
    logit_scale = queries.shape[-1] ** -0.5
    logits = jnp.einsum('bqhd,bkhd->bhqk', queries, key_all, preferred_element_type=jnp.float32) * logit_scale
    row_max = jnp.max(logits, axis=-1, keepdims=True)
    weights = jnp.exp(logits - row_max)
    row_sum = jnp.sum(weights, axis=-1, keepdims=True)
    weighted = jnp.einsum('bhqk,bkhd->bhqd', weights.astype(jnp.bfloat16), val_all, preferred_element_type=jnp.float32)
    return (weighted / row_sum).astype(jnp.bfloat16)


def out_project(attended, weight):
    return jnp.einsum('bhqd,hdc->bqc', attended, weight, preferred_element_type=jnp.float32)


def transformer(hidden, context, attn_norm, proj_inout, self_qkv, self_out, cross_q, cross_kv, cross_out, ff_in, ff_out, elem_count):
    batch_size, band_rows, img_width, channels = hidden.shape
    band_shape = (batch_size, band_rows * img_width, self_qkv.shape[2], self_qkv.shape[3])
    row_count = batch_size * band_rows * img_width
    normed = group_norm(hidden, attn_norm, elem_count).astype(jnp.bfloat16).reshape(row_count, channels)
    tokens = jnp.dot(normed, proj_inout[0], preferred_element_type=jnp.float32).astype(jnp.bfloat16)
    ln_tokens = layer_norm(tokens)
    key_all = lax.all_gather(project(ln_tokens, self_qkv[1]).reshape(band_shape), 'sp', axis=1, tiled=True)
    val_all = lax.all_gather(project(ln_tokens, self_qkv[2]).reshape(band_shape), 'sp', axis=1, tiled=True)
    self_query = project(ln_tokens, self_qkv[0]).reshape(band_shape)
    self_att = out_project(attend(self_query, key_all, val_all), self_out).reshape(row_count, channels)
    tok_one = (tokens.astype(jnp.float32) + self_att).astype(jnp.bfloat16)
    ctx_key = jnp.einsum('btc,chd->bthd', context, cross_kv[0], preferred_element_type=jnp.float32).astype(jnp.bfloat16)
    ctx_val = jnp.einsum('btc,chd->bthd', context, cross_kv[1], preferred_element_type=jnp.float32).astype(jnp.bfloat16)
    cross_query = project(layer_norm(tok_one), cross_q).reshape(band_shape)
    cross_att = out_project(attend(cross_query, ctx_key, ctx_val), cross_out).reshape(row_count, channels)
    tok_two = (tok_one.astype(jnp.float32) + cross_att).astype(jnp.bfloat16)
    hidden_ff = jnp.dot(layer_norm(tok_two), ff_in, preferred_element_type=jnp.float32)
    ff_width = ff_out.shape[0]
    gated_ff = (hidden_ff[:, :ff_width] * jax.nn.gelu(hidden_ff[:, ff_width:], approximate=False)).astype(jnp.bfloat16)
    tok_three = (tok_two.astype(jnp.float32) + jnp.dot(gated_ff, ff_out, preferred_element_type=jnp.float32)).astype(jnp.bfloat16)
    block_out = hidden.reshape(row_count, channels).astype(jnp.float32) + jnp.dot(tok_three, proj_inout[1], preferred_element_type=jnp.float32)
    return block_out.astype(jnp.bfloat16).reshape(hidden.shape)


def solution(mesh):
    num_bands = mesh.shape['sp']

    def local_stage(latent, time_emb, context, res_conv, res_time, res_norm, attn_norm, proj_inout, self_qkv, self_out, cross_q, cross_kv, cross_out, ff_in, ff_out):
        elem_count = float(latent.shape[1] * num_bands * latent.shape[2] * res_norm.shape[4])
        first_out = res_block(latent, time_project(time_emb, res_time[0]), res_conv[0], res_norm[0], elem_count, num_bands)
        middle = transformer(first_out, context, attn_norm, proj_inout, self_qkv, self_out, cross_q, cross_kv, cross_out, ff_in, ff_out, elem_count)
        return res_block(middle, time_project(time_emb, res_time[1]), res_conv[1], res_norm[1], elem_count, num_bands)

    band_spec = P('dp', 'sp', None, None)
    shared = P()
    in_specs = (band_spec, P('dp', None), P('dp', None, None)) + (shared,) * 12
    return jax.shard_map(local_stage, mesh=mesh, in_specs=in_specs, out_specs=band_spec, check_vma=False)
```

profile of v0, /device:TPU:30, one launch (start us, length us, event | category | flops | bytes accessed | tf_op | source)
XLA Modules:
  0.0 1647.8 jit_solution(13548146524969062241)
XLA Ops:
  6.6 3.9 convert_reduce_fusion
  11.5 1.8 reduce_sum.185
  14.6 52.4 %psum.35 = f32[2,16,32]{2,1,0:T(8,128)S(1)} all-reduce(f32[2,16,32]{2,1,0:T(8,128)S(1)} %pad_maximum_fusion), channel_id=1, replica_groups=mesh['dp'=4,'sp'=16] {'sp'}, use_global_device_ids=true, to_apply=%region_4.5 | all-reduce | flops 1024 | bytes 8192 | tf_op jit(solution)/shard_map/psum | solution.py:14
  68.2 1.5 slice_convert_fusion.1
  74.2 3.9 fusion.85
  78.2 1.5 copy-done.7
  79.7 1.7 fusion.299
  81.3 2.4 collective-permute-start
  86.4 2.5 fusion.164
  88.9 37.2 %convert_reduce_fusion.5 = (f32[16,1280]{1,0:T(8,128)}, f32[16,1280]{1,0:T(8,128)}, bf16[16,2,32,1280]{3,0,2,1:T(8,128)(2,1)}) fusion(f32[16,1280]{1,0:T(8,128)S(1)} %fusion.164, bf16[2,2,3,3,1280,1280]{5,4,3,2,1,0:T(8,128)(2,1)} %param.18, bf16[16,1,32,1280]{3,0,2,1:T(8,128)(2,1)} %collective-permute-done.1, bf16[16,2,32,1280]{3,0,2,1:T(8,128)(2,1)} %copy-done.7, ...), kind=kOutput, calls=%fused_computation.66 | convolution fusion | flops 29593395200 | bytes 37601280 | tf_op jit(solution)/shard_map/conv_general_dilated | solution.py:28
  130.5 57.9 %psum.36 = f32[2,16,32]{2,1,0:T(8,128)S(1)} all-reduce(f32[2,16,32]{2,1,0:T(8,128)S(1)} %pad_maximum_fusion.1), channel_id=1, replica_groups=mesh['dp'=4,'sp'=16] {'sp'}, use_global_device_ids=true, to_apply=%region_9.10 | all-reduce | flops 1024 | bytes 8192 | tf_op jit(solution)/shard_map/psum | solution.py:14
  191.5 3.6 fusion.61
  195.1 1.5 copy-done.5
  196.6 1.7 fusion.298
  198.3 2.4 collective-permute-start.2
  200.7 1.3 collective-permute-start.3
  202.2 7.7 fusion.295
  211.1 36.8 %convert_reduce_fusion.6 = (f32[16,1280]{1,0:T(8,128)}, f32[16,1280]{1,0:T(8,128)}, bf16[16,2,32,1280]{3,0,2,1:T(8,128)(2,1)}) fusion(bf16[2,2,3,3,1280,1280]{5,4,3,2,1,0:T(8,128)(2,1)} %param.18, bf16[16,1,32,1280]{3,0,2,1:T(8,128)(2,1)} %collective-permute-done.3, bf16[16,2,32,1280]{3,0,2,1:T(8,128)(2,1)S(1)} %copy-done.6, ...), kind=kOutput, calls=%fused_computation.159 | convolution fusion | flops 29594705920 | bytes 40140800 | tf_op jit(solution)/shard_map/conv_general_dilated | solution.py:28
  252.3 53.5 %psum.37 = f32[2,16,32]{2,1,0:T(8,128)S(1)} all-reduce(f32[2,16,32]{2,1,0:T(8,128)S(1)} %pad_maximum_fusion.2), channel_id=1, replica_groups=mesh['dp'=4,'sp'=16] {'sp'}, use_global_device_ids=true, to_apply=%region_14.15 | all-reduce | flops 1024 | bytes 8192 | tf_op jit(solution)/shard_map/psum | solution.py:14
  309.0 2.8 add_convert_fusion.2
  312.5 6.0 convert_reduce_fusion.4
  319.4 3.8 fusion.288
  323.2 1.9 convert_element_type.193
  325.1 7.8 reshape.282
  332.9 8.8 copy.46
  341.8 6.5 fusion.286
  348.4 1.9 convert_element_type.195
  350.3 8.2 reshape.283
  358.5 10.4 copy.48
  370.9 17.8 %fusion.152 = bf16[16,77,20,64]{3,0,2,1:T(8,128)(2,1)} fusion(bf16[2,2048,20,64]{1,3,2,0:T(8,128)(2,1)} %param.26, bf16[16,77,2048]{2,0,1:T(8,128)(2,1)} %param.17), kind=kOutput, calls=%fused_computation.162 | convolution fusion | flops 6460805120 | bytes 13443072 | tf_op jit(solution)/shard_map/btc,chd->bthd/dot_general | solution.py:80
  388.7 3.5 copy.44
  393.3 3.8 fusion.290
  397.1 1.9 convert_element_type.192
  399.0 7.8 reshape.281
  406.8 350.2 %all-gather.3.cloned.1.call-done = bf16[16,1024,20,64]{3,1,2,0:T(8,128)(2,1)} async-done(((bf16[16,64,20,64]{3,1,2,0:T(8,128)(2,1)}), bf16[16,1024,20,64]{3,1,2,0:T(8,128)(2,1)}) %all-gather.3.cloned.1.call-update) | async-done | bytes 41943056 | tf_op jit(solution)/shard_map/all_gather | solution.py:74
  757.0 64.7 %multiply_reduce_fusion = (f32[16,20,64]{2,1,0:T(8,128)S(1)}, f32[16,20,64,1024]{3,2,1,0:T(8,128)}) fusion(bf16[16,1024,20,64]{3,1,2,0:T(8,128)(2,1)} %all-gather.3.cloned.1.call-done, bf16[16,64,20,64]{1,0,3,2:T(8,128)(2,1)} %reshape.281), kind=kOutput, calls=%fused_computation.3 | convolution fusion | flops 2726277120 | bytes 128532480 | tf_op jit(solution)/shard_map/bqhd,bkhd->bhqk/dot_general | solution.py:55
  821.7 26.9 %fusion.2 = f32[16,20,64]{2,1,0:T(8,128)} fusion(f32[16,20,64,1024]{3,2,1,0:T(8,128)} %get-tuple-element.45, f32[16,20,64]{2,1,0:T(8,128)S(1)} %get-tuple-element.44), kind=kLoop, calls=%fused_computation.4 | loop fusion | flops 62894080 | bytes 84049920 | tf_op jit(solution)/shard_map/reduce_sum | solution.py:58
  848.6 316.7 %all-gather.5.cloned.1.call-done = bf16[16,1024,20,64]{3,0,2,1:T(8,128)(2,1)} async-done(((bf16[16,64,20,64]{3,0,2,1:T(8,128)(2,1)}), bf16[16,1024,20,64]{3,0,2,1:T(8,128)(2,1)}) %all-gather.5.cloned.1.call-update) | async-done | bytes 41943056 | tf_op jit(solution)/shard_map/all_gather | solution.py:75
  1165.3 59.0 %divide_convert_fusion.1 = bf16[16,20,64,64]{3,2,1,0:T(8,128)(2,1)} fusion(bf16[16,1024,20,64]{3,0,2,1:T(8,128)(2,1)} %all-gather.5.cloned.1.call-done, f32[16,20,64,1024]{3,2,1,0:T(8,128)} %get-tuple-element.45, f32[16,20,64]{2,1,0:T(8,128)S(1)} %get-tuple-element.44, f32[16,20,64]{2,1,0:T(8,128)} %fusion.2), kind=kOutput, calls=%fused_computation.43 | convolution fusion | flops 2749890560 | bytes 128614400 | tf_op jit(solution)/shard_map/bhqk,bkhd->bhqd/dot_general | solution.py:59
  1224.3 6.9 fusion.161
  1232.7 3.8 fusion.170
  1237.0 5.0 reshape.285
  1242.0 25.9 %multiply_reduce_fusion.2 = (f32[16,20,64]{2,1,0:T(8,128)S(1)}, f32[16,20,64,77]{3,2,1,0:T(8,128)}) fusion(bf16[16,77,2048,1]{2,0,1,3:T(8,128)(2,1)} %bitcast.240, bf16[2,2048,20,64]{1,3,2,0:T(8,128)(2,1)} %param.26, bf16[16,64,20,64]{1,0,3,2:T(8,128)(2,1)} %reshape.285), kind=kOutput, calls=%fused_computation.45 | convolution fusion | flops 6665789440 | bytes 21921792 | tf_op jit(solution)/shard_map/bqhd,bkhd->bhqk/dot_general | solution.py:55
  1267.9 8.4 fusion.32
  1276.3 19.9 %fusion.131 = f32[16,64,1280,1]{2,1,3,0:T(8,128)} fusion(f32[16,20,64]{2,1,0:T(8,128)S(1)} %fusion.32, bf16[20,64,1280]{2,1,0:T(8,128)(2,1)} %param.27, bf16[16,77,20,64]{3,0,2,1:T(8,128)(2,1)} %fusion.152, f32[16,20,64,77]{3,2,1,0:T(8,128)} %get-tuple-element.47, f32[16,20,64]{2,1,0:T(8,128)S(1)} %get-tuple-element.46), kind=kOutput, calls=%fused_computation.157 | convolution fusion | flops 3564646400 | bytes 18145280 | tf_op jit(solution)/shard_map/bhqd,hdc->bqc/dot_general | solution.py:64
  1296.2 3.1 convert_reduce_fusion.2
  1300.2 35.3 %fusion.172 = f32[1024,10240]{1,0:T(8,128)} fusion(bf16[1280,10240]{1,0:T(8,128)(2,1)} %param.28, bf16[1024,1280]{1,0:T(8,128)(2,1)S(1)} %get-tuple-element.16, f32[1024]{0:T(1024)S(1)} %add_rsqrt_fusion, f32[1024]{0:T(1024)S(1)} %broadcast_multiply_fusion), kind=kOutput, calls=%fused_computation.177 | convolution fusion | flops 26848788480 | bytes 70787072 | tf_op jit(solution)/shard_map/dot_general | solution.py:84
  1335.4 66.7 %fusion.64.clone.5 = bf16[1024,1280]{1,0:T(8,128)(2,1)S(1)} fusion(bf16[1024,1280]{1,0:T(8,128)(2,1)S(1)} %get-tuple-element.16, bf16[5120,1280]{1,0:T(8,128)(2,1)} %param.29, f32[1024,10240]{1,0:T(8,128)} %fusion.172), kind=kOutput, calls=%fused_computation.93.clone.clone.clone.2 | convolution fusion | flops 13771735040 | bytes 60293120 | tf_op jit(solution)/shard_map/dot_general | solution.py:87
  1402.1 7.4 fusion.147
  1409.5 16.0 reshape.295
  1425.6 9.0 fusion.292
  1434.6 46.9 %psum.38 = f32[2,16,32]{2,1,0:T(8,128)S(1)} all-reduce(f32[2,16,32]{2,1,0:T(8,128)S(1)} %pad_maximum_fusion.3), channel_id=1, replica_groups=mesh['dp'=4,'sp'=16] {'sp'}, use_global_device_ids=true, to_apply=%region_27.28 | all-reduce | flops 1024 | bytes 8192 | tf_op jit(solution)/shard_map/psum | solution.py:14
  1482.1 6.3 multiply_convert_fusion
  1488.5 1.7 fusion.297
  1490.1 2.4 collective-permute-start.4
  1494.0 2.5 fusion.157
  1497.4 35.8 %convert_reduce_fusion.1 = (f32[16,1280]{1,0:T(8,128)S(1)}, f32[16,1280]{1,0:T(8,128)S(1)}, bf16[16,2,32,1280]{3,0,2,1:T(8,128)(2,1)}) fusion(f32[16,1280]{1,0:T(8,128)S(1)} %fusion.157, bf16[2,2,3,3,1280,1280]{5,4,3,2,1,0:T(8,128)(2,1)} %param.18, bf16[16,1,32,1280]{3,0,2,1:T(8,128)(2,1)} %collective-permute-done.5, ...), kind=kOutput, calls=%fused_computation.54 | convolution fusion | flops 29593395200 | bytes 37601280 | tf_op jit(solution)/shard_map/conv_general_dilated | solution.py:28
  1533.9 57.9 %psum.39 = f32[2,16,32]{2,1,0:T(8,128)S(1)} all-reduce(f32[2,16,32]{2,1,0:T(8,128)S(1)} %pad_maximum_fusion.4), channel_id=1, replica_groups=mesh['dp'=4,'sp'=16] {'sp'}, use_global_device_ids=true, to_apply=%region_32.33 | all-reduce | flops 1024 | bytes 8192 | tf_op jit(solution)/shard_map/psum | solution.py:14
  1592.4 3.7 fusion.74
  1596.3 1.4 collective-permute-start.6
  1597.7 1.3 collective-permute-start.7
  1600.2 2.4 collective-permute-done.7
  1602.6 35.8 %add_convert_fusion = bf16[16,2,32,1280]{3,0,2,1:T(8,128)(2,1)S(1)} fusion(f32[16,2,32,1280]{3,2,1,0:T(8,128)S(1)} %bitcast.221, bf16[2,2,3,3,1280,1280]{5,4,3,2,1,0:T(8,128)(2,1)} %param.18, bf16[16,1,32,1280]{3,0,2,1:T(8,128)(2,1)S(1)} %collective-permute-done.7, bf16[16,2,32,1280]{3,0,2,1:T(8,128)(2,1)S(1)} %fusion.74, ...), kind=kOutput, calls=%fused_computation.146 | convolution fusion | flops 29588193280 | bytes 42598400 | tf_op jit(solution)/shard_map/conv_general_dilated | solution.py:28
  1638.5 2.3 copy.55
  (144 shorter events, 40.5 us)
Async XLA Ops:
  6.5 1226.2 %copy-start = (bf16[1280,20,64]{0,2,1:T(8,128)(2,1)S(1)}, bf16[1280,20,64]{0,2,1:T(8,128)(2,1)}, u32[]{:S(2)}) copy-start(bf16[1280,20,64]{0,2,1:T(8,128)(2,1)} %param.25) | copy-start | bytes 9830404
  6.6 750.4 %all-gather.3.cloned.1.call-start = ((), (), s32[]{:S(2)}) async-start(), calls=%async_computation | async-start | bytes 89128960 | tf_op jit(solution)/shard_map/all_gather | solution.py:74
  74.2 10.8 copy-start.19
  74.2 12.2 copy-start.25
  78.2 1.5 copy-start.7
  81.3 7.5 collective-permute-start
  83.7 5.2 collective-permute-start.1
  88.9 102.6 %copy-start.20 = (f32[1280]{0:T(1024)S(1)}, f32[1280]{0:T(1024)}, u32[]{:S(2)}) copy-start(f32[1280]{0:T(1024)} %reshape.289) | copy-start | bytes 15364
  88.9 102.6 %copy-start.21 = (f32[1280]{0:T(1024)S(1)}, f32[1280]{0:T(1024)}, u32[]{:S(2)}) copy-start(f32[1280]{0:T(1024)} %reshape.290) | copy-start | bytes 15364
  191.5 10.5 copy-start.24
  195.1 1.5 copy-start.5
  198.3 11.6 collective-permute-start.2
  200.7 9.2 collective-permute-start.3
  202.2 7.7 copy-start.4
  202.2 8.9 copy-start.6
  312.5 6.9 copy-start.14
  318.5 4.7 copy-start.9
  341.8 823.5 %all-gather.5.cloned.1.call-start = ((), (), s32[]{:S(2)}) async-start(), calls=%async_computation.1 | async-start | bytes 89128960 | tf_op jit(solution)/shard_map/all_gather | solution.py:75
  368.9 0.7 copy-start.18
  368.9 1.4 copy-start.17
  370.9 17.8 %copy-start.8 = (bf16[16,2,32,1280]{3,0,2,1:T(8,128)(2,1)S(1)}, bf16[16,2,32,1280]{3,0,2,1:T(8,128)(2,1)}, u32[]{:S(2)}) copy-start(bf16[16,2,32,1280]{3,0,2,1:T(8,128)(2,1)} %get-tuple-element.41) | copy-start | bytes 7864324
  388.7 3.5 copy-start.10
  388.7 4.6 copy-start.13
  1224.3 6.9 copy-start.11
  1231.9 4.7 copy-start.2
  1276.2 19.9 %copy-start.3 = (bf16[1024,1280]{1,0:T(8,128)(2,1)S(1)}, bf16[1024,1280]{1,0:T(8,128)(2,1)}, u32[]{:S(2)}) copy-start(bf16[1024,1280]{1,0:T(8,128)(2,1)} %copy-done.2) | copy-start | bytes 7864324
  1335.4 66.7 %copy-start.12 = (f32[16,2,32,1280]{3,2,1,0:T(8,128)S(1)}, f32[16,2,32,1280]{3,2,1,0:T(8,128)}, u32[]{:S(2)}) copy-start(f32[16,2,32,1280]{3,2,1,0:T(8,128)} %copy.44) | copy-start | bytes 15728644
  1425.6 56.5 %copy-start.22 = (f32[1280]{0:T(1024)S(1)}, f32[1280]{0:T(1024)}, u32[]{:S(2)}) copy-start(f32[1280]{0:T(1024)} %reshape.296) | copy-start | bytes 15364
  1425.6 56.5 %copy-start.23 = (f32[1280]{0:T(1024)S(1)}, f32[1280]{0:T(1024)}, u32[]{:S(2)}) copy-start(f32[1280]{0:T(1024)} %reshape.297) | copy-start | bytes 15364
  1482.1 11.7 copy-start.16
  1482.1 11.8 copy-start.15
  1482.1 11.9 copy-start.26
  1490.1 6.4 collective-permute-start.4
  1492.5 4.9 collective-permute-start.5
  1592.4 10.2 slice-start
  1592.4 10.2 slice-start.1
  1596.3 4.0 collective-permute-start.6
  1597.7 5.0 collective-permute-start.7
  1602.6 38.1 %copy-start.1 = (bf16[1280,20,64]{0,2,1:T(8,128)(2,1)S(1)}, bf16[1280,20,64]{0,2,1:T(8,128)(2,1)}, u32[]{:S(2)}) copy-start(bf16[1280,20,64]{0,2,1:T(8,128)(2,1)} %param.25) | copy-start | bytes 9830404
Sparse Core Ops, SparseCore 0:
  341.9 415.0 all-gather.2
  758.6 406.6 all-gather.4
where the time goes:
time: 1680 us; the launch traced here: 1650 us
  waiting for transfers between devices  672 us (40%)
  matrix products  478 us (28%)
  blocking collectives  269 us (16%)
  local copies, waits for them, and re-layouts  111 us (7%)
  other arithmetic  90.8 us (5%)
    all_gather x1, waiting for transfers between devices, transformer(): lax.all_gather(project(ln_tokens, self_qkv[1]).reshape(band_shape), 'sp',...  350 us
    all_gather x1, waiting for transfers between devices, transformer(): lax.all_gather(project(ln_tokens, self_qkv[2]).reshape(band_shape), 'sp',...  317 us
    psum x5, blocking collectives, group_norm(): stat_sums = lax.psum(local_sums, 'sp')  269 us
    conv_general_dilated x4, matrix products, conv_band(): lax.conv_general_dilated(padded, kernel, (1, 1), ((0, 0), (1, 1)), dimens...  146 us
    dot_general x2, matrix products, attend(): jnp.einsum('bqhd,bkhd->bhqk', queries, key_all, preferred_element_type=jn...  90.5 us
    dot_general x1, matrix products, transformer(): jnp.dot(gated_ff, ff_out, preferred_element_type=jnp.float32)  66.7 us
    dot_general x1, matrix products, attend(): jnp.einsum('bhqk,bkhd->bhqd', weights.astype(jnp.bfloat16), val_all, pref...  59 us
    reduce_sum x2, other arithmetic, attend(): row_sum = jnp.sum(weights, axis=-1, keepdims=True)  35.3 us
  transfers between devices with their start and end apart: 10, of which 5 were waited for; matrix products, arithmetic and copies ran while one was open for 10% of the time, Pallas kernels for 0%

commit v1 on v0

v1 whole, which is shorter than its diff:
```python
import functools

import jax
import jax.numpy as jnp
from jax import lax
from jax.experimental import pallas as pl
from jax.experimental.pallas import tpu as pltpu
from jax.sharding import PartitionSpec as P

BF16 = jnp.bfloat16
F32 = jnp.float32
MESH = pl.DeviceIdType.MESH
GN_EPS = 1e-6
LN_EPS = 1e-5
TM = 256
CK = 256
VMEM_LIMIT = 67_000_000


def nn(lhs, rhs):
    return lax.dot_general(lhs, rhs, (((1,), (0,)), ((), ())), preferred_element_type=F32)


def nt(lhs, rhs):
    return lax.dot_general(lhs, rhs, (((1,), (1,)), ((), ())), preferred_element_type=F32)


def split3(vals):
    high = vals.astype(BF16).astype(F32)
    rest = vals - high
    mid = rest.astype(BF16).astype(F32)
    return [high, mid, rest - mid]


def channel_sums(src, rows, chans):
    def step(idx, carry):
        tot, sqr = carry
        vals = src[pl.ds(pl.multiple_of(idx * 64, 64), 64), :].astype(F32).reshape(8, 8, chans)
        return tot + jnp.sum(vals, axis=0), sqr + jnp.sum(vals * vals, axis=0)

    zero = jnp.zeros((8, chans), F32)
    return lax.fori_loop(0, rows // 64, step, (zero, zero))


def group_affine(tot, sqr, gain, shift, groups, count, coef):
    chans = tot.shape[1]
    width = chans // groups
    terms = split3(jnp.sum(tot, axis=0, keepdims=True)) + split3(jnp.sum(sqr, axis=0, keepdims=True))
    rows = jnp.concatenate(terms + [jnp.zeros((2, chans), F32)], axis=0).astype(BF16)
    chan = lax.broadcasted_iota(jnp.int32, (chans, 128), 0)
    low = lax.broadcasted_iota(jnp.int32, (chans, 128), 1) * width
    member = jnp.where((chan >= low) & (chan < low + width), 1.0, 0.0).astype(BF16)
    sums = nn(rows, member)
    mean = (sums[0:1] + sums[1:2] + sums[2:3]) / count
    msq = (sums[3:4] + sums[4:5] + sums[5:6]) / count
    rstd = lax.rsqrt(msq - mean * mean + GN_EPS)
    back = jnp.concatenate(split3(mean) + split3(rstd) + [jnp.zeros((2, 128), F32)], axis=0).astype(BF16)
    wide = nt(back, member)
    coef[0:1, :] = wide[0:1] + wide[1:2] + wide[2:3]
    coef[1:2, :] = (wide[3:4] + wide[4:5] + wide[5:6]) * gain
    coef[2:3, :] = shift


def layer_norm(tokens):
    centred = tokens - jnp.mean(tokens, axis=-1, keepdims=True)
    return (centred * lax.rsqrt(jnp.mean(centred * centred, axis=-1, keepdims=True) + LN_EPS)).astype(BF16)


def exchange(blocks, collective):
    num = blocks.shape[0]

    def kernel(src, dst, stage, send_sem, recv_sem, own_sem):
        me = lax.axis_index('sp')
        barrier = pltpu.get_barrier_semaphore()
        for step in range(1, num):
            pl.semaphore_signal(barrier, inc=1, device_id={'sp': lax.rem(me + step, num)}, device_id_type=MESH)
        pl.semaphore_wait(barrier, num - 1)
        copies = []
        order = sorted(range(1, num), key=lambda step: -min(step, num - step))
        for step in order:
            peer = lax.rem(me + step, num)
            copy = pltpu.make_async_remote_copy(src.at[peer], dst.at[me], send_sem.at[step], recv_sem.at[step], device_id={'sp': peer}, device_id_type=MESH)
            copy.start()
            copies.append(copy)
        own_in = pltpu.make_async_copy(src.at[me], stage, own_sem)
        own_in.start()
        own_in.wait()
        own_out = pltpu.make_async_copy(stage, dst.at[me], own_sem)
        own_out.start()
        own_out.wait()
        for copy in copies:
            copy.wait()

    return pl.pallas_call(
        kernel,
        out_shape=jax.ShapeDtypeStruct(blocks.shape, blocks.dtype),
        in_specs=[pl.BlockSpec(memory_space=pl.ANY)],
        out_specs=pl.BlockSpec(memory_space=pl.ANY),
        scratch_shapes=[pltpu.VMEM(blocks.shape[1:], blocks.dtype), pltpu.SemaphoreType.DMA((num,)), pltpu.SemaphoreType.DMA((num,)), pltpu.SemaphoreType.DMA],
        compiler_params=pltpu.CompilerParams(collective_id=collective, has_side_effects=True),
        name='exchange',
    )(blocks)


def res_block(hidden, res_conv, norms, time_proj, which, width, groups):
    tokens, chans = hidden.shape
    chunks = chans // CK
    tiles = tokens // TM
    count = float(tokens * (chans // groups))

    def kernel(x_ref, kern, norm_ref, time_ref, out_ref, acc, mid, act, wbuf, coef, wsem):
        def fetch(step, slot):
            conv, chunk = step // chunks, lax.rem(step, chunks)
            rows = pl.ds(pl.multiple_of(chunk * CK, CK), CK)
            return [pltpu.make_async_copy(kern.at[which, conv, dy, dx, rows, :], wbuf.at[slot, dy, pl.ds(dx * CK, CK), :], wsem.at[slot])
                    for dy in range(3) for dx in range(3)]

        for copy in fetch(0, 0):
            copy.start()
        edge = jnp.zeros((width, 3 * CK), BF16)
        for slot in range(2):
            act[slot, 0:width, :] = edge
            act[slot, width + tokens:2 * width + tokens, :] = edge
        column = lax.rem(lax.broadcasted_iota(jnp.int32, (TM, CK), 0), width)

        def build(src, chunk, tile, slot):
            cols = pl.ds(pl.multiple_of(chunk * CK, CK), CK)
            rows = pl.multiple_of(tile * TM, TM)
            vals = src[pl.ds(rows, TM), cols].astype(F32)
            vals = (vals - coef[0:1, cols]) * coef[1:2, cols] + coef[2:3, cols]
            vals = vals * (1.0 / (1.0 + jnp.exp(-vals)))
            put = pl.ds(rows + width, TM)
            act[slot, put, 0:CK] = jnp.where(column == 0, 0.0, pltpu.roll(vals, 1, 0)).astype(BF16)
            act[slot, put, CK:2 * CK] = vals.astype(BF16)
            act[slot, put, 2 * CK:3 * CK] = jnp.where(column == width - 1, 0.0, pltpu.roll(vals, TM - 1, 0)).astype(BF16)

        def conv(src, index):
            @pl.loop(0, tiles)
            def _(tile):
                build(src, 0, tile, 0)

            acc[...] = jnp.zeros_like(acc)

            @pl.loop(0, chunks)
            def _(chunk):
                step = index * chunks + chunk
                wslot = lax.rem(step, 2)
                slot = lax.rem(chunk, 2)

                @pl.when(step + 1 < 2 * chunks)
                def _():
                    for copy in fetch(step + 1, 1 - wslot):
                        copy.start()

                for copy in fetch(step, wslot):
                    copy.wait()

                @pl.loop(0, tiles)
                def _(tile):
                    rows = pl.multiple_of(tile * TM, TM)
                    part = nn(act[slot, pl.ds(rows, TM), :], wbuf[wslot, 0])
                    part += nn(act[slot, pl.ds(rows + width, TM), :], wbuf[wslot, 1])
                    part += nn(act[slot, pl.ds(rows + 2 * width, TM), :], wbuf[wslot, 2])
                    acc[pl.ds(rows, TM), :] += part
                    build(src, lax.rem(chunk + 1, chunks), tile, 1 - slot)

        tot, sqr = channel_sums(x_ref, tokens, chans)
        group_affine(tot, sqr, norm_ref[0:1], norm_ref[1:2], groups, count, coef)
        conv(x_ref, 0)

        @pl.loop(0, tokens // 64)
        def _(idx):
            rows = pl.ds(pl.multiple_of(idx * 64, 64), 64)
            mid[rows, :] = (acc[rows, :] + time_ref[0:1]).astype(BF16)

        tot, sqr = channel_sums(mid, tokens, chans)
        group_affine(tot, sqr, norm_ref[2:3], norm_ref[3:4], groups, count, coef)
        conv(mid, 1)

        @pl.loop(0, tokens // 64)
        def _(idx):
            rows = pl.ds(pl.multiple_of(idx * 64, 64), 64)
            out_ref[rows, :] = (x_ref[rows, :].astype(F32) + acc[rows, :]).astype(BF16)

    flops = 2 * 2 * 9 * tokens * chans * chans
    vmem = pl.BlockSpec(memory_space=pltpu.VMEM)
    return pl.pallas_call(
        kernel,
        out_shape=jax.ShapeDtypeStruct(hidden.shape, BF16),
        in_specs=[vmem, pl.BlockSpec(memory_space=pl.ANY), vmem, vmem],
        out_specs=vmem,
        scratch_shapes=[
            pltpu.VMEM((tokens, chans), F32),
            pltpu.VMEM((tokens, chans), BF16),
            pltpu.VMEM((2, tokens + 2 * width, 3 * CK), BF16),
            pltpu.VMEM((2, 3, 3 * CK, chans), BF16),
            pltpu.VMEM((8, chans), F32),
            pltpu.SemaphoreType.DMA((2,)),
        ],
        compiler_params=pltpu.CompilerParams(vmem_limit_bytes=VMEM_LIMIT),
        cost_estimate=pl.CostEstimate(flops=flops, bytes_accessed=2 * 9 * chans * chans * 2, transcendentals=0),
        name='res_block',
    )(hidden, res_conv, norms, time_proj)


def transformer(hidden, context, norms, proj_inout, qkv_t, self_out, cross_q_t, cross_kv_t, cross_out, ff_in, ff_out, groups, heads, text):
    tokens, chans = hidden.shape
    text_rows, text_dim = context.shape
    head_dim = chans // heads
    pairs = heads // 2
    pair = 2 * head_dim
    count = float(tokens * (chans // groups))
    tiles = tokens // TM
    ff_steps = ff_out.shape[0] // chans
    slots = 4
    qb = 256
    scale = head_dim ** -0.5
    half = chans // 2

    def kernel(h_ref, ctx_ref, norm_ref, pio, wqkv, wo, cq, ckv, co, f1, f2, out_ref,
               ring, ckvbuf, tok, aux, q_t, keys, v_t, logit, acc, ctx_k, ctx_v, coef, rsem, csem):
        units = [pio.at[0], wqkv.at[0], wqkv.at[1], wqkv.at[2], wo, cq, co]
        for f in range(ff_steps):
            units += [f1.at[:, pl.ds(f * chans, chans)], f1.at[:, pl.ds((ff_steps + f) * chans, chans)], f2.at[pl.ds(f * chans, chans), :]]
        units.append(pio.at[1])

        def copy_of(unit):
            return pltpu.make_async_copy(units[unit], ring.at[unit % slots], rsem.at[unit % slots])

        def take(unit):
            copy_of(unit).wait()
            return ring.at[unit % slots]

        def done(unit):
            if unit + slots < len(units):
                copy_of(unit + slots).start()

        for unit in range(slots):
            copy_of(unit).start()
        ctx_copy = pltpu.make_async_copy(ckv, ckvbuf, csem)
        ctx_copy.start()

        def tile_rows(tile):
            return pl.ds(pl.multiple_of(tile * TM, TM), TM)

        tot, sqr = channel_sums(h_ref, tokens, chans)
        group_affine(tot, sqr, norm_ref[0:1], norm_ref[1:2], groups, count, coef)

        w_in = take(0)

        @pl.loop(0, tiles)
        def _(tile):
            rows = tile_rows(tile)
            normed = ((h_ref[rows, :].astype(F32) - coef[0:1]) * coef[1:2] + coef[2:3]).astype(BF16)
            t = nn(normed, w_in[...]).astype(BF16)
            tok[rows, :] = t
            aux[rows, :] = layer_norm(t.astype(F32))
        done(0)

        def transposed(weight, src, dst, factor):
            @pl.loop(0, 2)
            def _(part):
                rows = pl.ds(pl.multiple_of(part * half, half), half)
                dst[rows, :] = (nt(weight[rows, :], src[...]).astype(BF16) * factor).astype(BF16) if factor != 1.0 else nt(weight[rows, :], src[...]).astype(BF16)

        transposed(take(1), aux, q_t, scale)
        done(1)
        w_key = take(2)

        @pl.loop(0, tokens // 512)
        def _(part):
            rows = pl.ds(pl.multiple_of(part * 512, 512), 512)
            keys[rows, :] = nt(aux[rows, :], w_key[...]).astype(BF16)
        done(2)
        transposed(take(3), aux, v_t, 1.0)
        done(3)

        lane_head = lax.broadcasted_iota(jnp.int32, (pair, qb), 0)

        def softmax_block(scores, valid):
            if valid is not None:
                scores = jnp.where(valid, scores, -jnp.inf)
            top = jnp.max(scores, axis=0, keepdims=True)
            weights = jnp.exp(scores - top)
            return weights.astype(BF16), jnp.sum(weights, axis=0, keepdims=True)

        def attend(key_ref, val_ref, key_rows, valid, dst):
            @pl.loop(0, pairs)
            def _(hp):
                cols = pl.ds(pl.multiple_of(hp * pair, pair), pair)
                for j in range(tokens // qb):
                    both = q_t[cols, j * qb:(j + 1) * qb]
                    outs = []
                    for h in range(2):
                        mine = (lane_head < head_dim) if h == 0 else (lane_head >= head_dim)
                        query = jnp.where(mine, both, jnp.zeros_like(both))
                        scores = nn(key_ref[:, cols], query)
                        weights, denom = softmax_block(scores, valid)
                        vals = val_ref[pl.ds(pl.multiple_of(hp * pair + h * head_dim, head_dim), head_dim), :]
                        outs.append(nn(vals, weights) / denom)
                    out = jnp.concatenate(outs, axis=0)
                    dst[j * qb:(j + 1) * qb, cols] = out.T.astype(BF16)

        attend(keys, v_t, tokens, None, aux)

        w_out = take(4)

        @pl.loop(0, tiles)
        def _(tile):
            rows = tile_rows(tile)
            t = (tok[rows, :].astype(F32) + nn(aux[rows, :], w_out[...])).astype(BF16)
            tok[rows, :] = t
            keys[rows, :] = layer_norm(t.astype(F32))
        done(4)

        transposed(take(5), keys, q_t, scale)
        done(5)
        ctx_copy.wait()
        ctx_k[...] = nt(ctx_ref[...], ckvbuf[0]).astype(BF16)

        @pl.loop(0, chans // 256)
        def _(part):
            rows = pl.ds(pl.multiple_of(part * 256, 256), 256)
            ctx_v[rows, :] = nt(ckvbuf[1, rows, :], ctx_ref[...]).astype(BF16)

        text_valid = lax.broadcasted_iota(jnp.int32, (text_rows, qb), 0) < text
        attend(ctx_k, ctx_v, text_rows, text_valid, aux)

        w_cross = take(6)

        @pl.loop(0, tiles)
        def _(tile):
            rows = tile_rows(tile)
            t = (tok[rows, :].astype(F32) + nn(aux[rows, :], w_cross[...])).astype(BF16)
            tok[rows, :] = t
            keys[rows, :] = layer_norm(t.astype(F32))
        done(6)

        acc[...] = jnp.zeros_like(acc)
        for f in range(ff_steps):
            base = 7 + 3 * f
            w_val, w_gate, w_down = take(base), take(base + 1), take(base + 2)

            @pl.loop(0, tiles)
            def _(tile):
                rows = tile_rows(tile)
                src = keys[rows, :]
                value = nn(src, w_val[...])
                gate = nn(src, w_gate[...])
                gated = (value * (0.5 * gate * (1.0 + lax.erf(gate * (0.5 ** 0.5))))).astype(BF16)
                acc[rows, :] += nn(gated, w_down[...])
            done(base)
            done(base + 1)
            done(base + 2)

        last = len(units) - 1
        w_fin = take(last)

        @pl.loop(0, tiles)
        def _(tile):
            rows = tile_rows(tile)
            t = (tok[rows, :].astype(F32) + acc[rows, :]).astype(BF16)
            out_ref[rows, :] = (h_ref[rows, :].astype(F32) + nn(t, w_fin[...])).astype(BF16)

    vmem = pl.BlockSpec(memory_space=pltpu.VMEM)
    hbm = pl.BlockSpec(memory_space=pl.ANY)
    flops = 2 * tokens * chans * chans * (8 + 3 * ff_steps) + 4 * tokens * tokens * chans
    return pl.pallas_call(
        kernel,
        out_shape=jax.ShapeDtypeStruct(hidden.shape, BF16),
        in_specs=[vmem, vmem, vmem] + [hbm] * 8,
        out_specs=vmem,
        scratch_shapes=[
            pltpu.VMEM((slots, chans, chans), BF16),
            pltpu.VMEM((2, chans, text_dim), BF16),
            pltpu.VMEM((tokens, chans), BF16),
            pltpu.VMEM((tokens, chans), BF16),
            pltpu.VMEM((chans, tokens), BF16),
            pltpu.VMEM((tokens, chans), BF16),
            pltpu.VMEM((chans, tokens), BF16),
            pltpu.VMEM((8, 128), F32),
            pltpu.VMEM((tokens, chans), F32),
            pltpu.VMEM((text_rows, chans), BF16),
            pltpu.VMEM((chans, text_rows), BF16),
            pltpu.VMEM((8, chans), F32),
            pltpu.SemaphoreType.DMA((slots,)),
            pltpu.SemaphoreType.DMA,
        ],
        compiler_params=pltpu.CompilerParams(vmem_limit_bytes=VMEM_LIMIT),
        cost_estimate=pl.CostEstimate(flops=flops, bytes_accessed=80_000_000, transcendentals=tokens * tokens * heads),
        name='transformer',
    )(hidden, context, norms, proj_inout, qkv_t, self_out, cross_q_t, cross_kv_t, cross_out, ff_in, ff_out)


def solution(mesh):
    num_bands = mesh.shape['sp']

    def local_stage(latent, time_emb, context, res_conv, res_time, res_norm, attn_norm, proj_inout, self_qkv, self_out, cross_q, cross_kv, cross_out, ff_in, ff_out):
        images, band_rows, width, chans = latent.shape
        assert images == num_bands
        band = band_rows * width
        heads, head_dim = self_out.shape[:2]
        groups = res_norm.shape[3]
        text, text_dim = context.shape[1:]
        me = lax.axis_index('sp')

        image = exchange(latent.reshape(images, band, chans), 0).reshape(images * band, chans)
        time_row = lax.dynamic_slice_in_dim(time_emb, me, 1, 0)
        time_act = jax.nn.silu(time_row.astype(F32)).astype(BF16)
        time_proj = jnp.einsum('tc,bcd->btd', time_act, res_time, preferred_element_type=F32)
        norms = res_norm.astype(F32).reshape(2, 4, chans)
        ctx_rows = -(-text // 16) * 16
        ctx = lax.dynamic_index_in_dim(context, me, 0, keepdims=False)
        ctx = jnp.pad(ctx, ((0, ctx_rows - text), (0, 0)))

        first = res_block(image, res_conv, norms[0], time_proj[0], 0, width, groups)
        middle = transformer(
            first, ctx, attn_norm.astype(F32).reshape(2, chans), proj_inout,
            jnp.transpose(self_qkv, (0, 2, 3, 1)).reshape(3, chans, chans),
            self_out.reshape(chans, chans),
            jnp.transpose(cross_q, (1, 2, 0)).reshape(chans, chans),
            jnp.transpose(cross_kv, (0, 2, 3, 1)).reshape(2, chans, text_dim),
            cross_out.reshape(chans, chans), ff_in, ff_out, groups, heads, text)
        last = res_block(middle, res_conv, norms[1], time_proj[1], 1, width, groups)
        out = exchange(last.reshape(num_bands, band, chans), 1)
        return out.reshape(latent.shape)

    band_spec = P('dp', 'sp', None, None)
    shared = P()
    in_specs = (band_spec, P('dp', None), P('dp', None, None)) + (shared,) * 12
    return jax.shard_map(local_stage, mesh=mesh, in_specs=in_specs, out_specs=band_spec, check_vma=False)
```

time: 1680 us -> 486 us (0.29); the launches traced: 1650 us -> 477 us
  waiting for transfers between devices: 672 us -> 0 us
  matrix products: 478 us -> 3.86 us
  Pallas kernels: 0 us -> 463 us
  blocking collectives: 269 us -> 0 us
  local copies, waits for them, and re-layouts: 111 us -> 9.53 us
  other arithmetic: 90.8 us -> 0 us
    all_gather x2 -> x0, waiting for transfers between devices: 667 us -> none  [the longest x1 350 us: transformer(): lax.all_gather(project(ln_tokens, self_qkv[1]).reshape(band_shape), 'sp',...]
    pallas_call x0 -> x5, Pallas kernels: none -> 463 us  [the longest x1 168 us: transformer(): pl.pallas_call(kernel, out_shape=jax.ShapeDtypeStruct(hidden.shape, BF16)...]
    dot_general x12 -> x1, matrix products: 314 us -> 3.86 us  [local_stage(): jnp.einsum('tc,bcd->btd', time_act, res_time, preferred_element_type=F32)]
    psum x5 -> x0, blocking collectives: 269 us -> none  [group_norm(): stat_sums = lax.psum(local_sums, 'sp')]
    conv_general_dilated x4 -> x0, matrix products: 146 us -> none  [conv_band(): lax.conv_general_dilated(padded, kernel, (1, 1), ((0, 0), (1, 1)), dimens...]
    reduce_sum x17 -> x0, other arithmetic: 59 us -> none  [the longest x2 35.3 us: attend(): row_sum = jnp.sum(weights, axis=-1, keepdims=True)]
    reshape x6 -> x1, local copies, waits for them, and re-layouts: 48 us -> 0.7 us  [local_stage(): attn_norm.astype(F32).reshape(2, chans)]
    convert_element_type x10 -> x0, other arithmetic: 26.4 us -> none  [the longest x2 10.3 us: res_block(): jax.nn.silu(group_norm(hidden, norm_pair[0], elem_count))]
  transfers between devices with their start and end apart: 10 -> 0, of which waited for: 5 -> 0; matrix products, arithmetic and copies ran while one was open for 10% -> 0% of each run, Pallas kernels for 0% -> 0%
where the time goes in v1:
time: 486 us; the launch traced here: 477 us
  Pallas kernels  463 us (95%)
  local copies, waits for them, and re-layouts  9.53 us (2%)
    pallas_call x1, Pallas kernels, transformer(): pl.pallas_call(kernel, out_shape=jax.ShapeDtypeStruct(hidden.shape, BF16)...  168 us
    pallas_call x2, Pallas kernels, res_block(): pl.pallas_call(kernel, out_shape=jax.ShapeDtypeStruct(hidden.shape, BF16)...  164 us
    pallas_call x2, Pallas kernels, exchange(): pl.pallas_call(kernel, out_shape=jax.ShapeDtypeStruct(blocks.shape, block...  131 us

profile of v1, /device:TPU:30, one launch (start us, length us, event | category | flops | bytes accessed | tf_op | source)
XLA Modules:
  0.0 477.2 jit_solution(5573591307990011654)
XLA Ops:
  0.0 0.0 copy-start.1
  0.0 0.0 copy-start
  0.0 3.9 fusion
  3.9 0.6 fusion.11
  4.5 0.0 copy-done.1
  4.5 0.7 reshape.59.norm_ref
  5.2 0.0 copy-done
  5.2 0.7 squeeze.14.norm_ref
  5.9 0.7 squeeze.12.norm_ref
  6.6 2.4 constant_dynamic-slice_fusion
  9.0 0.2 copy.21
  9.2 0.8 pad.4.ctx_ref
  9.9 65.7 %exchange.2 = bf16[16,64,1280]{2,1,0:T(8,128)(2,1)} custom-call(bf16[16,64,1280]{2,1,0:T(8,128)(2,1)} %bitcast.30), custom_call_target="tpu_custom_call" | custom-call | tf_op jit(solution)/shard_map/exchange/pallas_call | solution.py:94
  75.6 82.1 %res_block.2.h_ref = bf16[1024,1280]{1,0:T(8,128)(2,1)} custom-call(bf16[1024,1280]{1,0:T(8,128)(2,1)} %bitcast.32, bf16[2,2,3,3,1280,1280]{5,4,3,2,1,0:T(8,128)(2,1)} %kern.3, f32[4,1280]{1,0:T(4,128)} %squeeze.12.norm_ref, f32[1,1280]{1,0:T(1,128)} %get-tuple-element.8.time_ref), custom_call_target="tpu_custom_call" | custom-call | flops 60397977600 | bytes 58982400 | tf_op jit(solution)/shard_map/res_block/pallas_call | solution.py:187
  157.8 168.2 %transformer.1.x_ref = bf16[1024,1280]{1,0:T(8,128)(2,1)} custom-call(bf16[1024,1280]{1,0:T(8,128)(2,1)} %res_block.2.h_ref, bf16[80,2048]{1,0:T(8,128)(2,1)} %pad.4.ctx_ref, f32[2,1280]{1,0:T(2,128)} %reshape.59.norm_ref, bf16[2,1280,1280]{2,1,0:T(8,128)(2,1)} %pio.1, bf16[3,1280,1280]{2,1,0:T(8,128)(2,1)} %bitcast.36, bf16[1280,1280]{1,0:T(8,128)(2,1)} %bitcast.37, ...), custom_call_target="tpu_custom_call" | custom-call | flops 72477573120 | bytes 80000000 | tf_op jit(solution)/shard_map/transformer/pallas_call | solution.py:368
  326.0 82.3 %res_block.3 = bf16[1024,1280]{1,0:T(8,128)(2,1)} custom-call(bf16[1024,1280]{1,0:T(8,128)(2,1)} %transformer.1.x_ref, bf16[2,2,3,3,1280,1280]{5,4,3,2,1,0:T(8,128)(2,1)} %kern.3, f32[4,1280]{1,0:T(4,128)} %squeeze.14.norm_ref, f32[1,1280]{1,0:T(1,128)} %get-tuple-element.7.time_ref), custom_call_target="tpu_custom_call" | custom-call | flops 60397977600 | bytes 58982400 | tf_op jit(solution)/shard_map/res_block/pallas_call | solution.py:187
  408.3 65.0 %exchange.3 = bf16[16,64,1280]{2,1,0:T(8,128)(2,1)} custom-call(bf16[16,64,1280]{2,1,0:T(8,128)(2,1)} %bitcast.31), custom_call_target="tpu_custom_call" | custom-call | tf_op jit(solution)/shard_map/exchange/pallas_call | solution.py:94
  473.3 3.5 copy.24
  (2 shorter events, 0.0 us)
Async XLA Ops:
  0.0 4.5 copy-start.1
  0.0 5.2 %copy-start = (bf16[2,2,2,32,40]{4,3,2,1,0:T(8,128)(2,1)S(1)}, bf16[2,2,2,32,40]{4,3,2,1,0:T(8,128)(2,1)}, u32[]{:S(2)}) copy-start(bf16[2,2,2,32,40]{4,3,2,1,0:T(8,128)(2,1)} %param.20) | copy-start | bytes 61444

commit v2 on v1

--- a/solution.py
+++ b/solution.py
@@ -42,7 +42,7 @@
     return lax.fori_loop(0, rows // 64, step, (zero, zero))
 
 
-def group_affine(tot, sqr, gain, shift, groups, count, coef):
+def group_affine(tot, sqr, gain, shift, groups, count, coef, factor):
     chans = tot.shape[1]
     width = chans // groups
     terms = split3(jnp.sum(tot, axis=0, keepdims=True)) + split3(jnp.sum(sqr, axis=0, keepdims=True))
@@ -56,9 +56,9 @@
     rstd = lax.rsqrt(msq - mean * mean + GN_EPS)
     back = jnp.concatenate(split3(mean) + split3(rstd) + [jnp.zeros((2, 128), F32)], axis=0).astype(BF16)
     wide = nt(back, member)
-    coef[0:1, :] = wide[0:1] + wide[1:2] + wide[2:3]
-    coef[1:2, :] = (wide[3:4] + wide[4:5] + wide[5:6]) * gain
-    coef[2:3, :] = shift
+    scale = (wide[3:4] + wide[4:5] + wide[5:6]) * gain
+    coef[0:1, :] = factor * scale
+    coef[1:2, :] = factor * (shift - (wide[0:1] + wide[1:2] + wide[2:3]) * scale)
 
 
 def layer_norm(tokens):
@@ -127,8 +127,8 @@
             cols = pl.ds(pl.multiple_of(chunk * CK, CK), CK)
             rows = pl.multiple_of(tile * TM, TM)
             vals = src[pl.ds(rows, TM), cols].astype(F32)
-            vals = (vals - coef[0:1, cols]) * coef[1:2, cols] + coef[2:3, cols]
-            vals = vals * (1.0 / (1.0 + jnp.exp(-vals)))
+            half = vals * coef[0:1, cols] + coef[1:2, cols]
+            vals = half + half * jnp.tanh(half)
             put = pl.ds(rows + width, TM)
             act[slot, put, 0:CK] = jnp.where(column == 0, 0.0, pltpu.roll(vals, 1, 0)).astype(BF16)
             act[slot, put, CK:2 * CK] = vals.astype(BF16)
@@ -165,7 +165,7 @@
                     build(src, lax.rem(chunk + 1, chunks), tile, 1 - slot)
 
         tot, sqr = channel_sums(x_ref, tokens, chans)
-        group_affine(tot, sqr, norm_ref[0:1], norm_ref[1:2], groups, count, coef)
+        group_affine(tot, sqr, norm_ref[0:1], norm_ref[1:2], groups, count, coef, 0.5)
         conv(x_ref, 0)
 
         @pl.loop(0, tokens // 64)
@@ -174,7 +174,7 @@
             mid[rows, :] = (acc[rows, :] + time_ref[0:1]).astype(BF16)
 
         tot, sqr = channel_sums(mid, tokens, chans)
-        group_affine(tot, sqr, norm_ref[2:3], norm_ref[3:4], groups, count, coef)
+        group_affine(tot, sqr, norm_ref[2:3], norm_ref[3:4], groups, count, coef, 0.5)
         conv(mid, 1)
 
         @pl.loop(0, tokens // 64)
@@ -212,50 +212,68 @@
     count = float(tokens * (chans // groups))
     tiles = tokens // TM
     ff_steps = ff_out.shape[0] // chans
-    slots = 4
-    qb = 256
+    ctx_half = text_dim // 2
+    qw = 512 if chans >= 1024 else 256
+    kb = 256
     scale = head_dim ** -0.5
     half = chans // 2
 
     def kernel(h_ref, ctx_ref, norm_ref, pio, wqkv, wo, cq, ckv, co, f1, f2, out_ref,
-               ring, ckvbuf, tok, aux, q_t, keys, v_t, logit, acc, ctx_k, ctx_v, coef, rsem, csem):
-        units = [pio.at[0], wqkv.at[0], wqkv.at[1], wqkv.at[2], wo, cq, co]
-        for f in range(ff_steps):
-            units += [f1.at[:, pl.ds(f * chans, chans)], f1.at[:, pl.ds((ff_steps + f) * chans, chans)], f2.at[pl.ds(f * chans, chans), :]]
-        units.append(pio.at[1])
-
-        def copy_of(unit):
-            return pltpu.make_async_copy(units[unit], ring.at[unit % slots], rsem.at[unit % slots])
-
-        def take(unit):
-            copy_of(unit).wait()
-            return ring.at[unit % slots]
-
-        def done(unit):
-            if unit + slots < len(units):
-                copy_of(unit + slots).start()
-
-        for unit in range(slots):
-            copy_of(unit).start()
-        ctx_copy = pltpu.make_async_copy(ckv, ckvbuf, csem)
-        ctx_copy.start()
+               ring, tok, aux, q_t, keys, v_t, acc, ctx_k, ctx_v, coef, rsem):
+        units = {
+            'in': (pio.at[0], 0, 0), 'q': (wqkv.at[0], 0, 1), 'k': (wqkv.at[1], 1, 0), 'v': (wqkv.at[2], 1, 1),
+            'ck0': (ckv.at[0, :, 0:ctx_half], 1, 2), 'ck1': (ckv.at[0, :, ctx_half:text_dim], 0, 2),
+            'cv0': (ckv.at[1, :, 0:ctx_half], 0, 0), 'cv1': (ckv.at[1, :, ctx_half:text_dim], 0, 1),
+            'o': (wo, 1, 0), 'cq': (cq, 1, 1), 'co': (co, 1, 2), 'out': (pio.at[1], 0, 0),
+        }
+
+        def spot(group, place, wide):
+            return ring.at[group, place] if wide == chans else ring.at[group, place, :, 0:wide]
+
+        def copy_of(name):
+            src, group, place = units[name]
+            return pltpu.make_async_copy(src, spot(group, place, src.shape[1]), rsem.at[group, place])
+
+        def start(*names):
+            for name in names:
+                copy_of(name).start()
+
+        def take(name):
+            copy_of(name).wait()
+            src, group, place = units[name]
+            return spot(group, place, src.shape[1])
+
+        def ff_copies(step, group):
+            cols = pl.multiple_of(step * chans, chans)
+            return [
+                pltpu.make_async_copy(f1.at[:, pl.ds(cols, chans)], ring.at[group, 0], rsem.at[group, 0]),
+                pltpu.make_async_copy(f1.at[:, pl.ds(cols + ff_steps * chans, chans)], ring.at[group, 1], rsem.at[group, 1]),
+                pltpu.make_async_copy(f2.at[pl.ds(cols, chans), :], ring.at[group, 2], rsem.at[group, 2]),
+            ]
+
+        start('in', 'q', 'k', 'v', 'ck0', 'ck1')
 
         def tile_rows(tile):
             return pl.ds(pl.multiple_of(tile * TM, TM), TM)
 
         tot, sqr = channel_sums(h_ref, tokens, chans)
-        group_affine(tot, sqr, norm_ref[0:1], norm_ref[1:2], groups, count, coef)
-
-        w_in = take(0)
-
-        @pl.loop(0, tiles)
-        def _(tile):
-            rows = tile_rows(tile)
-            normed = ((h_ref[rows, :].astype(F32) - coef[0:1]) * coef[1:2] + coef[2:3]).astype(BF16)
-            t = nn(normed, w_in[...]).astype(BF16)
-            tok[rows, :] = t
-            aux[rows, :] = layer_norm(t.astype(F32))
-        done(0)
+        group_affine(tot, sqr, norm_ref[0:1], norm_ref[1:2], groups, count, coef, 1.0)
+
+        def project_rows(weight, src, base, normed_to):
+            def norm_tile(tile):
+                rows = tile_rows(tile)
+                normed_to[rows, :] = layer_norm(tok[rows, :].astype(F32))
+
+            @pl.loop(0, tiles)
+            def _(tile):
+                norm_tile(jnp.maximum(tile - 1, 0))
+                rows = tile_rows(tile)
+                tok[rows, :] = (base(rows) + nn(src(rows), weight[...])).astype(BF16)
+
+            norm_tile(tiles - 1)
+
+        project_rows(take('in'), lambda rows: (h_ref[rows, :].astype(F32) * coef[0:1] + coef[1:2]).astype(BF16), lambda rows: 0.0, aux)
+        start('cv0')
 
         def transposed(weight, src, dst, factor):
             @pl.loop(0, 2)
@@ -263,98 +281,149 @@
                 rows = pl.ds(pl.multiple_of(part * half, half), half)
                 dst[rows, :] = (nt(weight[rows, :], src[...]).astype(BF16) * factor).astype(BF16) if factor != 1.0 else nt(weight[rows, :], src[...]).astype(BF16)
 
-        transposed(take(1), aux, q_t, scale)
-        done(1)
-        w_key = take(2)
+        transposed(take('q'), aux, q_t, scale)
+        start('cv1')
+        w_key = take('k')
 
         @pl.loop(0, tokens // 512)
         def _(part):
             rows = pl.ds(pl.multiple_of(part * 512, 512), 512)
             keys[rows, :] = nt(aux[rows, :], w_key[...]).astype(BF16)
-        done(2)
-        transposed(take(3), aux, v_t, 1.0)
-        done(3)
-
-        lane_head = lax.broadcasted_iota(jnp.int32, (pair, qb), 0)
-
-        def softmax_block(scores, valid):
-            if valid is not None:
-                scores = jnp.where(valid, scores, -jnp.inf)
-            top = jnp.max(scores, axis=0, keepdims=True)
-            weights = jnp.exp(scores - top)
-            return weights.astype(BF16), jnp.sum(weights, axis=0, keepdims=True)
-
-        def attend(key_ref, val_ref, key_rows, valid, dst):
-            @pl.loop(0, pairs)
-            def _(hp):
-                cols = pl.ds(pl.multiple_of(hp * pair, pair), pair)
-                for j in range(tokens // qb):
-                    both = q_t[cols, j * qb:(j + 1) * qb]
-                    outs = []
-                    for h in range(2):
-                        mine = (lane_head < head_dim) if h == 0 else (lane_head >= head_dim)
-                        query = jnp.where(mine, both, jnp.zeros_like(both))
-                        scores = nn(key_ref[:, cols], query)
-                        weights, denom = softmax_block(scores, valid)
-                        vals = val_ref[pl.ds(pl.multiple_of(hp * pair + h * head_dim, head_dim), head_dim), :]
-                        outs.append(nn(vals, weights) / denom)
-                    out = jnp.concatenate(outs, axis=0)
-                    dst[j * qb:(j + 1) * qb, cols] = out.T.astype(BF16)
-
-        attend(keys, v_t, tokens, None, aux)
-
-        w_out = take(4)
-
-        @pl.loop(0, tiles)
-        def _(tile):
-            rows = tile_rows(tile)
-            t = (tok[rows, :].astype(F32) + nn(aux[rows, :], w_out[...])).astype(BF16)
-            tok[rows, :] = t
-            keys[rows, :] = layer_norm(t.astype(F32))
-        done(4)
-
-        transposed(take(5), keys, q_t, scale)
-        done(5)
-        ctx_copy.wait()
-        ctx_k[...] = nt(ctx_ref[...], ckvbuf[0]).astype(BF16)
+        start('o')
+        transposed(take('v'), aux, v_t, 1.0)
+        start('cq')
+        w_ck = take('ck0'), take('ck1')
+        ctx_k[...] = (nt(ctx_ref[:, 0:ctx_half], w_ck[0][...]) + nt(ctx_ref[:, ctx_half:text_dim], w_ck[1][...])).astype(BF16)
+        start('co')
+        w_cv = take('cv0'), take('cv1')
 
         @pl.loop(0, chans // 256)
         def _(part):
             rows = pl.ds(pl.multiple_of(part * 256, 256), 256)
-            ctx_v[rows, :] = nt(ckvbuf[1, rows, :], ctx_ref[...]).astype(BF16)
-
-        text_valid = lax.broadcasted_iota(jnp.int32, (text_rows, qb), 0) < text
-        attend(ctx_k, ctx_v, text_rows, text_valid, aux)
-
-        w_cross = take(6)
-
-        @pl.loop(0, tiles)
-        def _(tile):
-            rows = tile_rows(tile)
-            t = (tok[rows, :].astype(F32) + nn(aux[rows, :], w_cross[...])).astype(BF16)
-            tok[rows, :] = t
-            keys[rows, :] = layer_norm(t.astype(F32))
-        done(6)
-
+            ctx_v[rows, :] = (nt(w_cv[0][rows, :], ctx_ref[:, 0:ctx_half]) + nt(w_cv[1][rows, :], ctx_ref[:, ctx_half:text_dim])).astype(BF16)
+
+        for copy in ff_copies(0, 0):
+            copy.start()
+
+        row_head = lax.broadcasted_iota(jnp.int32, (pair, 1), 0) < head_dim
+
+        def query_of(hp, first, wide, head):
+            both = q_t[pl.ds(pl.multiple_of(hp * pair, pair), pair), pl.ds(first, wide)]
+            keep = row_head if head == 0 else jnp.logical_not(row_head)
+            return jnp.where(keep, both, jnp.zeros_like(both))
+
+        def pair_cols(hp):
+            return pl.ds(pl.multiple_of(hp * pair, pair), pair)
+
+        halves = tokens // qw
+        blocks = pairs * halves
+        scores = [acc.at[:, pl.ds(h * qw, qw)] for h in range(2)]
+        probs = [out_ref.at[:, pl.ds(h * qw, qw)] for h in range(2)]
+        parts = tokens // kb
+
+        def place(block):
+            hp = lax.div(block, halves)
+            return hp, pl.multiple_of((block - hp * halves) * qw, qw)
+
+        def fold(vals, func):
+            return func(vals.reshape(-1, 8, vals.shape[-1]), axis=0)
+
+        def score_part(block, head, part):
+            hp, first = place(block)
+            query = query_of(hp, first, qw, head)
+            vals = nn(keys[part * kb:(part + 1) * kb, pair_cols(hp)], query)
+            scores[head][part * kb:(part + 1) * kb, :] = vals
+            return fold(vals, jnp.max)
+
+        def exp_part(head, part, top):
+            vals = jnp.exp(scores[head][part * kb:(part + 1) * kb, :] - top)
+            probs[head][part * kb:(part + 1) * kb, :] = vals.astype(BF16)
+            return fold(vals, jnp.sum)
+
+        def value_of(block, head, denom):
+            hp, _ = place(block)
+            vals = v_t[pl.ds(pl.multiple_of(hp * pair + head * head_dim, head_dim), head_dim), :]
+            return nn(vals, probs[head][...]) / denom
+
+        def softmax_stage(score_block, score_head, exp_head, top):
+            tops, sums = [], []
+            for part in range(parts):
+                tops.append(score_part(score_block, score_head, part))
+                sums.append(exp_part(exp_head, part, top))
+            new_top = jnp.max(functools.reduce(jnp.maximum, tops), axis=0, keepdims=True)
+            return new_top, jnp.sum(functools.reduce(jnp.add, sums), axis=0, keepdims=True)
+
+        def emit(block, low, high):
+            hp, first = place(block)
+            aux[pl.ds(first, qw), pair_cols(hp)] = jnp.concatenate([low, high], axis=0).T.astype(BF16)
+
+        top_first = jnp.max(functools.reduce(jnp.maximum, [score_part(0, 0, part) for part in range(parts)]), axis=0, keepdims=True)
+        zero_row = jnp.ones((1, qw), F32)
+        zero_out = jnp.zeros((head_dim, qw), F32)
+
+        def attend_block(block, carry):
+            top0, denom1, low = carry
+            before = jnp.maximum(block - 1, 0)
+            high = value_of(before, 1, denom1)
+            emit(before, low, high)
+            top1, denom0 = softmax_stage(block, 1, 0, top0)
+            after = jnp.minimum(block + 1, blocks - 1)
+            low = value_of(block, 0, denom0)
+            top0, denom1 = softmax_stage(after, 0, 1, top1)
+            return top0, denom1, low
+
+        _, denom1, low = lax.fori_loop(0, blocks, attend_block, (top_first, zero_row, zero_out))
+        emit(blocks - 1, low, value_of(blocks - 1, 1, denom1))
+
+        project_rows(take('o'), lambda rows: aux[rows, :], lambda rows: tok[rows, :].astype(F32), keys)
+        transposed(take('cq'), keys, q_t, scale)
+
+        text_valid = lax.broadcasted_iota(jnp.int32, (text_rows, 1), 0) < text
+
+        @pl.loop(0, pairs // 2)
+        def _(step):
+            for sub in range(2):
+                hp = step * 2 + sub
+                outs = []
+                for head in range(2):
+                    vals = nn(ctx_k[:, pair_cols(hp)], query_of(hp, 0, tokens, head))
+                    vals = jnp.where(text_valid, vals, -jnp.inf)
+                    weights = jnp.exp(vals - jnp.max(vals, axis=0, keepdims=True))
+                    denom = jnp.sum(weights, axis=0, keepdims=True)
+                    text_vals = ctx_v[pl.ds(pl.multiple_of(hp * pair + head * head_dim, head_dim), head_dim), :]
+                    outs.append(nn(text_vals, weights.astype(BF16)) / denom)
+                aux[:, pair_cols(hp)] = jnp.concatenate(outs, axis=0).T.astype(BF16)
+
+        project_rows(take('co'), lambda rows: aux[rows, :], lambda rows: tok[rows, :].astype(F32), keys)
+        for copy in ff_copies(1, 1):
+            copy.start()
         acc[...] = jnp.zeros_like(acc)
-        for f in range(ff_steps):
-            base = 7 + 3 * f
-            w_val, w_gate, w_down = take(base), take(base + 1), take(base + 2)
+
+        @pl.loop(0, ff_steps)
+        def _(step):
+            group = lax.rem(step, 2)
+            for copy in ff_copies(step, group):
+                copy.wait()
 
             @pl.loop(0, tiles)
             def _(tile):
                 rows = tile_rows(tile)
                 src = keys[rows, :]
-                value = nn(src, w_val[...])
-                gate = nn(src, w_gate[...])
+                value = nn(src, ring[group, 0])
+                gate = nn(src, ring[group, 1])
                 gated = (value * (0.5 * gate * (1.0 + lax.erf(gate * (0.5 ** 0.5))))).astype(BF16)
-                acc[rows, :] += nn(gated, w_down[...])
-            done(base)
-            done(base + 1)
-            done(base + 2)
-
-        last = len(units) - 1
-        w_fin = take(last)
+                acc[rows, :] += nn(gated, ring[group, 2])
+
+            @pl.when(step + 2 < ff_steps)
+            def _():
+                for copy in ff_copies(step + 2, group):
+                    copy.start()
+
+            @pl.when(step == ff_steps - 2)
+            def _():
+                start('out')
+
+        w_fin = take('out')
 
         @pl.loop(0, tiles)
         def _(tile):
@@ -371,20 +440,17 @@
         in_specs=[vmem, vmem, vmem] + [hbm] * 8,
         out_specs=vmem,
         scratch_shapes=[
-            pltpu.VMEM((slots, chans, chans), BF16),
-            pltpu.VMEM((2, chans, text_dim), BF16),
+            pltpu.VMEM((2, 3, chans, chans), BF16),
             pltpu.VMEM((tokens, chans), BF16),
             pltpu.VMEM((tokens, chans), BF16),
             pltpu.VMEM((chans, tokens), BF16),
             pltpu.VMEM((tokens, chans), BF16),
             pltpu.VMEM((chans, tokens), BF16),
-            pltpu.VMEM((8, 128), F32),
             pltpu.VMEM((tokens, chans), F32),
             pltpu.VMEM((text_rows, chans), BF16),
             pltpu.VMEM((chans, text_rows), BF16),
             pltpu.VMEM((8, chans), F32),
-            pltpu.SemaphoreType.DMA((slots,)),
-            pltpu.SemaphoreType.DMA,
+            pltpu.SemaphoreType.DMA((2, 3)),
         ],
         compiler_params=pltpu.CompilerParams(vmem_limit_bytes=VMEM_LIMIT),
         cost_estimate=pl.CostEstimate(flops=flops, bytes_accessed=80_000_000, transcendentals=tokens * tokens * heads),

time: 486 us -> 437 us (0.90); the launches traced: 477 us -> 436 us
  Pallas kernels: 463 us -> 423 us
    pallas_call x1, Pallas kernels: 168 us -> 128 us  [transformer(): pl.pallas_call(kernel, out_shape=jax.ShapeDtypeStruct(hidden.shape, BF16)...]
where the time goes in v2:
time: 437 us; the launch traced here: 436 us
  Pallas kernels  423 us (97%)
  local copies, waits for them, and re-layouts  9.53 us (2%)
    pallas_call x2, Pallas kernels, res_block(): pl.pallas_call(kernel, out_shape=jax.ShapeDtypeStruct(hidden.shape, BF16)...  165 us
    pallas_call x2, Pallas kernels, exchange(): pl.pallas_call(kernel, out_shape=jax.ShapeDtypeStruct(blocks.shape, block...  131 us
    pallas_call x1, Pallas kernels, transformer(): pl.pallas_call(kernel, out_shape=jax.ShapeDtypeStruct(hidden.shape, BF16)...  128 us

profile of v2, /device:TPU:30, one launch (start us, length us, event | category | flops | bytes accessed | tf_op | source)
XLA Modules:
  0.0 436.4 jit_solution(9496581335407915748)
XLA Ops:
  0.0 0.0 copy-start.1
  0.0 0.0 copy-start
  0.0 3.9 fusion
  3.9 0.6 fusion.11
  4.5 0.0 copy-done.1
  4.5 0.7 reshape.59.norm_ref
  5.2 0.0 copy-done
  5.2 0.7 squeeze.14.norm_ref
  5.9 0.7 squeeze.12.norm_ref
  6.6 2.4 constant_dynamic-slice_fusion
  9.0 0.2 copy.21
  9.2 0.8 pad.4.ctx_ref
  9.9 65.7 %exchange.2 = bf16[16,64,1280]{2,1,0:T(8,128)(2,1)} custom-call(bf16[16,64,1280]{2,1,0:T(8,128)(2,1)} %bitcast.30), custom_call_target="tpu_custom_call" | custom-call | tf_op jit(solution)/shard_map/exchange/pallas_call | solution.py:94
  75.6 82.2 %res_block.2.h_ref = bf16[1024,1280]{1,0:T(8,128)(2,1)} custom-call(bf16[1024,1280]{1,0:T(8,128)(2,1)} %bitcast.32, bf16[2,2,3,3,1280,1280]{5,4,3,2,1,0:T(8,128)(2,1)} %kern.3, f32[4,1280]{1,0:T(4,128)} %squeeze.12.norm_ref, f32[1,1280]{1,0:T(1,128)} %get-tuple-element.8.time_ref), custom_call_target="tpu_custom_call" | custom-call | flops 60397977600 | bytes 58982400 | tf_op jit(solution)/shard_map/res_block/pallas_call | solution.py:187
  157.9 127.6 %transformer.1.x_ref = bf16[1024,1280]{1,0:T(8,128)(2,1)} custom-call(bf16[1024,1280]{1,0:T(8,128)(2,1)} %res_block.2.h_ref, bf16[80,2048]{1,0:T(8,128)(2,1)} %pad.4.ctx_ref, f32[2,1280]{1,0:T(2,128)} %reshape.59.norm_ref, bf16[2,1280,1280]{2,1,0:T(8,128)(2,1)} %pio.1, bf16[3,1280,1280]{2,1,0:T(8,128)(2,1)} %bitcast.36, bf16[1280,1280]{1,0:T(8,128)(2,1)} %bitcast.37, ...), custom_call_target="tpu_custom_call" | custom-call | flops 72477573120 | bytes 80000000 | tf_op jit(solution)/shard_map/transformer/pallas_call | solution.py:437
  285.5 82.4 %res_block.3 = bf16[1024,1280]{1,0:T(8,128)(2,1)} custom-call(bf16[1024,1280]{1,0:T(8,128)(2,1)} %transformer.1.x_ref, bf16[2,2,3,3,1280,1280]{5,4,3,2,1,0:T(8,128)(2,1)} %kern.3, f32[4,1280]{1,0:T(4,128)} %squeeze.14.norm_ref, f32[1,1280]{1,0:T(1,128)} %get-tuple-element.7.time_ref), custom_call_target="tpu_custom_call" | custom-call | flops 60397977600 | bytes 58982400 | tf_op jit(solution)/shard_map/res_block/pallas_call | solution.py:187
  367.9 65.0 %exchange.3 = bf16[16,64,1280]{2,1,0:T(8,128)(2,1)} custom-call(bf16[16,64,1280]{2,1,0:T(8,128)(2,1)} %bitcast.31), custom_call_target="tpu_custom_call" | custom-call | tf_op jit(solution)/shard_map/exchange/pallas_call | solution.py:94
  432.9 3.5 copy.24
  (2 shorter events, 0.0 us)
Async XLA Ops:
  0.0 4.5 %copy-start.1 = (bf16[2,32,40]{2,1,0:T(8,128)(2,1)S(1)}, bf16[2,32,40]{2,1,0:T(8,128)(2,1)}, u32[]{:S(2)}) copy-start(bf16[2,32,40]{2,1,0:T(8,128)(2,1)} %param.21) | copy-start | bytes 15364
  0.0 5.2 %copy-start = (bf16[2,2,2,32,40]{4,3,2,1,0:T(8,128)(2,1)S(1)}, bf16[2,2,2,32,40]{4,3,2,1,0:T(8,128)(2,1)}, u32[]{:S(2)}) copy-start(bf16[2,2,2,32,40]{4,3,2,1,0:T(8,128)(2,1)} %param.20) | copy-start | bytes 61444

commit v3 on v2

--- a/solution.py
+++ b/solution.py
@@ -66,140 +66,300 @@
     return (centred * lax.rsqrt(jnp.mean(centred * centred, axis=-1, keepdims=True) + LN_EPS)).astype(BF16)
 
 
-def exchange(blocks, collective):
-    num = blocks.shape[0]
-
-    def kernel(src, dst, stage, send_sem, recv_sem, own_sem):
+def meet(peers, me):
+    barrier = pltpu.get_barrier_semaphore()
+
+    @pl.loop(1, peers)
+    def _(step):
+        pl.semaphore_signal(barrier, inc=1, device_id={'sp': lax.rem(me + step, peers)}, device_id_type=MESH)
+
+
+def await_peers(peers):
+    pl.semaphore_wait(pltpu.get_barrier_semaphore(), peers - 1)
+
+
+def drain(ref, sem):
+    pltpu.make_async_copy(ref, ref, sem).wait()
+
+
+def chunk_cols(chunk):
+    return pl.ds(pl.multiple_of(chunk * CK, CK), CK)
+
+
+def tile_rows(tile):
+    return pl.ds(pl.multiple_of(tile * TM, TM), TM)
+
+
+def activate(src, act, coef, chunk, tile, width):
+    cols = chunk_cols(chunk)
+    half = src[tile_rows(tile), cols].astype(F32) * coef[0:1, cols] + coef[1:2, cols]
+    vals = half + half * jnp.tanh(half)
+    column = lax.rem(lax.broadcasted_iota(jnp.int32, (TM, CK), 0), width)
+    put = pl.ds(pl.multiple_of(tile * TM + width, width), TM)
+    act[0, put, cols] = jnp.where(column == 0, 0.0, pltpu.roll(vals, 1, 0)).astype(BF16)
+    act[1, put, cols] = vals.astype(BF16)
+    act[2, put, cols] = jnp.where(column == width - 1, 0.0, pltpu.roll(vals, TM - 1, 0)).astype(BF16)
+
+
+def clear_edges(act, tokens, width):
+    edge = jnp.zeros((width, act.shape[2]), BF16)
+    for shift in range(3):
+        act[shift, 0:width, :] = edge
+        act[shift, width + tokens:2 * width + tokens, :] = edge
+
+
+def shifted(act, shift, tile, row, width, cols):
+    return act[shift, pl.ds(pl.multiple_of(tile * TM + row * width, width), TM), cols]
+
+
+def fetch_rows(kern, which, conv, chunk, wbuf, slot, sem):
+    return [pltpu.make_async_copy(kern.at[which, conv, dy, dx, chunk_cols(chunk), :], wbuf.at[slot, dy, pl.ds(dx * CK, CK), :], sem.at[slot])
+            for dy in range(3) for dx in range(3)]
+
+
+def fetch_cols(kern, which, conv, chunk, wbuf, slot, sem):
+    return [pltpu.make_async_copy(kern.at[which, conv, dy, dx, :, chunk_cols(chunk)], wbuf.at[slot, 3 * dy + dx], sem.at[slot])
+            for dy in range(3) for dx in range(3)]
+
+
+def rows_product(act, wbuf, slot, chunk, tile, width):
+    cols = chunk_cols(chunk)
+    part = None
+    for dy in range(3):
+        for dx in range(3):
+            term = nn(shifted(act, dx, tile, dy, width, cols), wbuf[slot, dy, dx * CK:(dx + 1) * CK, :])
+            part = term if part is None else part + term
+    return part
+
+
+def conv_rows(kern, which, conv, src, act, wbuf, wsem, coef, acc, tokens, width, ready):
+    tiles = tokens // TM
+    chunks = act.shape[2] // CK
+    acc[...] = jnp.zeros_like(acc)
+    if ready is None:
+        @pl.loop(0, tiles)
+        def _(tile):
+            activate(src, act, coef, 0, tile, width)
+
+    @pl.loop(0, chunks)
+    def _(chunk):
+        slot = lax.rem(chunk, 2)
+
+        @pl.when(chunk + 1 < chunks)
+        def _():
+            for copy in fetch_rows(kern, which, conv, chunk + 1, wbuf, 1 - slot, wsem):
+                copy.start()
+
+        for copy in fetch_rows(kern, which, conv, chunk, wbuf, slot, wsem):
+            copy.wait()
+        if ready is not None:
+            ready(chunk)
+
+            @pl.loop(0, tiles)
+            def _(tile):
+                activate(src, act, coef, chunk, tile, width)
+
+        @pl.loop(0, tiles)
+        def _(tile):
+            acc[tile_rows(tile), :] += rows_product(act, wbuf, slot, chunk, tile, width)
+            if ready is None:
+                activate(src, act, coef, lax.rem(chunk + 1, chunks), tile, width)
+
+
+def add_rows(dst, src, other):
+    @pl.loop(0, src.shape[0] // 64)
+    def _(idx):
+        rows = pl.ds(pl.multiple_of(idx * 64, 64), 64)
+        dst[rows, :] = (src[rows, :] + (other[0:1, :] if other.shape[0] == 1 else other[rows, :]).astype(F32)).astype(BF16)
+
+
+def res_block_in(latent, res_conv, norms, time_proj, which, width, groups):
+    peers, band, chans = latent.shape
+    tokens = peers * band
+    chunks = chans // CK
+    count = float(tokens * (chans // groups))
+
+    def kernel(lat, kern, norm_ref, time_ref, out_ref, own, image, mid, act, wbuf, acc, mine, stats, coef, wsem, own_sem, send_sem, recv_sem, stat_send, stat_recv):
         me = lax.axis_index('sp')
-        barrier = pltpu.get_barrier_semaphore()
-        for step in range(1, num):
-            pl.semaphore_signal(barrier, inc=1, device_id={'sp': lax.rem(me + step, num)}, device_id_type=MESH)
-        pl.semaphore_wait(barrier, num - 1)
-        copies = []
-        order = sorted(range(1, num), key=lambda step: -min(step, num - step))
-        for step in order:
-            peer = lax.rem(me + step, num)
-            copy = pltpu.make_async_remote_copy(src.at[peer], dst.at[me], send_sem.at[step], recv_sem.at[step], device_id={'sp': peer}, device_id_type=MESH)
+        load = pltpu.make_async_copy(lat, own, own_sem)
+        load.start()
+        for copy in fetch_rows(kern, which, 0, 0, wbuf, 0, wsem):
             copy.start()
-            copies.append(copy)
-        own_in = pltpu.make_async_copy(src.at[me], stage, own_sem)
-        own_in.start()
-        own_in.wait()
-        own_out = pltpu.make_async_copy(stage, dst.at[me], own_sem)
-        own_out.start()
-        own_out.wait()
-        for copy in copies:
-            copy.wait()
-
+        meet(peers, me)
+        clear_edges(act, tokens, width)
+        load.wait()
+
+        @pl.loop(0, peers)
+        def _(peer):
+            vals = own[peer].astype(F32)
+            mine[peer, 0:1, :] = jnp.sum(vals, axis=0, keepdims=True)
+            mine[peer, 1:2, :] = jnp.sum(vals * vals, axis=0, keepdims=True)
+
+        await_peers(peers)
+
+        def peer_of(step):
+            return lax.rem(me + step, peers)
+
+        @pl.loop(1, peers)
+        def _(step):
+            peer = peer_of(step)
+            pltpu.make_async_remote_copy(mine.at[peer], stats.at[me], stat_send, stat_recv, device_id={'sp': peer}, device_id_type=MESH).start()
+
+        for chunk in range(chunks):
+            @pl.loop(1, peers)
+            def _(step):
+                peer = peer_of(step)
+                cols = pl.ds(chunk * CK, CK)
+                pltpu.make_async_remote_copy(
+                    own.at[peer, :, cols], image.at[pl.ds(pl.multiple_of(me * band, band), band), cols], send_sem.at[chunk], recv_sem.at[chunk],
+                    device_id={'sp': peer}, device_id_type=MESH).start()
+
+        image[pl.ds(pl.multiple_of(me * band, band), band), :] = own[me]
+        stats[me] = mine[me]
+        others = pl.ds(0, tokens - band)
+        drain(stats.at[pl.ds(0, peers - 1)], stat_recv)
+        tot, sqr = stats[0, 0:1, :], stats[0, 1:2, :]
+        for peer in range(1, peers):
+            tot, sqr = tot + stats[peer, 0:1, :], sqr + stats[peer, 1:2, :]
+        group_affine(tot, sqr, norm_ref[0:1], norm_ref[1:2], groups, count, coef, 0.5)
+        conv_rows(kern, which, 0, image, act, wbuf, wsem, coef, acc, tokens, width,
+                  lambda chunk: drain(image.at[others, chunk_cols(chunk)], recv_sem.at[chunk]))
+        for copy in fetch_rows(kern, which, 1, 0, wbuf, 0, wsem):
+            copy.start()
+        add_rows(mid, acc, time_ref)
+        tot, sqr = channel_sums(mid, tokens, chans)
+        group_affine(tot, sqr, norm_ref[2:3], norm_ref[3:4], groups, count, coef, 0.5)
+        conv_rows(kern, which, 1, mid, act, wbuf, wsem, coef, acc, tokens, width, None)
+        add_rows(out_ref, acc, image)
+        drain(stats.at[pl.ds(0, peers - 1)], stat_send)
+        for chunk in range(chunks):
+            drain(image.at[others, chunk_cols(chunk)], send_sem.at[chunk])
+
+    vmem = pl.BlockSpec(memory_space=pltpu.VMEM)
+    hbm = pl.BlockSpec(memory_space=pl.ANY)
     return pl.pallas_call(
         kernel,
-        out_shape=jax.ShapeDtypeStruct(blocks.shape, blocks.dtype),
-        in_specs=[pl.BlockSpec(memory_space=pl.ANY)],
-        out_specs=pl.BlockSpec(memory_space=pl.ANY),
-        scratch_shapes=[pltpu.VMEM(blocks.shape[1:], blocks.dtype), pltpu.SemaphoreType.DMA((num,)), pltpu.SemaphoreType.DMA((num,)), pltpu.SemaphoreType.DMA],
-        compiler_params=pltpu.CompilerParams(collective_id=collective, has_side_effects=True),
-        name='exchange',
-    )(blocks)
-
-
-def res_block(hidden, res_conv, norms, time_proj, which, width, groups):
+        out_shape=jax.ShapeDtypeStruct((tokens, chans), BF16),
+        in_specs=[hbm, hbm, vmem, vmem],
+        out_specs=vmem,
+        scratch_shapes=[
+            pltpu.VMEM(latent.shape, BF16),
+            pltpu.VMEM((tokens, chans), BF16),
+            pltpu.VMEM((tokens, chans), BF16),
+            pltpu.VMEM((3, tokens + 2 * width, chans), BF16),
+            pltpu.VMEM((2, 3, 3 * CK, chans), BF16),
+            pltpu.VMEM((tokens, chans), F32),
+            pltpu.VMEM((peers, 2, chans), F32),
+            pltpu.VMEM((peers, 2, chans), F32),
+            pltpu.VMEM((8, chans), F32),
+            pltpu.SemaphoreType.DMA((2,)),
+            pltpu.SemaphoreType.DMA,
+            pltpu.SemaphoreType.DMA((chunks,)),
+            pltpu.SemaphoreType.DMA((chunks,)),
+            pltpu.SemaphoreType.DMA,
+            pltpu.SemaphoreType.DMA,
+        ],
+        compiler_params=pltpu.CompilerParams(vmem_limit_bytes=VMEM_LIMIT, collective_id=0, has_side_effects=True),
+        cost_estimate=pl.CostEstimate(flops=36 * tokens * chans * chans, bytes_accessed=36 * chans * chans, transcendentals=0),
+        name='res_block_in',
+    )(latent, res_conv, norms, time_proj)
+
+
+def res_block_out(hidden, res_conv, norms, time_proj, which, width, groups, peers):
     tokens, chans = hidden.shape
+    band = tokens // peers
     chunks = chans // CK
     tiles = tokens // TM
+    per_tile = TM // band
     count = float(tokens * (chans // groups))
 
-    def kernel(x_ref, kern, norm_ref, time_ref, out_ref, acc, mid, act, wbuf, coef, wsem):
-        def fetch(step, slot):
-            conv, chunk = step // chunks, lax.rem(step, chunks)
-            rows = pl.ds(pl.multiple_of(chunk * CK, CK), CK)
-            return [pltpu.make_async_copy(kern.at[which, conv, dy, dx, rows, :], wbuf.at[slot, dy, pl.ds(dx * CK, CK), :], wsem.at[slot])
-                    for dy in range(3) for dx in range(3)]
-
-        for copy in fetch(0, 0):
+    def kernel(x_ref, kern, norm_ref, time_ref, out_ref, mid, act, wbuf, cbuf, acc, result, coef, wsem, csem, own_sem, send_sem, recv_sem):
+        me = lax.axis_index('sp')
+        for copy in fetch_rows(kern, which, 0, 0, wbuf, 0, wsem):
             copy.start()
-        edge = jnp.zeros((width, 3 * CK), BF16)
-        for slot in range(2):
-            act[slot, 0:width, :] = edge
-            act[slot, width + tokens:2 * width + tokens, :] = edge
-        column = lax.rem(lax.broadcasted_iota(jnp.int32, (TM, CK), 0), width)
-
-        def build(src, chunk, tile, slot):
-            cols = pl.ds(pl.multiple_of(chunk * CK, CK), CK)
-            rows = pl.multiple_of(tile * TM, TM)
-            vals = src[pl.ds(rows, TM), cols].astype(F32)
-            half = vals * coef[0:1, cols] + coef[1:2, cols]
-            vals = half + half * jnp.tanh(half)
-            put = pl.ds(rows + width, TM)
-            act[slot, put, 0:CK] = jnp.where(column == 0, 0.0, pltpu.roll(vals, 1, 0)).astype(BF16)
-            act[slot, put, CK:2 * CK] = vals.astype(BF16)
-            act[slot, put, 2 * CK:3 * CK] = jnp.where(column == width - 1, 0.0, pltpu.roll(vals, TM - 1, 0)).astype(BF16)
-
-        def conv(src, index):
+        meet(peers, me)
+        clear_edges(act, tokens, width)
+        tot, sqr = channel_sums(x_ref, tokens, chans)
+        group_affine(tot, sqr, norm_ref[0:1], norm_ref[1:2], groups, count, coef, 0.5)
+        conv_rows(kern, which, 0, x_ref, act, wbuf, wsem, coef, acc, tokens, width, None)
+        for copy in fetch_cols(kern, which, 1, 0, cbuf, 0, csem):
+            copy.start()
+        add_rows(mid, acc, time_ref)
+        tot, sqr = channel_sums(mid, tokens, chans)
+        group_affine(tot, sqr, norm_ref[2:3], norm_ref[3:4], groups, count, coef, 0.5)
+
+        @pl.loop(0, chunks)
+        def _(chunk):
             @pl.loop(0, tiles)
             def _(tile):
-                build(src, 0, tile, 0)
-
-            acc[...] = jnp.zeros_like(acc)
-
-            @pl.loop(0, chunks)
-            def _(chunk):
-                step = index * chunks + chunk
-                wslot = lax.rem(step, 2)
-                slot = lax.rem(chunk, 2)
-
-                @pl.when(step + 1 < 2 * chunks)
-                def _():
-                    for copy in fetch(step + 1, 1 - wslot):
-                        copy.start()
-
-                for copy in fetch(step, wslot):
-                    copy.wait()
-
-                @pl.loop(0, tiles)
-                def _(tile):
-                    rows = pl.multiple_of(tile * TM, TM)
-                    part = nn(act[slot, pl.ds(rows, TM), :], wbuf[wslot, 0])
-                    part += nn(act[slot, pl.ds(rows + width, TM), :], wbuf[wslot, 1])
-                    part += nn(act[slot, pl.ds(rows + 2 * width, TM), :], wbuf[wslot, 2])
-                    acc[pl.ds(rows, TM), :] += part
-                    build(src, lax.rem(chunk + 1, chunks), tile, 1 - slot)
-
-        tot, sqr = channel_sums(x_ref, tokens, chans)
-        group_affine(tot, sqr, norm_ref[0:1], norm_ref[1:2], groups, count, coef, 0.5)
-        conv(x_ref, 0)
-
-        @pl.loop(0, tokens // 64)
-        def _(idx):
-            rows = pl.ds(pl.multiple_of(idx * 64, 64), 64)
-            mid[rows, :] = (acc[rows, :] + time_ref[0:1]).astype(BF16)
-
-        tot, sqr = channel_sums(mid, tokens, chans)
-        group_affine(tot, sqr, norm_ref[2:3], norm_ref[3:4], groups, count, coef, 0.5)
-        conv(mid, 1)
-
-        @pl.loop(0, tokens // 64)
-        def _(idx):
-            rows = pl.ds(pl.multiple_of(idx * 64, 64), 64)
-            out_ref[rows, :] = (x_ref[rows, :].astype(F32) + acc[rows, :]).astype(BF16)
-
-    flops = 2 * 2 * 9 * tokens * chans * chans
+                activate(mid, act, coef, chunk, tile, width)
+
+        await_peers(peers)
+        turn = lax.div(me, per_tile) + tiles // 2
+
+        @pl.loop(0, chunks)
+        def _(chunk):
+            slot = lax.rem(chunk, 2)
+            cols = chunk_cols(chunk)
+
+            @pl.when(chunk + 1 < chunks)
+            def _():
+                for copy in fetch_cols(kern, which, 1, chunk + 1, cbuf, 1 - slot, csem):
+                    copy.start()
+
+            for copy in fetch_cols(kern, which, 1, chunk, cbuf, slot, csem):
+                copy.wait()
+
+            @pl.loop(0, tiles)
+            def _(step):
+                tile = lax.rem(step + turn, tiles)
+                part = None
+                for dy in range(3):
+                    for dx in range(3):
+                        term = nn(shifted(act, dx, tile, dy, width, slice(None)), cbuf[slot, 3 * dy + dx])
+                        part = term if part is None else part + term
+                rows = tile_rows(tile)
+                result[rows, cols] = (x_ref[rows, cols].astype(F32) + part).astype(BF16)
+                for idx in range(per_tile):
+                    peer = tile * per_tile + idx
+                    block = result.at[pl.ds(pl.multiple_of(peer * band, band), band), cols]
+
+                    @pl.when(peer == me)
+                    def _():
+                        pltpu.make_async_copy(block, out_ref.at[me, :, cols], own_sem).start()
+
+                    @pl.when(peer != me)
+                    def _():
+                        pltpu.make_async_remote_copy(block, out_ref.at[me, :, cols], send_sem, recv_sem, device_id={'sp': peer}, device_id_type=MESH).start()
+
+        pltpu.make_async_copy(result.at[pl.ds(0, band), :], out_ref.at[me], own_sem).wait()
+        drain(result.at[pl.ds(0, tokens - band), :], send_sem)
+        drain(out_ref.at[pl.ds(0, peers - 1)], recv_sem)
+
     vmem = pl.BlockSpec(memory_space=pltpu.VMEM)
+    hbm = pl.BlockSpec(memory_space=pl.ANY)
     return pl.pallas_call(
         kernel,
-        out_shape=jax.ShapeDtypeStruct(hidden.shape, BF16),
-        in_specs=[vmem, pl.BlockSpec(memory_space=pl.ANY), vmem, vmem],
-        out_specs=vmem,
+        out_shape=jax.ShapeDtypeStruct((peers, band, chans), BF16),
+        in_specs=[vmem, hbm, vmem, vmem],
+        out_specs=hbm,
         scratch_shapes=[
+            pltpu.VMEM((tokens, chans), BF16),
+            pltpu.VMEM((3, tokens + 2 * width, chans), BF16),
+            pltpu.VMEM((2, 3, 3 * CK, chans), BF16),
+            pltpu.VMEM((2, 9, chans, CK), BF16),
             pltpu.VMEM((tokens, chans), F32),
             pltpu.VMEM((tokens, chans), BF16),
-            pltpu.VMEM((2, tokens + 2 * width, 3 * CK), BF16),
-            pltpu.VMEM((2, 3, 3 * CK, chans), BF16),
             pltpu.VMEM((8, chans), F32),
             pltpu.SemaphoreType.DMA((2,)),
+            pltpu.SemaphoreType.DMA((2,)),
+            pltpu.SemaphoreType.DMA,
+            pltpu.SemaphoreType.DMA,
+            pltpu.SemaphoreType.DMA,
         ],
-        compiler_params=pltpu.CompilerParams(vmem_limit_bytes=VMEM_LIMIT),
-        cost_estimate=pl.CostEstimate(flops=flops, bytes_accessed=2 * 9 * chans * chans * 2, transcendentals=0),
-        name='res_block',
+        compiler_params=pltpu.CompilerParams(vmem_limit_bytes=VMEM_LIMIT, collective_id=1, has_side_effects=True),
+        cost_estimate=pl.CostEstimate(flops=36 * tokens * chans * chans, bytes_accessed=36 * chans * chans, transcendentals=0),
+        name='res_block_out',
     )(hidden, res_conv, norms, time_proj)
 
 
@@ -252,9 +412,6 @@
             ]
 
         start('in', 'q', 'k', 'v', 'ck0', 'ck1')
-
-        def tile_rows(tile):
-            return pl.ds(pl.multiple_of(tile * TM, TM), TM)
 
         tot, sqr = channel_sums(h_ref, tokens, chans)
         group_affine(tot, sqr, norm_ref[0:1], norm_ref[1:2], groups, count, coef, 1.0)
@@ -470,7 +627,6 @@
         text, text_dim = context.shape[1:]
         me = lax.axis_index('sp')
 
-        image = exchange(latent.reshape(images, band, chans), 0).reshape(images * band, chans)
         time_row = lax.dynamic_slice_in_dim(time_emb, me, 1, 0)
         time_act = jax.nn.silu(time_row.astype(F32)).astype(BF16)
         time_proj = jnp.einsum('tc,bcd->btd', time_act, res_time, preferred_element_type=F32)
@@ -479,7 +635,7 @@
         ctx = lax.dynamic_index_in_dim(context, me, 0, keepdims=False)
         ctx = jnp.pad(ctx, ((0, ctx_rows - text), (0, 0)))
 
-        first = res_block(image, res_conv, norms[0], time_proj[0], 0, width, groups)
+        first = res_block_in(latent.reshape(images, band, chans), res_conv, norms[0], time_proj[0], 0, width, groups)
         middle = transformer(
             first, ctx, attn_norm.astype(F32).reshape(2, chans), proj_inout,
             jnp.transpose(self_qkv, (0, 2, 3, 1)).reshape(3, chans, chans),
@@ -487,8 +643,7 @@
             jnp.transpose(cross_q, (1, 2, 0)).reshape(chans, chans),
             jnp.transpose(cross_kv, (0, 2, 3, 1)).reshape(2, chans, text_dim),
             cross_out.reshape(chans, chans), ff_in, ff_out, groups, heads, text)
-        last = res_block(middle, res_conv, norms[1], time_proj[1], 1, width, groups)
-        out = exchange(last.reshape(num_bands, band, chans), 1)
+        out = res_block_out(middle, res_conv, norms[1], time_proj[1], 1, width, groups, num_bands)
         return out.reshape(latent.shape)
 
     band_spec = P('dp', 'sp', None, None)

time: 437 us -> 366 us (0.84)
  Pallas kernels: 423 us -> 352 us
    pallas_call x4 -> x2, Pallas kernels: 295 us -> 225 us  [the longest x1 122 us: res_block_in(): pl.pallas_call(kernel, out_shape=jax.ShapeDtypeStruct((tokens, chans), BF...]
where the time goes in v3:
time: 366 us
  Pallas kernels  352 us (96%)
  local copies, waits for them, and re-layouts  9.52 us (3%)
  matrix products  3.86 us (1%)
    pallas_call x1, Pallas kernels, transformer(): pl.pallas_call(kernel, out_shape=jax.ShapeDtypeStruct(hidden.shape, BF16)...  128 us
    pallas_call x1, Pallas kernels, res_block_in(): pl.pallas_call(kernel, out_shape=jax.ShapeDtypeStruct((tokens, chans), BF...  122 us
    pallas_call x1, Pallas kernels, res_block_out(): pl.pallas_call(kernel, out_shape=jax.ShapeDtypeStruct((peers, band, chans...  102 us

profile of v3, /device:TPU:30, one launch (start us, length us, event | category | flops | bytes accessed | tf_op | source)
XLA Modules:
  0.0 365.9 jit_solution(9429447319379159628)
XLA Ops:
  0.0 0.0 copy-start.1
  0.0 0.0 copy-start
  0.0 3.9 %fusion = f32[1,2,1280]{2,0,1:T(1,128)S(1)} fusion(bf16[2,1280,1280]{2,1,0:T(8,128)(2,1)} %param.19, bf16[16,1280]{1,0:T(8,128)(2,1)} %param.16, s32[]{:T(128)S(6)} %select_n.5), kind=kOutput, calls=%fused_computation.3 | convolution fusion | flops 6561280 | bytes 6568964 | tf_op jit(solution)/shard_map/tc,bcd->btd/dot_general | solution.py:632
  3.9 0.6 fusion.11
  4.5 0.0 copy-done.1
  4.5 0.7 reshape.51.norm_ref
  5.2 0.0 copy-done
  5.2 0.7 squeeze.14.norm_ref
  5.9 0.7 squeeze.12.norm_ref
  6.6 2.4 constant_dynamic-slice_fusion
  9.0 0.2 copy.21
  9.2 0.8 pad.4.ctx_ref
  9.9 122.4 %res_block_in.1.h_ref = bf16[1024,1280]{1,0:T(8,128)(2,1)} custom-call(bf16[16,64,1280]{2,1,0:T(8,128)(2,1)} %bitcast.35, bf16[2,2,3,3,1280,1280]{5,4,3,2,1,0:T(8,128)(2,1)} %kern.3, f32[4,1280]{1,0:T(4,128)} %squeeze.12.norm_ref, f32[1,1280]{1,0:T(1,128)} %get-tuple-element.8.time_ref), custom_call_target="tpu_custom_call" | custom-call | flops 60397977600 | bytes 58982400 | tf_op jit(solution)/shard_map/res_block_in/pallas_call | solution.py:240
  132.4 127.6 %transformer.1.x_ref = bf16[1024,1280]{1,0:T(8,128)(2,1)} custom-call(bf16[1024,1280]{1,0:T(8,128)(2,1)} %res_block_in.1.h_ref, bf16[80,2048]{1,0:T(8,128)(2,1)} %pad.4.ctx_ref, f32[2,1280]{1,0:T(2,128)} %reshape.51.norm_ref, bf16[2,1280,1280]{2,1,0:T(8,128)(2,1)} %pio.1, bf16[3,1280,1280]{2,1,0:T(8,128)(2,1)} %bitcast.31, bf16[1280,1280]{1,0:T(8,128)(2,1)} %bitcast.32, ...), custom_call_target="tpu_custom_call" | custom-call | flops 72477573120 | bytes 80000000 | tf_op jit(solution)/shard_map/transformer/pallas_call | solution.py:594
  259.9 102.5 %res_block_out.1 = bf16[16,64,1280]{2,1,0:T(8,128)(2,1)} custom-call(bf16[1024,1280]{1,0:T(8,128)(2,1)} %transformer.1.x_ref, bf16[2,2,3,3,1280,1280]{5,4,3,2,1,0:T(8,128)(2,1)} %kern.3, f32[4,1280]{1,0:T(4,128)} %squeeze.14.norm_ref, f32[1,1280]{1,0:T(1,128)} %get-tuple-element.7.time_ref), custom_call_target="tpu_custom_call" | custom-call | flops 60397977600 | bytes 58982400 | tf_op jit(solution)/shard_map/res_block_out/pallas_call | solution.py:341
  362.4 3.5 copy.24
  (2 shorter events, 0.0 us)
Async XLA Ops:
  0.0 4.5 %copy-start.1 = (bf16[2,32,40]{2,1,0:T(8,128)(2,1)S(1)}, bf16[2,32,40]{2,1,0:T(8,128)(2,1)}, u32[]{:S(2)}) copy-start(bf16[2,32,40]{2,1,0:T(8,128)(2,1)} %param.21) | copy-start | bytes 15364
  0.0 5.2 %copy-start = (bf16[2,2,2,32,40]{4,3,2,1,0:T(8,128)(2,1)S(1)}, bf16[2,2,2,32,40]{4,3,2,1,0:T(8,128)(2,1)}, u32[]{:S(2)}) copy-start(bf16[2,2,2,32,40]{4,3,2,1,0:T(8,128)(2,1)} %param.20) | copy-start | bytes 61444

commit v4 on v2

--- a/solution.py
+++ b/solution.py
@@ -42,18 +42,56 @@
     return lax.fori_loop(0, rows // 64, step, (zero, zero))
 
 
-def group_affine(tot, sqr, gain, shift, groups, count, coef, factor):
-    chans = tot.shape[1]
+def layer_norm(tokens):
+    centred = tokens - jnp.mean(tokens, axis=-1, keepdims=True)
+    return (centred * lax.rsqrt(jnp.mean(centred * centred, axis=-1, keepdims=True) + LN_EPS)).astype(BF16)
+
+
+def meet(peers, me):
+    barrier = pltpu.get_barrier_semaphore()
+
+    @pl.loop(1, peers)
+    def _(step):
+        pl.semaphore_signal(barrier, inc=1, device_id={'sp': lax.rem(me + step, peers)}, device_id_type=MESH)
+
+
+def await_peers(peers):
+    pl.semaphore_wait(pltpu.get_barrier_semaphore(), peers - 1)
+
+
+def drain(ref, sem):
+    pltpu.make_async_copy(ref, ref, sem).wait()
+
+
+def remote(src, dst, send_sem, recv_sem, peer):
+    return pltpu.make_async_remote_copy(src, dst, send_sem, recv_sem, device_id={'sp': peer}, device_id_type=MESH)
+
+
+def chunk_cols(chunk):
+    return pl.ds(pl.multiple_of(chunk * CK, CK), CK)
+
+
+def tile_rows(tile, first=0):
+    return pl.ds(pl.multiple_of(first + tile * TM, 32), TM)
+
+
+def members(chans, groups, offset=0):
     width = chans // groups
-    terms = split3(jnp.sum(tot, axis=0, keepdims=True)) + split3(jnp.sum(sqr, axis=0, keepdims=True))
-    rows = jnp.concatenate(terms + [jnp.zeros((2, chans), F32)], axis=0).astype(BF16)
     chan = lax.broadcasted_iota(jnp.int32, (chans, 128), 0)
-    low = lax.broadcasted_iota(jnp.int32, (chans, 128), 1) * width
-    member = jnp.where((chan >= low) & (chan < low + width), 1.0, 0.0).astype(BF16)
-    sums = nn(rows, member)
-    mean = (sums[0:1] + sums[1:2] + sums[2:3]) / count
-    msq = (sums[3:4] + sums[4:5] + sums[5:6]) / count
-    rstd = lax.rsqrt(msq - mean * mean + GN_EPS)
+    low = (lax.broadcasted_iota(jnp.int32, (chans, 128), 1) - offset) * width
+    return jnp.where((chan >= low) & (chan < low + width), 1.0, 0.0).astype(BF16)
+
+
+def group_sums(rows, member):
+    count = rows.shape[0]
+    high, mid, low = split3(rows)
+    sums = nn(jnp.concatenate([high, mid, low], axis=0).astype(BF16), member)
+    return sums[0:count] + sums[count:2 * count] + sums[2 * count:3 * count]
+
+
+def group_affine(sums, gain, shift, member, count, coef, factor):
+    mean = sums[0:1] / count
+    rstd = lax.rsqrt(sums[1:2] / count - mean * mean + GN_EPS)
     back = jnp.concatenate(split3(mean) + split3(rstd) + [jnp.zeros((2, 128), F32)], axis=0).astype(BF16)
     wide = nt(back, member)
     scale = (wide[3:4] + wide[4:5] + wide[5:6]) * gain
@@ -61,151 +99,457 @@
     coef[1:2, :] = factor * (shift - (wide[0:1] + wide[1:2] + wide[2:3]) * scale)
 
 
-def layer_norm(tokens):
-    centred = tokens - jnp.mean(tokens, axis=-1, keepdims=True)
-    return (centred * lax.rsqrt(jnp.mean(centred * centred, axis=-1, keepdims=True) + LN_EPS)).astype(BF16)
-
-
-def exchange(blocks, collective):
-    num = blocks.shape[0]
-
-    def kernel(src, dst, stage, send_sem, recv_sem, own_sem):
+def two_rows(tot, sqr):
+    rows = [jnp.sum(tot, axis=0, keepdims=True), jnp.sum(sqr, axis=0, keepdims=True)]
+    return jnp.concatenate(rows + [jnp.zeros((6, tot.shape[1]), F32)], axis=0)
+
+
+def activate(src, first, act, put, count, coef, chunk, width):
+    cols = chunk_cols(chunk)
+    half = src[pl.ds(pl.multiple_of(first, width), count), cols].astype(F32) * coef[0:1, cols] + coef[1:2, cols]
+    vals = half + half * jnp.tanh(half)
+    column = lax.rem(lax.broadcasted_iota(jnp.int32, (count, CK), 0), width)
+    rows = pl.ds(pl.multiple_of(put, width), count)
+    act[0, rows, cols] = jnp.where(column == 0, 0.0, pltpu.roll(vals, 1, 0)).astype(BF16)
+    act[1, rows, cols] = vals.astype(BF16)
+    act[2, rows, cols] = jnp.where(column == width - 1, 0.0, pltpu.roll(vals, count - 1, 0)).astype(BF16)
+
+
+def clear_edges(act, width):
+    edge = jnp.zeros((width, act.shape[2]), BF16)
+    for shift in range(3):
+        act[shift, 0:width, :] = edge
+        act[shift, act.shape[1] - width:act.shape[1], :] = edge
+
+
+def shifted(act, shift, tile, row, width, cols):
+    return act[shift, tile_rows(tile, row * width), cols]
+
+
+def fetch_rows(kern, which, conv, chunk, wbuf, sem):
+    slot = lax.rem(chunk, 2)
+    return [pltpu.make_async_copy(kern.at[which, conv, dy, dx, chunk_cols(chunk), :], wbuf.at[slot, dy, pl.ds(dx * CK, CK), :], sem.at[slot])
+            for dy in range(3) for dx in range(3)]
+
+
+def fetch_cols(kern, which, conv, chunk, wbuf, sem):
+    slot = lax.rem(chunk, 2)
+    return [pltpu.make_async_copy(kern.at[which, conv, dy, dx, :, chunk_cols(chunk)], wbuf.at[slot, 3 * dy + dx], sem.at[slot])
+            for dy in range(3) for dx in range(3)]
+
+
+def start_all(copies):
+    for copy in copies:
+        copy.start()
+
+
+def wait_all(copies):
+    for copy in copies:
+        copy.wait()
+
+
+def conv_rows(fetch, parts, act, wbuf, coef, acc, width, ready):
+    tokens, chans = acc.shape
+    tiles = tokens // TM
+    chunks = chans // CK
+    (src, first, put, _), (halo, halo_first, halo_put, halo_rows) = parts
+    acc[...] = jnp.zeros_like(acc)
+
+    def build_tile(chunk, tile):
+        activate(src, first + tile * TM, act, put + tile * TM, TM, coef, chunk, width)
+
+    def build_halo(chunk):
+        activate(halo, halo_first, act, halo_put, halo_rows, coef, chunk, width)
+
+    if ready is None:
+        build_halo(0)
+
+        @pl.loop(0, tiles)
+        def _(tile):
+            build_tile(0, tile)
+
+    @pl.loop(0, chunks)
+    def _(chunk):
+        slot = lax.rem(chunk, 2)
+
+        @pl.when(chunk + 1 < chunks)
+        def _():
+            start_all(fetch(chunk + 1))
+
+        wait_all(fetch(chunk))
+        if ready is None:
+            build_halo(lax.rem(chunk + 1, chunks))
+        else:
+            ready(chunk)
+            build_halo(chunk)
+
+            @pl.loop(0, tiles)
+            def _(tile):
+                build_tile(chunk, tile)
+
+        @pl.loop(0, tiles)
+        def _(tile):
+            cols = chunk_cols(chunk)
+            part = None
+            for dy in range(3):
+                for dx in range(3):
+                    term = nn(shifted(act, dx, tile, dy, width, cols), wbuf[slot, dy, dx * CK:(dx + 1) * CK, :])
+                    part = term if part is None else part + term
+            acc[tile_rows(tile), :] += part
+            if ready is None:
+                build_tile(lax.rem(chunk + 1, chunks), tile)
+
+
+def add_rows(dst, acc, src, first):
+    @pl.loop(0, acc.shape[0] // 64)
+    def _(idx):
+        rows = pl.ds(pl.multiple_of(idx * 64, 64), 64)
+        other = src if first is None else src[pl.ds(pl.multiple_of(first + idx * 64, 32), 64), :].astype(F32)
+        dst[rows, :] = (other + acc[rows, :]).astype(BF16)
+
+
+def time_rows(time_ref, weight, out):
+    emb = time_ref[...].astype(F32)
+    act = (emb / (1.0 + jnp.exp(-emb))).astype(BF16)
+    total = None
+    for place, first, count in time_pieces(act.shape[1], weight.shape[1]):
+        term = nn(act[:, first:first + count], weight[place, 0:count])
+        total = term if total is None else total + term
+    out[...] = total
+
+
+def time_pieces(depth, rows):
+    return [(place, first, min(rows, depth - first)) for place, first in enumerate(range(0, depth, rows))]
+
+
+def time_copies(res_time, which, weight, sem):
+    return [pltpu.make_async_copy(res_time.at[which, pl.ds(first, count), :], weight.at[place, pl.ds(0, count), :], sem)
+            for place, first, count in time_pieces(res_time.shape[1], weight.shape[1])]
+
+
+def half_places(core, half_tokens, width):
+    return core * width, (1 - core) * half_tokens, width, (1 - core) * (half_tokens + width)
+
+
+def middle_norm(mid, acc, time_row, halo, sums, core, partner, member, gain, shift, count, coef, send_sem, recv_sem, width):
+    half_tokens, chans = acc.shape
+    add_rows(mid, acc, time_row, None)
+    tot, sqr = channel_sums(mid, half_tokens, chans)
+    edge = remote(mid.at[pl.ds(pl.multiple_of((1 - core) * (half_tokens - width), width), width), :], halo, send_sem.at[0], recv_sem.at[0], partner)
+    edge.start()
+    sums[0] = group_sums(two_rows(tot, sqr), member)
+    swap = remote(sums.at[0], sums.at[1], send_sem.at[1], recv_sem.at[1], partner)
+    swap.start()
+    swap.wait()
+    group_affine(sums[0, 0:2] + sums[1, 0:2], gain, shift, member, count, coef, 0.5)
+    edge.wait()
+
+
+def res_block_in(latent, time_emb, res_conv, res_time, norms, which, width, groups):
+    peers, band, chans = latent.shape
+    chips = peers // 2
+    half_tokens = chips * band
+    chunks = chans // CK
+    count = float(peers * band * (chans // groups))
+
+    def kernel(lat, time_ref, kern, wtime, norm_ref, out_ref, own, image, mid, halo, act, wbuf, acc, tproj, result, mine, stats, sums, swaps, coef,
+               wsem, tsem, own_sem, send_sem, side_send, recv_sem, stat_send, stat_recv, swap_send, swap_recv, done_send, done_recv):
         me = lax.axis_index('sp')
-        barrier = pltpu.get_barrier_semaphore()
-        for step in range(1, num):
-            pl.semaphore_signal(barrier, inc=1, device_id={'sp': lax.rem(me + step, num)}, device_id_type=MESH)
-        pl.semaphore_wait(barrier, num - 1)
-        copies = []
-        order = sorted(range(1, num), key=lambda step: -min(step, num - step))
-        for step in order:
-            peer = lax.rem(me + step, num)
-            copy = pltpu.make_async_remote_copy(src.at[peer], dst.at[me], send_sem.at[step], recv_sem.at[step], device_id={'sp': peer}, device_id_type=MESH)
-            copy.start()
-            copies.append(copy)
-        own_in = pltpu.make_async_copy(src.at[me], stage, own_sem)
-        own_in.start()
-        own_in.wait()
-        own_out = pltpu.make_async_copy(stage, dst.at[me], own_sem)
-        own_out.start()
-        own_out.wait()
-        for copy in copies:
-            copy.wait()
-
+        chip, core = lax.div(me, 2), lax.rem(me, 2)
+        partner = me + 1 - 2 * core
+        load = pltpu.make_async_copy(lat, own, own_sem)
+        load.start()
+        start_all(fetch_rows(kern, which, 0, 0, wbuf, wsem))
+        start_all(time_copies(wtime, which, wbuf.at[1], tsem))
+        meet(peers, me)
+        clear_edges(act, width)
+        member = members(chans, groups)
+        side = lax.div(me, chips)
+        place = lax.rem(me, chips) * band
+        await_peers(peers)
+
+        def send_to(src, dst, sent, index, chunk, peer):
+            @pl.when(peer == me)
+            def _():
+                pltpu.make_async_copy(src, dst, recv_sem.at[index, chunk]).start()
+
+            @pl.when(peer != me)
+            def _():
+                remote(src, dst, sent.at[index, chunk], recv_sem.at[index, chunk], peer).start()
+
+        def send_chunk(index, chunk):
+            cols = pl.ds(chunk * CK, CK)
+
+            @pl.loop(0, chips)
+            def _(step):
+                target = lax.rem(chip + step + chips // 2, chips)
+                source = lat.at[index * chips + target]
+                send_to(source.at[:, cols], image.at[index, pl.ds(pl.multiple_of(side * width + place, 32), band), cols], send_sem, index, chunk, 2 * target + side)
+
+                @pl.when(me == chips - 1)
+                def _():
+                    send_to(source.at[pl.ds(band - width, width), cols], image.at[index, pl.ds(0, width), cols], side_send, index, chunk, 2 * target + 1)
+
+                @pl.when(me == chips)
+                def _():
+                    send_to(source.at[pl.ds(0, width), cols], image.at[index, pl.ds(half_tokens, width), cols], side_send, index, chunk, 2 * target)
+
+        def drain_sends(index, chunk):
+            cols = chunk_cols(chunk)
+            extra = (me == chips - 1) | (me == chips)
+            inside = side == core
+
+            @pl.when(inside)
+            def _():
+                drain(image.at[index, pl.ds(0, half_tokens - band), cols], send_sem.at[index, chunk])
+
+            @pl.when(jnp.logical_not(inside))
+            def _():
+                drain(image.at[index, pl.ds(0, half_tokens), cols], send_sem.at[index, chunk])
+
+            @pl.when(extra)
+            def _():
+                drain(image.at[index, pl.ds(0, (chips - 1) * width), cols], side_send.at[index, chunk])
+
+        send_chunk(0, 0)
+        load.wait()
+
+        @pl.loop(0, chips)
+        def _(target):
+            rows = []
+            for index in range(2):
+                vals = own[index * chips + target].astype(F32)
+                rows += [jnp.sum(vals, axis=0, keepdims=True), jnp.sum(vals * vals, axis=0, keepdims=True)]
+            mine[target] = group_sums(jnp.concatenate(rows + [jnp.zeros((4, chans), F32)], axis=0), member)
+
+        @pl.loop(1, peers)
+        def _(step):
+            peer = lax.rem(me + step, peers)
+            remote(mine.at[lax.div(peer, 2)], stats.at[me], stat_send, stat_recv, peer).start()
+
+        for index in range(2):
+            for chunk in range(chunks):
+                if (index, chunk) != (0, 0):
+                    send_chunk(index, chunk)
+        wait_all(time_copies(wtime, which, wbuf.at[1], tsem))
+        time_rows(time_ref, wbuf.at[1], tproj)
+        stats[me] = mine[chip]
+        drain(stats.at[pl.ds(0, peers - 1)], stat_recv)
+        drain(stats.at[pl.ds(0, peers - 1)], stat_send)
+        both = jnp.sum(stats[...], axis=0)
+        sums[0] = both
+        sums[1] = pltpu.roll(both, 6, 0)
+        half_at, halo_at, put, halo_put = half_places(core, half_tokens, width)
+        norm = [norm_ref[4 * which + row:4 * which + row + 1] for row in range(4)]
+
+        @pl.loop(0, 2)
+        def _(index):
+            group_affine(sums[index, 0:2], norm[0], norm[1], member, count, coef, 0.5)
+            conv_rows(lambda chunk: fetch_rows(kern, which, 0, chunk, wbuf, wsem),
+                      [(image.at[index], half_at, put, half_tokens), (image.at[index], halo_at, halo_put, width)],
+                      act, wbuf, coef, acc, width, lambda chunk: drain(image.at[index, :, chunk_cols(chunk)], recv_sem.at[index, chunk]))
+            start_all(fetch_rows(kern, which, 1, 0, wbuf, wsem))
+            middle_norm(mid, acc, tproj[pl.ds(index * chips + chip, 1), :], halo.at[index], swaps.at[index], core, partner, member, norm[2], norm[3], count, coef, swap_send.at[index], swap_recv.at[index], width)
+            conv_rows(lambda chunk: fetch_rows(kern, which, 1, chunk, wbuf, wsem),
+                      [(mid, 0, put, half_tokens), (halo.at[index], 0, halo_put, width)], act, wbuf, coef, acc, width, None)
+
+            @pl.when(index == 0)
+            def _():
+                start_all(fetch_rows(kern, which, 0, 0, wbuf, wsem))
+
+            add_rows(result.at[index], acc, image.at[index], half_at)
+            mine_rows = pl.ds(pl.multiple_of(core * half_tokens, half_tokens), half_tokens)
+
+            @pl.when(index == core)
+            def _():
+                out_ref[mine_rows, :] = result[index]
+
+            @pl.when(index != core)
+            def _():
+                remote(result.at[index], out_ref.at[mine_rows, :], done_send, done_recv, partner).start()
+
+        drain(result.at[0], done_recv)
+        drain(result.at[0], done_send)
+        for index in range(2):
+            @pl.loop(0, chunks)
+            def _(chunk):
+                drain_sends(index, chunk)
+
+    vmem = pl.BlockSpec(memory_space=pltpu.VMEM)
+    hbm = pl.BlockSpec(memory_space=pl.ANY)
+    dma = pltpu.SemaphoreType.DMA
     return pl.pallas_call(
         kernel,
-        out_shape=jax.ShapeDtypeStruct(blocks.shape, blocks.dtype),
-        in_specs=[pl.BlockSpec(memory_space=pl.ANY)],
-        out_specs=pl.BlockSpec(memory_space=pl.ANY),
-        scratch_shapes=[pltpu.VMEM(blocks.shape[1:], blocks.dtype), pltpu.SemaphoreType.DMA((num,)), pltpu.SemaphoreType.DMA((num,)), pltpu.SemaphoreType.DMA],
-        compiler_params=pltpu.CompilerParams(collective_id=collective, has_side_effects=True),
-        name='exchange',
-    )(blocks)
-
-
-def res_block(hidden, res_conv, norms, time_proj, which, width, groups):
+        out_shape=jax.ShapeDtypeStruct((2 * half_tokens, chans), BF16),
+        in_specs=[hbm, vmem, hbm, hbm, vmem],
+        out_specs=vmem,
+        scratch_shapes=[
+            pltpu.VMEM(latent.shape, BF16),
+            pltpu.VMEM((2, half_tokens + width, chans), BF16),
+            pltpu.VMEM((half_tokens, chans), BF16),
+            pltpu.VMEM((2, width, chans), BF16),
+            pltpu.VMEM((3, half_tokens + 2 * width, chans), BF16),
+            pltpu.VMEM((2, 3, 3 * CK, chans), BF16),
+            pltpu.VMEM((half_tokens, chans), F32),
+            pltpu.VMEM((peers, chans), F32),
+            pltpu.VMEM((2, half_tokens, chans), BF16),
+            pltpu.VMEM((chips, 8, 128), F32),
+            pltpu.VMEM((peers, 8, 128), F32),
+            pltpu.VMEM((2, 8, 128), F32),
+            pltpu.VMEM((2, 2, 8, 128), F32),
+            pltpu.VMEM((8, chans), F32),
+            dma((2,)), dma, dma, dma((2, chunks)), dma((2, chunks)), dma((2, chunks)), dma, dma, dma((2, 2)), dma((2, 2)), dma, dma,
+        ],
+        compiler_params=pltpu.CompilerParams(vmem_limit_bytes=52000000, collective_id=0, has_side_effects=True),
+        cost_estimate=pl.CostEstimate(flops=72 * half_tokens * chans * chans, bytes_accessed=72 * chans * chans, transcendentals=0),
+        name='res_block_in',
+    )(latent, time_emb, res_conv, res_time, norms)
+
+
+def res_block_out(hidden, time_emb, res_conv, res_time, norms, which, width, groups, peers):
     tokens, chans = hidden.shape
+    chips = peers // 2
+    band = tokens // peers
+    half_tokens = tokens // 2
     chunks = chans // CK
-    tiles = tokens // TM
+    tiles = half_tokens // TM
+    per_tile = TM // band
     count = float(tokens * (chans // groups))
 
-    def kernel(x_ref, kern, norm_ref, time_ref, out_ref, acc, mid, act, wbuf, coef, wsem):
-        def fetch(step, slot):
-            conv, chunk = step // chunks, lax.rem(step, chunks)
-            rows = pl.ds(pl.multiple_of(chunk * CK, CK), CK)
-            return [pltpu.make_async_copy(kern.at[which, conv, dy, dx, rows, :], wbuf.at[slot, dy, pl.ds(dx * CK, CK), :], wsem.at[slot])
-                    for dy in range(3) for dx in range(3)]
-
-        for copy in fetch(0, 0):
-            copy.start()
-        edge = jnp.zeros((width, 3 * CK), BF16)
-        for slot in range(2):
-            act[slot, 0:width, :] = edge
-            act[slot, width + tokens:2 * width + tokens, :] = edge
-        column = lax.rem(lax.broadcasted_iota(jnp.int32, (TM, CK), 0), width)
-
-        def build(src, chunk, tile, slot):
-            cols = pl.ds(pl.multiple_of(chunk * CK, CK), CK)
-            rows = pl.multiple_of(tile * TM, TM)
-            vals = src[pl.ds(rows, TM), cols].astype(F32)
-            half = vals * coef[0:1, cols] + coef[1:2, cols]
-            vals = half + half * jnp.tanh(half)
-            put = pl.ds(rows + width, TM)
-            act[slot, put, 0:CK] = jnp.where(column == 0, 0.0, pltpu.roll(vals, 1, 0)).astype(BF16)
-            act[slot, put, CK:2 * CK] = vals.astype(BF16)
-            act[slot, put, 2 * CK:3 * CK] = jnp.where(column == width - 1, 0.0, pltpu.roll(vals, TM - 1, 0)).astype(BF16)
-
-        def conv(src, index):
-            @pl.loop(0, tiles)
-            def _(tile):
-                build(src, 0, tile, 0)
-
-            acc[...] = jnp.zeros_like(acc)
+    def kernel(hid, time_ref, kern, wtime, norm_ref, out_ref, image, mid, halo, act, wbuf, cbuf, acc, tproj, result, sums, swaps, coef,
+       wsem, csem, tsem, give_send, give_recv, swap_send, swap_recv, send_sem, recv_sem):
+        me = lax.axis_index('sp')
+        chip, core = lax.div(me, 2), lax.rem(me, 2)
+        partner = me + 1 - 2 * core
+        span = half_tokens + width
+
+        def window(part):
+            return pl.ds(pl.multiple_of(part * (half_tokens - width), width), span)
+
+        start_all(fetch_rows(kern, which, 0, 0, wbuf, wsem))
+        start_all(time_copies(wtime, which, wbuf.at[1], tsem))
+        meet(peers, me)
+        clear_edges(act, width)
+        member = members(chans, groups)
+        await_peers(peers)
+        give = remote(hid.at[window(1 - core), :], image.at[core], give_send.at[0], give_recv.at[0], partner)
+        give.start()
+        image[core] = hid[window(core), :]
+        tot, sqr = channel_sums(hid, tokens, chans)
+        sums[core] = group_sums(two_rows(tot, sqr), member)
+        wait_all(time_copies(wtime, which, wbuf.at[1], tsem))
+        time_rows(time_ref, wbuf.at[1], tproj)
+        tell = remote(sums.at[core], sums.at[core], give_send.at[1], give_recv.at[1], partner)
+        tell.start()
+        tell.wait()
+        give.wait()
+        half_at, halo_at, put, halo_put = half_places(core, half_tokens, width)
+        norm = [norm_ref[4 * which + row:4 * which + row + 1] for row in range(4)]
+
+        @pl.loop(0, 2)
+        def _(index):
+            group_affine(sums[index, 0:2], norm[0], norm[1], member, count, coef, 0.5)
+            conv_rows(lambda chunk: fetch_rows(kern, which, 0, chunk, wbuf, wsem),
+                      [(image.at[index], half_at, put, half_tokens), (image.at[index], halo_at, halo_put, width)],
+                      act, wbuf, coef, acc, width, None)
+            start_all(fetch_cols(kern, which, 1, 0, cbuf, csem))
+
+            @pl.when(index == 0)
+            def _():
+                start_all(fetch_rows(kern, which, 0, 0, wbuf, wsem))
+
+            middle_norm(mid, acc, tproj[pl.ds(index * chips + chip, 1), :], halo.at[index], swaps.at[index], core, partner, member, norm[2], norm[3], count, coef, swap_send.at[index], swap_recv.at[index], width)
 
             @pl.loop(0, chunks)
             def _(chunk):
-                step = index * chunks + chunk
-                wslot = lax.rem(step, 2)
-                slot = lax.rem(chunk, 2)
-
-                @pl.when(step + 1 < 2 * chunks)
-                def _():
-                    for copy in fetch(step + 1, 1 - wslot):
-                        copy.start()
-
-                for copy in fetch(step, wslot):
-                    copy.wait()
+                activate(halo.at[index], 0, act, halo_put, width, coef, chunk, width)
 
                 @pl.loop(0, tiles)
                 def _(tile):
-                    rows = pl.multiple_of(tile * TM, TM)
-                    part = nn(act[slot, pl.ds(rows, TM), :], wbuf[wslot, 0])
-                    part += nn(act[slot, pl.ds(rows + width, TM), :], wbuf[wslot, 1])
-                    part += nn(act[slot, pl.ds(rows + 2 * width, TM), :], wbuf[wslot, 2])
-                    acc[pl.ds(rows, TM), :] += part
-                    build(src, lax.rem(chunk + 1, chunks), tile, 1 - slot)
-
-        tot, sqr = channel_sums(x_ref, tokens, chans)
-        group_affine(tot, sqr, norm_ref[0:1], norm_ref[1:2], groups, count, coef, 0.5)
-        conv(x_ref, 0)
-
-        @pl.loop(0, tokens // 64)
-        def _(idx):
-            rows = pl.ds(pl.multiple_of(idx * 64, 64), 64)
-            mid[rows, :] = (acc[rows, :] + time_ref[0:1]).astype(BF16)
-
-        tot, sqr = channel_sums(mid, tokens, chans)
-        group_affine(tot, sqr, norm_ref[2:3], norm_ref[3:4], groups, count, coef, 0.5)
-        conv(mid, 1)
-
-        @pl.loop(0, tokens // 64)
-        def _(idx):
-            rows = pl.ds(pl.multiple_of(idx * 64, 64), 64)
-            out_ref[rows, :] = (x_ref[rows, :].astype(F32) + acc[rows, :]).astype(BF16)
-
-    flops = 2 * 2 * 9 * tokens * chans * chans
+                    activate(mid, tile * TM, act, put + tile * TM, TM, coef, chunk, width)
+
+            slab = index * chips + chip
+
+            @pl.loop(0, chunks)
+            def _(chunk):
+                slot = lax.rem(chunk, 2)
+                cols = chunk_cols(chunk)
+
+                @pl.when(chunk + 1 < chunks)
+                def _():
+                    start_all(fetch_cols(kern, which, 1, chunk + 1, cbuf, csem))
+
+                wait_all(fetch_cols(kern, which, 1, chunk, cbuf, csem))
+
+                @pl.loop(0, tiles)
+                def _(step):
+                    tile = lax.rem(step + lax.div(chip, 2), tiles)
+                    part = None
+                    for dy in range(3):
+                        for dx in range(3):
+                            term = nn(shifted(act, dx, tile, dy, width, slice(None)), cbuf[slot, 3 * dy + dx])
+                            part = term if part is None else part + term
+                    rows = tile_rows(tile)
+                    result[index, rows, cols] = (image[index, tile_rows(tile, half_at), cols].astype(F32) + part).astype(BF16)
+                    for idx in range(per_tile):
+                        here = tile * per_tile + idx
+                        peer = core * chips + here
+                        block = result.at[index, pl.ds(pl.multiple_of(here * band, band), band), cols]
+
+                        @pl.when(peer == me)
+                        def _():
+                            out_ref[slab, :, cols] = block[...]
+
+                        @pl.when(peer != me)
+                        def _():
+                            remote(block, out_ref.at[slab, :, cols], send_sem, recv_sem, peer).start()
+
+        inside = lax.div(me, chips) == core
+
+        @pl.when(inside)
+        def _():
+            drain(out_ref.at[pl.ds(0, peers - 2)], send_sem)
+            drain(out_ref.at[pl.ds(0, peers - 2)], recv_sem)
+
+        @pl.when(jnp.logical_not(inside))
+        def _():
+            drain(out_ref, send_sem)
+            drain(out_ref, recv_sem)
+
     vmem = pl.BlockSpec(memory_space=pltpu.VMEM)
+    hbm = pl.BlockSpec(memory_space=pl.ANY)
+    dma = pltpu.SemaphoreType.DMA
     return pl.pallas_call(
         kernel,
-        out_shape=jax.ShapeDtypeStruct(hidden.shape, BF16),
-        in_specs=[vmem, pl.BlockSpec(memory_space=pl.ANY), vmem, vmem],
+        out_shape=jax.ShapeDtypeStruct((peers, band, chans), BF16),
+        in_specs=[vmem, vmem, hbm, hbm, vmem],
         out_specs=vmem,
         scratch_shapes=[
-            pltpu.VMEM((tokens, chans), F32),
-            pltpu.VMEM((tokens, chans), BF16),
-            pltpu.VMEM((2, tokens + 2 * width, 3 * CK), BF16),
+            pltpu.VMEM((2, half_tokens + width, chans), BF16),
+            pltpu.VMEM((half_tokens, chans), BF16),
+            pltpu.VMEM((2, width, chans), BF16),
+            pltpu.VMEM((3, half_tokens + 2 * width, chans), BF16),
             pltpu.VMEM((2, 3, 3 * CK, chans), BF16),
+            pltpu.VMEM((2, 9, chans, CK), BF16),
+            pltpu.VMEM((half_tokens, chans), F32),
+            pltpu.VMEM((peers, chans), F32),
+            pltpu.VMEM((2, half_tokens, chans), BF16),
+            pltpu.VMEM((2, 8, 128), F32),
+            pltpu.VMEM((2, 2, 8, 128), F32),
             pltpu.VMEM((8, chans), F32),
-            pltpu.SemaphoreType.DMA((2,)),
+            dma((2,)), dma((2,)), dma, dma((2,)), dma((2,)), dma((2, 2)), dma((2, 2)), dma, dma,
         ],
-        compiler_params=pltpu.CompilerParams(vmem_limit_bytes=VMEM_LIMIT),
-        cost_estimate=pl.CostEstimate(flops=flops, bytes_accessed=2 * 9 * chans * chans * 2, transcendentals=0),
-        name='res_block',
-    )(hidden, res_conv, norms, time_proj)
-
-
-def transformer(hidden, context, norms, proj_inout, qkv_t, self_out, cross_q_t, cross_kv_t, cross_out, ff_in, ff_out, groups, heads, text):
+        compiler_params=pltpu.CompilerParams(vmem_limit_bytes=49000000, collective_id=1, has_side_effects=True),
+        cost_estimate=pl.CostEstimate(flops=72 * half_tokens * chans * chans, bytes_accessed=72 * chans * chans, transcendentals=0),
+        name='res_block_out',
+    )(hidden, time_emb, res_conv, res_time, norms)
+
+
+def transformer(hidden, context, norms, norm_row, proj_inout, qkv_t, self_out, cross_q_t, cross_kv_t, cross_out, ff_in, ff_out, groups, heads, text):
     tokens, chans = hidden.shape
-    text_rows, text_dim = context.shape
+    text_dim = context.shape[1]
+    images = context.shape[0] // text
+    text_rows = -(-text // 16) * 16
     head_dim = chans // heads
     pairs = heads // 2
     pair = 2 * head_dim
@@ -219,7 +563,7 @@
     half = chans // 2
 
     def kernel(h_ref, ctx_ref, norm_ref, pio, wqkv, wo, cq, ckv, co, f1, f2, out_ref,
-               ring, tok, aux, q_t, keys, v_t, acc, ctx_k, ctx_v, coef, rsem):
+               ring, tok, aux, q_t, keys, v_t, acc, ctx_mine, ctx_k, ctx_v, coef, rsem):
         units = {
             'in': (pio.at[0], 0, 0), 'q': (wqkv.at[0], 0, 1), 'k': (wqkv.at[1], 1, 0), 'v': (wqkv.at[2], 1, 1),
             'ck0': (ckv.at[0, :, 0:ctx_half], 1, 2), 'ck1': (ckv.at[0, :, ctx_half:text_dim], 0, 2),
@@ -251,13 +595,20 @@
                 pltpu.make_async_copy(f2.at[pl.ds(cols, chans), :], ring.at[group, 2], rsem.at[group, 2]),
             ]
 
-        start('in', 'q', 'k', 'v', 'ck0', 'ck1')
-
-        def tile_rows(tile):
-            return pl.ds(pl.multiple_of(tile * TM, TM), TM)
+        me = lax.axis_index('sp')
+        ctx_rows = text * images
+        assert ctx_rows <= chans and ctx_half <= chans
+        ctx_copies = [
+            pltpu.make_async_copy(ctx_ref.at[:, pl.ds(part * ctx_half, ctx_half)], ring.at[1 - part, 2, 0:ctx_rows, 0:ctx_half], rsem.at[1 - part, 2])
+            for part in range(2)
+        ]
+        start_all(ctx_copies)
+        start('in', 'q', 'k', 'v')
 
         tot, sqr = channel_sums(h_ref, tokens, chans)
-        group_affine(tot, sqr, norm_ref[0:1], norm_ref[1:2], groups, count, coef, 1.0)
+        member = members(chans, groups)
+        sums = group_sums(two_rows(tot, sqr), member)
+        group_affine(sums, norm_ref[norm_row:norm_row + 1], norm_ref[norm_row + 1:norm_row + 2], member, count, coef, 1.0)
 
         def project_rows(weight, src, base, normed_to):
             def norm_tile(tile):
@@ -272,6 +623,13 @@
 
             norm_tile(tiles - 1)
 
+        place = (text_rows, ctx_rows)
+        wanted = lax.broadcasted_iota(jnp.int32, place, 0) * images + (lax.rem(me, 2) * (images // 2) + lax.div(me, 2))
+        pick = jnp.where(lax.broadcasted_iota(jnp.int32, place, 1) == wanted, 1.0, 0.0).astype(BF16)
+        wait_all(ctx_copies)
+        for part in range(2):
+            ctx_mine[part] = nn(pick, ring[1 - part, 2, 0:ctx_rows, 0:ctx_half]).astype(BF16)
+        start('ck0', 'ck1')
         project_rows(take('in'), lambda rows: (h_ref[rows, :].astype(F32) * coef[0:1] + coef[1:2]).astype(BF16), lambda rows: 0.0, aux)
         start('cv0')
 
@@ -293,14 +651,14 @@
         transposed(take('v'), aux, v_t, 1.0)
         start('cq')
         w_ck = take('ck0'), take('ck1')
-        ctx_k[...] = (nt(ctx_ref[:, 0:ctx_half], w_ck[0][...]) + nt(ctx_ref[:, ctx_half:text_dim], w_ck[1][...])).astype(BF16)
+        ctx_k[...] = (nt(ctx_mine[0], w_ck[0][...]) + nt(ctx_mine[1], w_ck[1][...])).astype(BF16)
         start('co')
         w_cv = take('cv0'), take('cv1')
 
         @pl.loop(0, chans // 256)
         def _(part):
             rows = pl.ds(pl.multiple_of(part * 256, 256), 256)
-            ctx_v[rows, :] = (nt(w_cv[0][rows, :], ctx_ref[:, 0:ctx_half]) + nt(w_cv[1][rows, :], ctx_ref[:, ctx_half:text_dim])).astype(BF16)
+            ctx_v[rows, :] = (nt(w_cv[0][rows, :], ctx_mine[0]) + nt(w_cv[1][rows, :], ctx_mine[1])).astype(BF16)
 
         for copy in ff_copies(0, 0):
             copy.start()
@@ -437,7 +795,7 @@
     return pl.pallas_call(
         kernel,
         out_shape=jax.ShapeDtypeStruct(hidden.shape, BF16),
-        in_specs=[vmem, vmem, vmem] + [hbm] * 8,
+        in_specs=[vmem, hbm, vmem] + [hbm] * 8,
         out_specs=vmem,
         scratch_shapes=[
             pltpu.VMEM((2, 3, chans, chans), BF16),
@@ -447,12 +805,13 @@
             pltpu.VMEM((tokens, chans), BF16),
             pltpu.VMEM((chans, tokens), BF16),
             pltpu.VMEM((tokens, chans), F32),
+            pltpu.VMEM((2, text_rows, ctx_half), BF16),
             pltpu.VMEM((text_rows, chans), BF16),
             pltpu.VMEM((chans, text_rows), BF16),
             pltpu.VMEM((8, chans), F32),
             pltpu.SemaphoreType.DMA((2, 3)),
         ],
-        compiler_params=pltpu.CompilerParams(vmem_limit_bytes=VMEM_LIMIT),
+        compiler_params=pltpu.CompilerParams(vmem_limit_bytes=49000000),
         cost_estimate=pl.CostEstimate(flops=flops, bytes_accessed=80_000_000, transcendentals=tokens * tokens * heads),
         name='transformer',
     )(hidden, context, norms, proj_inout, qkv_t, self_out, cross_q_t, cross_kv_t, cross_out, ff_in, ff_out)
@@ -468,27 +827,16 @@
         heads, head_dim = self_out.shape[:2]
         groups = res_norm.shape[3]
         text, text_dim = context.shape[1:]
-        me = lax.axis_index('sp')
-
-        image = exchange(latent.reshape(images, band, chans), 0).reshape(images * band, chans)
-        time_row = lax.dynamic_slice_in_dim(time_emb, me, 1, 0)
-        time_act = jax.nn.silu(time_row.astype(F32)).astype(BF16)
-        time_proj = jnp.einsum('tc,bcd->btd', time_act, res_time, preferred_element_type=F32)
-        norms = res_norm.astype(F32).reshape(2, 4, chans)
-        ctx_rows = -(-text // 16) * 16
-        ctx = lax.dynamic_index_in_dim(context, me, 0, keepdims=False)
-        ctx = jnp.pad(ctx, ((0, ctx_rows - text), (0, 0)))
-
-        first = res_block(image, res_conv, norms[0], time_proj[0], 0, width, groups)
+        norms = jnp.concatenate([res_norm.reshape(8, chans), attn_norm.reshape(2, chans)], axis=0).astype(F32)
+        first = res_block_in(latent.reshape(images, band, chans), time_emb, res_conv, res_time, norms, 0, width, groups)
         middle = transformer(
-            first, ctx, attn_norm.astype(F32).reshape(2, chans), proj_inout,
+            first, jnp.transpose(context, (1, 0, 2)).reshape(text * images, text_dim), norms, 8, proj_inout,
             jnp.transpose(self_qkv, (0, 2, 3, 1)).reshape(3, chans, chans),
             self_out.reshape(chans, chans),
             jnp.transpose(cross_q, (1, 2, 0)).reshape(chans, chans),
             jnp.transpose(cross_kv, (0, 2, 3, 1)).reshape(2, chans, text_dim),
             cross_out.reshape(chans, chans), ff_in, ff_out, groups, heads, text)
-        last = res_block(middle, res_conv, norms[1], time_proj[1], 1, width, groups)
-        out = exchange(last.reshape(num_bands, band, chans), 1)
+        out = res_block_out(middle, time_emb, res_conv, res_time, norms, 1, width, groups, num_bands)
         return out.reshape(latent.shape)
 
     band_spec = P('dp', 'sp', None, None)

time: 437 us -> 364 us (0.83)
  Pallas kernels: 423 us -> 359 us
  local copies, waits for them, and re-layouts: 9.53 us -> 4.07 us
    pallas_call x4 -> x2, Pallas kernels: 295 us -> 233 us  [the longest x1 121 us: res_block_in(): pl.pallas_call(kernel, out_shape=jax.ShapeDtypeStruct((2 * half_tokens, c...]
where the time goes in v4:
time: 364 us; the launch traced here: 363 us
  Pallas kernels  359 us (99%)
  local copies, waits for them, and re-layouts  4.07 us (1%)
    pallas_call x1, Pallas kernels, transformer(): pl.pallas_call(kernel, out_shape=jax.ShapeDtypeStruct(hidden.shape, BF16)...  126 us
    pallas_call x1, Pallas kernels, res_block_in(): pl.pallas_call(kernel, out_shape=jax.ShapeDtypeStruct((2 * half_tokens, c...  121 us
    pallas_call x1, Pallas kernels, res_block_out(): pl.pallas_call(kernel, out_shape=jax.ShapeDtypeStruct((peers, band, chans...  111 us

profile of v4, /device:TPU:30, one launch (start us, length us, event | category | flops | bytes accessed | tf_op | source)
XLA Modules:
  0.0 362.8 jit_solution(1391309203237519892)
XLA Ops:
  0.0 0.8 reshape.32
  0.8 1.0 reshape.31
  1.8 0.0 copy-start
  1.8 0.8 copy-done
  2.6 121.3 %res_block_in.1.h_ref = bf16[1024,1280]{1,0:T(8,128)(2,1)S(1)} custom-call(bf16[16,64,1280]{2,1,0:T(8,128)(2,1)} %bitcast.25, bf16[16,1280]{1,0:T(8,128)(2,1)S(1)} %copy-done, bf16[2,2,3,3,1280,1280]{5,4,3,2,1,0:T(8,128)(2,1)} %kern.3, bf16[2,1280,1280]{2,1,0:T(8,128)(2,1)} %wtime.3, f32[10,1280]{1,0:T(8,128)S(1)} %maximum_convert_fusion.norm_ref), custom_call_target="tpu_custom_call" | custom-call | flops 60397977600 | bytes 117964800 | tf_op jit(solution)/shard_map/res_block_in/pallas_call | solution.py:381
  123.9 0.0 copy-start.1
  123.9 126.0 %transformer.1.hid = bf16[1024,1280]{1,0:T(8,128)(2,1)S(1)} custom-call(bf16[1024,1280]{1,0:T(8,128)(2,1)S(1)} %res_block_in.1.h_ref, bf16[1232,2048]{1,0:T(8,128)(2,1)} %bitcast.21, f32[10,1280]{1,0:T(8,128)S(1)} %maximum_convert_fusion.norm_ref, bf16[2,1280,1280]{2,1,0:T(8,128)(2,1)} %pio.1, bf16[3,1280,1280]{2,1,0:T(8,128)(2,1)} %bitcast.20, ...), custom_call_target="tpu_custom_call" | custom-call | flops 72477573120 | bytes 80000000 | tf_op jit(solution)/shard_map/transformer/pallas_call | solution.py:795
  249.9 0.0 copy-done.1
  249.9 111.4 %res_block_out.1 = bf16[16,64,1280]{2,1,0:T(8,128)(2,1)S(1)} custom-call(bf16[1024,1280]{1,0:T(8,128)(2,1)S(1)} %transformer.1.hid, bf16[16,1280]{1,0:T(8,128)(2,1)S(1)} %copy-done.1, bf16[2,2,3,3,1280,1280]{5,4,3,2,1,0:T(8,128)(2,1)} %kern.3, bf16[2,1280,1280]{2,1,0:T(8,128)(2,1)} %wtime.3, f32[10,1280]{1,0:T(8,128)S(1)} %maximum_convert_fusion.norm_ref), custom_call_target="tpu_custom_call" | custom-call | flops 60397977600 | bytes 117964800 | tf_op jit(solution)/shard_map/res_block_out/pallas_call | solution.py:522
  361.3 1.5 copy.17
  (1 shorter events, 0.0 us)
Async XLA Ops:
  1.8 0.8 copy-start
  123.9 126.0 %copy-start.1 = (bf16[16,1280]{1,0:T(8,128)(2,1)S(1)}, bf16[16,1280]{1,0:T(8,128)(2,1)}, u32[]{:S(2)}) copy-start(bf16[16,1280]{1,0:T(8,128)(2,1)} %time_ref.3) | copy-start | bytes 122884

commit v5 on v3

v5 whole, which is shorter than its diff:
```python
import functools

import jax
import jax.numpy as jnp
from jax import lax
from jax.experimental import pallas as pl
from jax.experimental.pallas import tpu as pltpu
from jax.sharding import PartitionSpec as P

BF16 = jnp.bfloat16
F32 = jnp.float32
MESH = pl.DeviceIdType.MESH
GN_EPS = 1e-6
LN_EPS = 1e-5
TM = 256
CK = 256
VMEM_LIMIT = 67_000_000


def nn(lhs, rhs):
    return lax.dot_general(lhs, rhs, (((1,), (0,)), ((), ())), preferred_element_type=F32)


def nt(lhs, rhs):
    return lax.dot_general(lhs, rhs, (((1,), (1,)), ((), ())), preferred_element_type=F32)


def split3(vals):
    high = vals.astype(BF16).astype(F32)
    rest = vals - high
    mid = rest.astype(BF16).astype(F32)
    return [high, mid, rest - mid]


def channel_sums(src, rows, chans):
    def step(idx, carry):
        tot, sqr = carry
        vals = src[pl.ds(pl.multiple_of(idx * 64, 64), 64), :].astype(F32).reshape(8, 8, chans)
        return tot + jnp.sum(vals, axis=0), sqr + jnp.sum(vals * vals, axis=0)

    zero = jnp.zeros((8, chans), F32)
    return lax.fori_loop(0, rows // 64, step, (zero, zero))


def layer_norm(tokens):
    centred = tokens - jnp.mean(tokens, axis=-1, keepdims=True)
    return (centred * lax.rsqrt(jnp.mean(centred * centred, axis=-1, keepdims=True) + LN_EPS)).astype(BF16)


def meet(peers, me):
    barrier = pltpu.get_barrier_semaphore()

    @pl.loop(1, peers)
    def _(step):
        pl.semaphore_signal(barrier, inc=1, device_id={'sp': lax.rem(me + step, peers)}, device_id_type=MESH)


def await_peers(peers):
    pl.semaphore_wait(pltpu.get_barrier_semaphore(), peers - 1)


def drain(ref, sem):
    pltpu.make_async_copy(ref, ref, sem).wait()


def remote(src, dst, send_sem, recv_sem, peer):
    return pltpu.make_async_remote_copy(src, dst, send_sem, recv_sem, device_id={'sp': peer}, device_id_type=MESH)


def chunk_cols(chunk):
    return pl.ds(pl.multiple_of(chunk * CK, CK), CK)


def tile_rows(tile, first=0):
    return pl.ds(pl.multiple_of(first + tile * TM, 32), TM)


def members(chans, groups, offset=0):
    width = chans // groups
    chan = lax.broadcasted_iota(jnp.int32, (chans, 128), 0)
    low = (lax.broadcasted_iota(jnp.int32, (chans, 128), 1) - offset) * width
    return jnp.where((chan >= low) & (chan < low + width), 1.0, 0.0).astype(BF16)


def group_sums(rows, member):
    count = rows.shape[0]
    high, mid, low = split3(rows)
    sums = nn(jnp.concatenate([high, mid, low], axis=0).astype(BF16), member)
    return sums[0:count] + sums[count:2 * count] + sums[2 * count:3 * count]


def group_affine(sums, gain, shift, member, count, coef, factor):
    mean = sums[0:1] / count
    rstd = lax.rsqrt(sums[1:2] / count - mean * mean + GN_EPS)
    back = jnp.concatenate(split3(mean) + split3(rstd) + [jnp.zeros((2, 128), F32)], axis=0).astype(BF16)
    wide = nt(back, member)
    scale = (wide[3:4] + wide[4:5] + wide[5:6]) * gain
    coef[0:1, :] = factor * scale
    coef[1:2, :] = factor * (shift - (wide[0:1] + wide[1:2] + wide[2:3]) * scale)


def two_rows(tot, sqr):
    rows = [jnp.sum(tot, axis=0, keepdims=True), jnp.sum(sqr, axis=0, keepdims=True)]
    return jnp.concatenate(rows + [jnp.zeros((6, tot.shape[1]), F32)], axis=0)


def activate(src, act, coef, first, wide, tile, width):
    cols = pl.ds(first, wide)
    half = src[tile_rows(tile), cols].astype(F32) * coef[0:1, cols] + coef[1:2, cols]
    vals = half + half * jnp.tanh(half)
    column = lax.rem(lax.broadcasted_iota(jnp.int32, (TM, wide), 0), width)
    put = tile_rows(tile, width)
    act[0, put, cols] = jnp.where(column == 0, 0.0, pltpu.roll(vals, 1, 0)).astype(BF16)
    act[1, put, cols] = vals.astype(BF16)
    act[2, put, cols] = jnp.where(column == width - 1, 0.0, pltpu.roll(vals, TM - 1, 0)).astype(BF16)


def clear_edges(act, width):
    edge = jnp.zeros((width, act.shape[2]), BF16)
    for shift in range(3):
        act[shift, 0:width, :] = edge
        act[shift, act.shape[1] - width:act.shape[1], :] = edge


def shifted(act, shift, tile, row, width, cols):
    return act[shift, tile_rows(tile, row * width), cols]


def taps():
    return [(dy, dx) for dy in range(3) for dx in range(3)]


def fetch_rows(kern, which, conv, chunk, wbuf, sem):
    slot = lax.rem(chunk, 2)
    return [pltpu.make_async_copy(kern.at[which, conv, dy, dx, chunk_cols(chunk), :], wbuf.at[slot, pl.ds(tap * CK, CK), :], sem.at[slot])
            for tap, (dy, dx) in enumerate(taps())]


def fetch_halves(kern, which, conv, chunk, wbuf, sem):
    slot, half, count = lax.rem(chunk, 2), CK // 2, len(taps())
    return [pltpu.make_async_copy(kern.at[which, conv, dy, dx, pl.ds(chunk * CK + part * half, half), :], wbuf.at[slot, pl.ds((part * count + tap) * half, half), :], sem.at[slot])
            for part in range(2) for tap, (dy, dx) in enumerate(taps())]


def fetch_cols(kern, which, conv, chunk, wbuf, sem):
    slot = lax.rem(chunk, 2)
    return [pltpu.make_async_copy(kern.at[which, conv, dy, dx, :, chunk_cols(chunk)], wbuf.at[slot, tap], sem.at[slot])
            for tap, (dy, dx) in enumerate(taps())]


def start_all(copies):
    for copy in copies:
        copy.start()


def wait_all(copies):
    for copy in copies:
        copy.wait()


def chunk_product(act, wbuf, slot, chunk, tile, width):
    cols = chunk_cols(chunk)
    return sum(nn(shifted(act, dx, tile, dy, width, cols), wbuf[slot, tap * CK:(tap + 1) * CK, :]) for tap, (dy, dx) in enumerate(taps()))


def half_product(act, wbuf, slot, first, part, tile, width):
    depth = len(taps()) * (CK // 2)
    rows = jnp.concatenate([shifted(act, dx, tile, dy, width, pl.ds(first, CK // 2)) for dy, dx in taps()], axis=1)
    return nn(rows, wbuf[slot, pl.ds(pl.multiple_of(part * depth, depth), depth), :])


def conv_rows(fetch, src, act, wbuf, coef, acc, width):
    tokens, chans = acc.shape
    chunks = chans // CK
    acc[...] = jnp.zeros_like(acc)

    def build(chunk, tile):
        activate(src, act, coef, pl.multiple_of(chunk * CK, CK), CK, tile, width)

    @pl.loop(0, tokens // TM)
    def _(tile):
        build(0, tile)

    @pl.loop(0, chunks)
    def _(chunk):
        @pl.when(chunk + 1 < chunks)
        def _():
            start_all(fetch(chunk + 1))

        wait_all(fetch(chunk))

        @pl.loop(0, tokens // TM)
        def _(tile):
            acc[tile_rows(tile), :] += chunk_product(act, wbuf, lax.rem(chunk, 2), chunk, tile, width)
            build(lax.rem(chunk + 1, chunks), tile)


def add_rows(dst, acc, other):
    @pl.loop(0, acc.shape[0] // 64)
    def _(idx):
        rows = pl.ds(pl.multiple_of(idx * 64, 64), 64)
        dst[rows, :] = ((other if other.shape[0] == 1 else other[rows, :].astype(F32)) + acc[rows, :]).astype(BF16)


def time_copy(res_time, which, wbuf, sem):
    depth = res_time.shape[1]
    return pltpu.make_async_copy(res_time.at[which], wbuf.at[1, pl.ds(0, depth), :], sem)


def time_row(time_ref, wbuf, tproj, image):
    emb = time_ref[...].astype(F32)
    act = (emb / (1.0 + jnp.exp(-emb))).astype(BF16)
    tproj[...] = nn(act, wbuf[1, 0:act.shape[1], :])
    return tproj[pl.ds(image, 1), :]


def norm_from(src, member, norm_ref, row, count, coef):
    tot, sqr = channel_sums(src, src.shape[0], src.shape[1])
    group_affine(group_sums(two_rows(tot, sqr), member), norm_ref[row:row + 1], norm_ref[row + 1:row + 2], member, count, coef, 0.5)


def res_block_in(latent, time_emb, res_conv, res_time, norms, which, width, groups):
    peers, band, chans = latent.shape
    tokens = peers * band
    last = chans // CK - 1
    half = CK // 2
    pieces = [(chunk * CK, CK) for chunk in range(last)] + [(last * CK, half), (last * CK + half, half)]
    count = float(tokens * (chans // groups))
    tiles = tokens // TM

    def kernel(lat, time_ref, kern, wtime, norm_ref, out_ref, own, image, mid, act, wbuf, acc, tproj, rows, mine, stats, coef,
               wsem, tsem, own_sem, send_sem, recv_sem, stat_send, stat_recv):
        me = lax.axis_index('sp')
        load = pltpu.make_async_copy(lat, own, own_sem)
        load.start()
        start_all(fetch_rows(kern, which, 0, 0, wbuf, wsem))
        weight = time_copy(wtime, which, wbuf, tsem)
        weight.start()
        meet(peers, me)
        clear_edges(act, width)
        member = members(chans, groups)
        own_rows = pl.ds(pl.multiple_of(me * band, band), band)
        await_peers(peers)

        def send(index):
            first, wide = pieces[index]

            @pl.loop(1, peers)
            def _(step):
                peer = lax.rem(me + step, peers)
                remote(lat.at[peer, :, pl.ds(first, wide)], image.at[own_rows, pl.ds(first, wide)], send_sem.at[index], recv_sem.at[index], peer).start()

        send(0)
        load.wait()

        @pl.loop(0, peers)
        def _(peer):
            vals = own[peer].astype(F32).reshape(band // 8, 8, chans)
            rows[pl.ds(peer, 1), :] = jnp.sum(jnp.sum(vals, axis=0), axis=0, keepdims=True)
            rows[pl.ds(peers + peer, 1), :] = jnp.sum(jnp.sum(vals * vals, axis=0), axis=0, keepdims=True)

        sums = group_sums(rows[...], member)
        for peer in range(peers):
            mine[peer, 0:1, :] = sums[peer:peer + 1]
            mine[peer, 1:2, :] = sums[peers + peer:peers + peer + 1]

        @pl.loop(1, peers)
        def _(step):
            peer = lax.rem(me + step, peers)
            remote(mine.at[peer], stats.at[me], stat_send, stat_recv, peer).start()

        for index in range(1, len(pieces)):
            send(index)
        image[own_rows, :] = own[me]
        stats[me] = mine[me]
        weight.wait()
        bias = time_row(time_ref, wbuf, tproj, me)
        acc[...] = jnp.zeros_like(acc)
        drain(stats.at[pl.ds(0, peers - 1)], stat_recv)
        drain(stats.at[pl.ds(0, peers - 1)], stat_send)
        row = 4 * which
        group_affine(jnp.sum(stats[...], axis=0), norm_ref[row:row + 1], norm_ref[row + 1:row + 2], member, count, coef, 0.5)

        def landed(index):
            first, wide = pieces[index]
            return image.at[pl.ds(0, tokens - band), pl.ds(first, wide)]

        @pl.loop(0, last)
        def _(chunk):
            @pl.when(chunk + 1 < last)
            def _():
                start_all(fetch_rows(kern, which, 0, chunk + 1, wbuf, wsem))

            @pl.when(chunk + 1 == last)
            def _():
                start_all(fetch_halves(kern, which, 0, last, wbuf, wsem))

            wait_all(fetch_rows(kern, which, 0, chunk, wbuf, wsem))
            drain(image.at[pl.ds(0, tokens - band), chunk_cols(chunk)], recv_sem.at[chunk])

            @pl.loop(0, tiles)
            def _(tile):
                activate(image, act, coef, pl.multiple_of(chunk * CK, CK), CK, tile, width)

            @pl.loop(0, tiles)
            def _(tile):
                acc[tile_rows(tile), :] += chunk_product(act, wbuf, lax.rem(chunk, 2), chunk, tile, width)

        wait_all(fetch_halves(kern, which, 0, last, wbuf, wsem))

        @pl.loop(0, 2)
        def _(part):
            first = pl.multiple_of(last * CK + part * half, half)
            drain(image.at[pl.ds(0, tokens - band), pl.ds(first, half)], recv_sem.at[last + part])

            @pl.loop(0, tiles)
            def _(tile):
                activate(image, act, coef, first, half, tile, width)

            @pl.loop(0, tiles)
            def _(tile):
                acc[tile_rows(tile), :] += half_product(act, wbuf, last % 2, first, part, tile, width)

        start_all(fetch_rows(kern, which, 1, 0, wbuf, wsem))
        add_rows(mid, acc, bias)
        norm_from(mid, member, norm_ref, row + 2, count, coef)
        conv_rows(lambda chunk: fetch_rows(kern, which, 1, chunk, wbuf, wsem), mid, act, wbuf, coef, acc, width)
        add_rows(out_ref, acc, image)
        for index in range(len(pieces)):
            drain(landed(index), send_sem.at[index])

    vmem = pl.BlockSpec(memory_space=pltpu.VMEM)
    hbm = pl.BlockSpec(memory_space=pl.ANY)
    dma = pltpu.SemaphoreType.DMA
    return pl.pallas_call(
        kernel,
        out_shape=jax.ShapeDtypeStruct((tokens, chans), BF16),
        in_specs=[hbm, vmem, hbm, hbm, vmem],
        out_specs=vmem,
        scratch_shapes=[
            pltpu.VMEM(latent.shape, BF16),
            pltpu.VMEM((tokens, chans), BF16),
            pltpu.VMEM((tokens, chans), BF16),
            pltpu.VMEM((3, tokens + 2 * width, chans), BF16),
            pltpu.VMEM((2, len(taps()) * CK, chans), BF16),
            pltpu.VMEM((tokens, chans), F32),
            pltpu.VMEM((peers, chans), F32),
            pltpu.VMEM((2 * peers, chans), F32),
            pltpu.VMEM((peers, 8, 128), F32),
            pltpu.VMEM((peers, 8, 128), F32),
            pltpu.VMEM((8, chans), F32),
            dma((2,)), dma, dma, dma((len(pieces),)), dma((len(pieces),)), dma, dma,
        ],
        compiler_params=pltpu.CompilerParams(vmem_limit_bytes=52000000, collective_id=0, has_side_effects=True),
        cost_estimate=cost_of(36 * tokens * chans * chans, 36 * chans * chans),
        name='res_block_in',
    )(latent, time_emb, res_conv, res_time, norms)


def res_block_out(hidden, time_emb, res_conv, res_time, norms, which, width, groups, peers):
    tokens, chans = hidden.shape
    band = tokens // peers
    chunks = chans // CK
    tiles = tokens // TM
    per_tile = TM // band
    count = float(tokens * (chans // groups))

    def kernel(x_ref, time_ref, kern, wtime, norm_ref, out_ref, mid, act, wbuf, cbuf, acc, tproj, coef, wsem, csem, tsem, send_sem, recv_sem):
        me = lax.axis_index('sp')
        start_all(fetch_rows(kern, which, 0, 0, wbuf, wsem))
        weight = time_copy(wtime, which, wbuf, tsem)
        weight.start()
        meet(peers, me)
        clear_edges(act, width)
        member = members(chans, groups)
        row = 4 * which
        norm_from(x_ref, member, norm_ref, row, count, coef)
        weight.wait()
        bias = time_row(time_ref, wbuf, tproj, me)
        conv_rows(lambda chunk: fetch_rows(kern, which, 0, chunk, wbuf, wsem), x_ref, act, wbuf, coef, acc, width)
        start_all(fetch_cols(kern, which, 1, 0, cbuf, csem))
        add_rows(mid, acc, bias)
        norm_from(mid, member, norm_ref, row + 2, count, coef)

        @pl.loop(0, chunks)
        def _(chunk):
            @pl.loop(0, tiles)
            def _(tile):
                activate(mid, act, coef, pl.multiple_of(chunk * CK, CK), CK, tile, width)

        await_peers(peers)
        turn = lax.div(me, per_tile) + tiles // 2
        result = mid

        @pl.loop(0, chunks)
        def _(chunk):
            slot = lax.rem(chunk, 2)
            cols = chunk_cols(chunk)

            @pl.when(chunk + 1 < chunks)
            def _():
                start_all(fetch_cols(kern, which, 1, chunk + 1, cbuf, csem))

            wait_all(fetch_cols(kern, which, 1, chunk, cbuf, csem))

            @pl.loop(0, tiles)
            def _(step):
                tile = lax.rem(step + turn, tiles)
                part = sum(nn(shifted(act, dx, tile, dy, width, slice(None)), cbuf[slot, tap]) for tap, (dy, dx) in enumerate(taps()))
                rows = tile_rows(tile)
                result[rows, cols] = (x_ref[rows, cols].astype(F32) + part).astype(BF16)
                for idx in range(per_tile):
                    peer = tile * per_tile + idx
                    block = result.at[pl.ds(pl.multiple_of(peer * band, band), band), cols]

                    @pl.when(peer == me)
                    def _():
                        out_ref[me, :, cols] = block[...]

                    @pl.when(peer != me)
                    def _():
                        remote(block, out_ref.at[me, :, cols], send_sem, recv_sem, peer).start()

        others = out_ref.at[pl.ds(0, peers - 1)]
        drain(others, send_sem)
        drain(others, recv_sem)

    vmem = pl.BlockSpec(memory_space=pltpu.VMEM)
    hbm = pl.BlockSpec(memory_space=pl.ANY)
    dma = pltpu.SemaphoreType.DMA
    return pl.pallas_call(
        kernel,
        out_shape=jax.ShapeDtypeStruct((peers, band, chans), BF16),
        in_specs=[vmem, vmem, hbm, hbm, vmem],
        out_specs=vmem,
        scratch_shapes=[
            pltpu.VMEM((tokens, chans), BF16),
            pltpu.VMEM((3, tokens + 2 * width, chans), BF16),
            pltpu.VMEM((2, len(taps()) * CK, chans), BF16),
            pltpu.VMEM((2, len(taps()), chans, CK), BF16),
            pltpu.VMEM((tokens, chans), F32),
            pltpu.VMEM((peers, chans), F32),
            pltpu.VMEM((8, chans), F32),
            dma((2,)), dma((2,)), dma, dma, dma,
        ],
        compiler_params=pltpu.CompilerParams(vmem_limit_bytes=49000000, collective_id=1, has_side_effects=True),
        cost_estimate=cost_of(36 * tokens * chans * chans, 36 * chans * chans),
        name='res_block_out',
    )(hidden, time_emb, res_conv, res_time, norms)


def cost_of(flops, nbytes):
    return pl.CostEstimate(flops=flops, bytes_accessed=nbytes, transcendentals=0)


def transformer(hidden, context, norms, norm_row, proj_inout, qkv_t, self_out, cross_q_t, cross_kv_t, cross_out, ff_in, ff_out, groups, heads, text):
    tokens, chans = hidden.shape
    text_dim = context.shape[1]
    images = context.shape[0] // text
    text_rows = -(-text // 16) * 16
    head_dim = chans // heads
    pairs = heads // 2
    pair = 2 * head_dim
    count = float(tokens * (chans // groups))
    tiles = tokens // TM
    ff_steps = ff_out.shape[0] // chans
    ctx_half = text_dim // 2
    qw = 512 if chans >= 1024 else 256
    kb = 256
    scale = head_dim ** -0.5
    half = chans // 2

    def kernel(h_ref, ctx_ref, norm_ref, pio, wqkv, wo, cq, ckv, co, f1, f2, out_ref,
               ring, tok, aux, q_t, keys, v_t, acc, ctx_mine, ctx_k, ctx_v, coef, rsem):
        units = {
            'in': (pio.at[0], 0, 0), 'q': (wqkv.at[0], 0, 1), 'k': (wqkv.at[1], 1, 0), 'v': (wqkv.at[2], 1, 1),
            'ck0': (ckv.at[0, :, 0:ctx_half], 1, 2), 'ck1': (ckv.at[0, :, ctx_half:text_dim], 0, 2),
            'cv0': (ckv.at[1, :, 0:ctx_half], 0, 0), 'cv1': (ckv.at[1, :, ctx_half:text_dim], 0, 1),
            'o': (wo, 1, 0), 'cq': (cq, 1, 1), 'co': (co, 1, 2), 'out': (pio.at[1], 0, 0),
        }

        def spot(group, place, wide):
            return ring.at[group, place] if wide == chans else ring.at[group, place, :, 0:wide]

        def copy_of(name):
            src, group, place = units[name]
            return pltpu.make_async_copy(src, spot(group, place, src.shape[1]), rsem.at[group, place])

        def start(*names):
            for name in names:
                copy_of(name).start()

        def take(name):
            copy_of(name).wait()
            src, group, place = units[name]
            return spot(group, place, src.shape[1])

        def ff_copies(step, group):
            cols = pl.multiple_of(step * chans, chans)
            return [
                pltpu.make_async_copy(f1.at[:, pl.ds(cols, chans)], ring.at[group, 0], rsem.at[group, 0]),
                pltpu.make_async_copy(f1.at[:, pl.ds(cols + ff_steps * chans, chans)], ring.at[group, 1], rsem.at[group, 1]),
                pltpu.make_async_copy(f2.at[pl.ds(cols, chans), :], ring.at[group, 2], rsem.at[group, 2]),
            ]

        me = lax.axis_index('sp')
        ctx_rows = text * images
        assert ctx_rows <= chans and ctx_half <= chans
        ctx_copies = [
            pltpu.make_async_copy(ctx_ref.at[:, pl.ds(part * ctx_half, ctx_half)], ring.at[1 - part, 2, 0:ctx_rows, 0:ctx_half], rsem.at[1 - part, 2])
            for part in range(2)
        ]
        start_all(ctx_copies)
        start('in', 'q', 'k', 'v')

        tot, sqr = channel_sums(h_ref, tokens, chans)
        member = members(chans, groups)
        sums = group_sums(two_rows(tot, sqr), member)
        group_affine(sums, norm_ref[norm_row:norm_row + 1], norm_ref[norm_row + 1:norm_row + 2], member, count, coef, 1.0)

        def project_rows(weight, src, base, normed_to):
            def norm_tile(tile):
                rows = tile_rows(tile)
                normed_to[rows, :] = layer_norm(tok[rows, :].astype(F32))

            @pl.loop(0, tiles)
            def _(tile):
                norm_tile(jnp.maximum(tile - 1, 0))
                rows = tile_rows(tile)
                tok[rows, :] = (base(rows) + nn(src(rows), weight[...])).astype(BF16)

            norm_tile(tiles - 1)

        place = (text_rows, ctx_rows)
        wanted = lax.broadcasted_iota(jnp.int32, place, 0) * images + me
        pick = jnp.where(lax.broadcasted_iota(jnp.int32, place, 1) == wanted, 1.0, 0.0).astype(BF16)
        wait_all(ctx_copies)
        for part in range(2):
            ctx_mine[part] = nn(pick, ring[1 - part, 2, 0:ctx_rows, 0:ctx_half]).astype(BF16)
        start('ck0', 'ck1')
        project_rows(take('in'), lambda rows: (h_ref[rows, :].astype(F32) * coef[0:1] + coef[1:2]).astype(BF16), lambda rows: 0.0, aux)
        start('cv0')

        def transposed(weight, src, dst, factor):
            @pl.loop(0, 2)
            def _(part):
                rows = pl.ds(pl.multiple_of(part * half, half), half)
                dst[rows, :] = (nt(weight[rows, :], src[...]).astype(BF16) * factor).astype(BF16) if factor != 1.0 else nt(weight[rows, :], src[...]).astype(BF16)

        transposed(take('q'), aux, q_t, scale)
        start('cv1')
        w_key = take('k')

        @pl.loop(0, tokens // 512)
        def _(part):
            rows = pl.ds(pl.multiple_of(part * 512, 512), 512)
            keys[rows, :] = nt(aux[rows, :], w_key[...]).astype(BF16)
        start('o')
        transposed(take('v'), aux, v_t, 1.0)
        start('cq')
        w_ck = take('ck0'), take('ck1')
        ctx_k[...] = (nt(ctx_mine[0], w_ck[0][...]) + nt(ctx_mine[1], w_ck[1][...])).astype(BF16)
        start('co')
        w_cv = take('cv0'), take('cv1')

        @pl.loop(0, chans // 256)
        def _(part):
            rows = pl.ds(pl.multiple_of(part * 256, 256), 256)
            ctx_v[rows, :] = (nt(w_cv[0][rows, :], ctx_mine[0]) + nt(w_cv[1][rows, :], ctx_mine[1])).astype(BF16)

        for copy in ff_copies(0, 0):
            copy.start()

        row_head = lax.broadcasted_iota(jnp.int32, (pair, 1), 0) < head_dim

        def query_of(hp, first, wide, head):
            both = q_t[pl.ds(pl.multiple_of(hp * pair, pair), pair), pl.ds(first, wide)]
            keep = row_head if head == 0 else jnp.logical_not(row_head)
            return jnp.where(keep, both, jnp.zeros_like(both))

        def pair_cols(hp):
            return pl.ds(pl.multiple_of(hp * pair, pair), pair)

        halves = tokens // qw
        blocks = pairs * halves
        scores = [acc.at[:, pl.ds(h * qw, qw)] for h in range(2)]
        probs = [out_ref.at[:, pl.ds(h * qw, qw)] for h in range(2)]
        parts = tokens // kb

        def place(block):
            hp = lax.div(block, halves)
            return hp, pl.multiple_of((block - hp * halves) * qw, qw)

        def fold(vals, func):
            return func(vals.reshape(-1, 8, vals.shape[-1]), axis=0)

        def score_part(block, query, head, part):
            hp, _ = place(block)
            vals = nn(keys[part * kb:(part + 1) * kb, pair_cols(hp)], query)
            scores[head][part * kb:(part + 1) * kb, :] = vals
            return fold(vals, jnp.max)

        def exp_part(head, part, top):
            vals = jnp.exp(scores[head][part * kb:(part + 1) * kb, :] - top)
            probs[head][part * kb:(part + 1) * kb, :] = vals.astype(BF16)
            return fold(vals, jnp.sum)

        def value_of(block, head, denom):
            hp, _ = place(block)
            vals = v_t[pl.ds(pl.multiple_of(hp * pair + head * head_dim, head_dim), head_dim), :]
            return nn(vals, probs[head][...]) * (1.0 / denom)

        def block_query(block, head):
            hp, first = place(block)
            return query_of(hp, first, qw, head)

        def softmax_stage(score_block, score_head, exp_head, top):
            tops, sums = [], []
            query = block_query(score_block, score_head)
            for part in range(parts):
                tops.append(score_part(score_block, query, score_head, part))
                sums.append(exp_part(exp_head, part, top))
            new_top = jnp.max(functools.reduce(jnp.maximum, tops), axis=0, keepdims=True)
            return new_top, jnp.sum(functools.reduce(jnp.add, sums), axis=0, keepdims=True)

        def emit(block, low, high):
            hp, first = place(block)
            aux[pl.ds(first, qw), pair_cols(hp)] = jnp.concatenate([low, high], axis=0).T.astype(BF16)

        top_first = jnp.max(functools.reduce(jnp.maximum, [score_part(0, block_query(0, 0), 0, part) for part in range(parts)]), axis=0, keepdims=True)
        zero_row = jnp.ones((1, qw), F32)
        zero_out = jnp.zeros((head_dim, qw), F32)

        def attend_block(block, carry):
            top0, denom1, low = carry
            before = jnp.maximum(block - 1, 0)
            high = value_of(before, 1, denom1)
            emit(before, low, high)
            top1, denom0 = softmax_stage(block, 1, 0, top0)
            after = jnp.minimum(block + 1, blocks - 1)
            low = value_of(block, 0, denom0)
            top0, denom1 = softmax_stage(after, 0, 1, top1)
            return top0, denom1, low

        def attend_blocks(step, carry):
            for sub in range(4):
                carry = attend_block(step * 4 + sub, carry)
            return carry

        _, denom1, low = lax.fori_loop(0, blocks // 4, attend_blocks, (top_first, zero_row, zero_out))
        emit(blocks - 1, low, value_of(blocks - 1, 1, denom1))

        project_rows(take('o'), lambda rows: aux[rows, :], lambda rows: tok[rows, :].astype(F32), keys)
        transposed(take('cq'), keys, q_t, scale)

        text_valid = lax.broadcasted_iota(jnp.int32, (text_rows, 1), 0) < text

        @pl.loop(0, pairs // 2)
        def _(step):
            for sub in range(2):
                hp = step * 2 + sub
                outs = []
                for head in range(2):
                    vals = nn(ctx_k[:, pair_cols(hp)], query_of(hp, 0, tokens, head))
                    vals = jnp.where(text_valid, vals, -jnp.inf)
                    weights = jnp.exp(vals - jnp.max(vals, axis=0, keepdims=True))
                    denom = jnp.sum(weights, axis=0, keepdims=True)
                    text_vals = ctx_v[pl.ds(pl.multiple_of(hp * pair + head * head_dim, head_dim), head_dim), :]
                    outs.append(nn(text_vals, weights.astype(BF16)) * (1.0 / denom))
                aux[:, pair_cols(hp)] = jnp.concatenate(outs, axis=0).T.astype(BF16)

        project_rows(take('co'), lambda rows: aux[rows, :], lambda rows: tok[rows, :].astype(F32), keys)
        for copy in ff_copies(1, 1):
            copy.start()
        acc[...] = jnp.zeros_like(acc)

        @pl.loop(0, ff_steps)
        def _(step):
            group = lax.rem(step, 2)
            for copy in ff_copies(step, group):
                copy.wait()

            @pl.loop(0, tiles, unroll=2)
            def _(tile):
                rows = tile_rows(tile)
                src = keys[rows, :]
                value = nn(src, ring[group, 0])
                gate = nn(src, ring[group, 1])
                gated = (value * (0.5 * gate * (1.0 + lax.erf(gate * (0.5 ** 0.5))))).astype(BF16)
                acc[rows, :] += nn(gated, ring[group, 2])

            @pl.when(step + 2 < ff_steps)
            def _():
                for copy in ff_copies(step + 2, group):
                    copy.start()

            @pl.when(step == ff_steps - 2)
            def _():
                start('out')

        w_fin = take('out')

        @pl.loop(0, tiles)
        def _(tile):
            rows = tile_rows(tile)
            t = (tok[rows, :].astype(F32) + acc[rows, :]).astype(BF16)
            out_ref[rows, :] = (h_ref[rows, :].astype(F32) + nn(t, w_fin[...])).astype(BF16)

    vmem = pl.BlockSpec(memory_space=pltpu.VMEM)
    hbm = pl.BlockSpec(memory_space=pl.ANY)
    flops = 2 * tokens * chans * chans * (8 + 3 * ff_steps) + 4 * tokens * tokens * chans
    return pl.pallas_call(
        kernel,
        out_shape=jax.ShapeDtypeStruct(hidden.shape, BF16),
        in_specs=[vmem, hbm, vmem] + [hbm] * 8,
        out_specs=vmem,
        scratch_shapes=[
            pltpu.VMEM((2, 3, chans, chans), BF16),
            pltpu.VMEM((tokens, chans), BF16),
            pltpu.VMEM((tokens, chans), BF16),
            pltpu.VMEM((chans, tokens), BF16),
            pltpu.VMEM((tokens, chans), BF16),
            pltpu.VMEM((chans, tokens), BF16),
            pltpu.VMEM((tokens, chans), F32),
            pltpu.VMEM((2, text_rows, ctx_half), BF16),
            pltpu.VMEM((text_rows, chans), BF16),
            pltpu.VMEM((chans, text_rows), BF16),
            pltpu.VMEM((8, chans), F32),
            pltpu.SemaphoreType.DMA((2, 3)),
        ],
        compiler_params=pltpu.CompilerParams(vmem_limit_bytes=49000000),
        cost_estimate=cost_of(flops, 50 * chans * chans),
        name='transformer',
    )(hidden, context, norms, proj_inout, qkv_t, self_out, cross_q_t, cross_kv_t, cross_out, ff_in, ff_out)


def solution(mesh):
    num_bands = mesh.shape['sp']

    def local_stage(latent, time_emb, context, res_conv, res_time, res_norm, attn_norm, proj_inout, self_qkv, self_out, cross_q, cross_kv, cross_out, ff_in, ff_out):
        images, band_rows, width, chans = latent.shape
        assert images == num_bands
        band = band_rows * width
        heads, head_dim = self_out.shape[:2]
        groups = res_norm.shape[3]
        text, text_dim = context.shape[1:]
        norms = jnp.concatenate([res_norm.reshape(8, chans), attn_norm.reshape(2, chans)], axis=0).astype(F32)
        first = res_block_in(latent.reshape(images, band, chans), time_emb, res_conv, res_time, norms, 0, width, groups)
        middle = transformer(
            first, jnp.transpose(context, (1, 0, 2)).reshape(text * images, text_dim), norms, 8, proj_inout,
            jnp.transpose(self_qkv, (0, 2, 3, 1)).reshape(3, chans, chans),
            self_out.reshape(chans, chans),
            jnp.transpose(cross_q, (1, 2, 0)).reshape(chans, chans),
            jnp.transpose(cross_kv, (0, 2, 3, 1)).reshape(2, chans, text_dim),
            cross_out.reshape(chans, chans), ff_in, ff_out, groups, heads, text)
        out = res_block_out(middle, time_emb, res_conv, res_time, norms, 1, width, groups, num_bands)
        return out.reshape(latent.shape)

    band_spec = P('dp', 'sp', None, None)
    shared = P()
    in_specs = (band_spec, P('dp', None), P('dp', None, None)) + (shared,) * 12
    return jax.shard_map(local_stage, mesh=mesh, in_specs=in_specs, out_specs=band_spec, check_vma=False)
```

time: 366 us -> 343 us (0.937)
  Pallas kernels: 352 us -> 337 us
  local copies, waits for them, and re-layouts: 9.52 us -> 4.07 us
  matrix products: 3.86 us -> 0 us
    pallas_call x1, Pallas kernels: 122 us -> 112 us  [res_block_in(): pl.pallas_call(kernel, out_shape=jax.ShapeDtypeStruct((tokens, chans), BF...]
    pallas_call x1, Pallas kernels: 128 us -> 120 us  [transformer(): pl.pallas_call(kernel, out_shape=jax.ShapeDtypeStruct(hidden.shape, BF16)...]
    dot_general x1 -> x0, matrix products: 3.86 us -> none  [local_stage(): jnp.einsum('tc,bcd->btd', time_act, res_time, preferred_element_type=F32)]
where the time goes in v5:
time: 343 us; the launch traced here: 341 us
  Pallas kernels  337 us (98%)
  local copies, waits for them, and re-layouts  4.07 us (1%)
    pallas_call x1, Pallas kernels, transformer(): pl.pallas_call(kernel, out_shape=jax.ShapeDtypeStruct(hidden.shape, BF16)...  120 us
    pallas_call x1, Pallas kernels, res_block_in(): pl.pallas_call(kernel, out_shape=jax.ShapeDtypeStruct((tokens, chans), BF...  112 us
    pallas_call x1, Pallas kernels, res_block_out(): pl.pallas_call(kernel, out_shape=jax.ShapeDtypeStruct((peers, band, chans...  106 us

profile of v5, /device:TPU:30, one launch (start us, length us, event | category | flops | bytes accessed | tf_op | source)
XLA Modules:
  0.0 340.8 jit_solution(6357089629344683857)
XLA Ops:
  0.0 0.8 reshape.32
  0.8 1.0 reshape.31
  1.8 0.0 copy-start
  1.8 0.8 copy-done
  2.6 111.6 %res_block_in.1.h_ref = bf16[1024,1280]{1,0:T(8,128)(2,1)S(1)} custom-call(bf16[16,64,1280]{2,1,0:T(8,128)(2,1)} %bitcast.25, bf16[16,1280]{1,0:T(8,128)(2,1)S(1)} %copy-done, bf16[2,2,3,3,1280,1280]{5,4,3,2,1,0:T(8,128)(2,1)} %kern.3, bf16[2,1280,1280]{2,1,0:T(8,128)(2,1)} %wtime.3, f32[10,1280]{1,0:T(8,128)S(1)} %maximum_convert_fusion.norm_ref), custom_call_target="tpu_custom_call" | custom-call | flops 60397977600 | bytes 58982400 | tf_op jit(solution)/shard_map/res_block_in/pallas_call | solution.py:335
  114.2 0.0 copy-start.1
  114.2 119.6 %transformer.1.x_ref = bf16[1024,1280]{1,0:T(8,128)(2,1)S(1)} custom-call(bf16[1024,1280]{1,0:T(8,128)(2,1)S(1)} %res_block_in.1.h_ref, bf16[1232,2048]{1,0:T(8,128)(2,1)} %bitcast.21, f32[10,1280]{1,0:T(8,128)S(1)} %maximum_convert_fusion.norm_ref, bf16[2,1280,1280]{2,1,0:T(8,128)(2,1)} %pio.1, bf16[3,1280,1280]{2,1,0:T(8,128)(2,1)} %bitcast.20, ...), custom_call_target="tpu_custom_call" | custom-call | flops 72477573120 | bytes 81920000 | tf_op jit(solution)/shard_map/transformer/pallas_call | solution.py:712
  233.8 0.0 copy-done.1
  233.8 105.5 %res_block_out.1 = bf16[16,64,1280]{2,1,0:T(8,128)(2,1)S(1)} custom-call(bf16[1024,1280]{1,0:T(8,128)(2,1)S(1)} %transformer.1.x_ref, bf16[16,1280]{1,0:T(8,128)(2,1)S(1)} %copy-done.1, bf16[2,2,3,3,1280,1280]{5,4,3,2,1,0:T(8,128)(2,1)} %kern.3, bf16[2,1280,1280]{2,1,0:T(8,128)(2,1)} %wtime.3, f32[10,1280]{1,0:T(8,128)S(1)} %maximum_convert_fusion.norm_ref), custom_call_target="tpu_custom_call" | custom-call | flops 60397977600 | bytes 58982400 | tf_op jit(solution)/shard_map/res_block_out/pallas_call | solution.py:431
  339.3 1.5 copy.17
  (1 shorter events, 0.0 us)
Async XLA Ops:
  1.8 0.8 copy-start
  114.2 119.6 %copy-start.1 = (bf16[16,1280]{1,0:T(8,128)(2,1)S(1)}, bf16[16,1280]{1,0:T(8,128)(2,1)}, u32[]{:S(2)}) copy-start(bf16[16,1280]{1,0:T(8,128)(2,1)} %time_ref.3) | copy-start | bytes 122884

commit v6 on v5

--- a/solution.py
+++ b/solution.py
@@ -14,11 +14,12 @@
 LN_EPS = 1e-5
 TM = 256
 CK = 256
+CROSS_PAIRS = 5
 VMEM_LIMIT = 67_000_000
 
 
 def nn(lhs, rhs):
-    return lax.dot_general(lhs, rhs, (((1,), (0,)), ((), ())), preferred_element_type=F32)
+    return jnp.dot(lhs, rhs, preferred_element_type=F32)
 
 
 def nt(lhs, rhs):
@@ -94,9 +95,9 @@
     rstd = lax.rsqrt(sums[1:2] / count - mean * mean + GN_EPS)
     back = jnp.concatenate(split3(mean) + split3(rstd) + [jnp.zeros((2, 128), F32)], axis=0).astype(BF16)
     wide = nt(back, member)
-    scale = (wide[3:4] + wide[4:5] + wide[5:6]) * gain
+    scale = jnp.sum(wide[3:6], axis=0, keepdims=True) * gain
     coef[0:1, :] = factor * scale
-    coef[1:2, :] = factor * (shift - (wide[0:1] + wide[1:2] + wide[2:3]) * scale)
+    coef[1:2, :] = factor * (shift - jnp.sum(wide[:3], axis=0, keepdims=True) * scale)
 
 
 def two_rows(tot, sqr):
@@ -104,15 +105,15 @@
     return jnp.concatenate(rows + [jnp.zeros((6, tot.shape[1]), F32)], axis=0)
 
 
-def activate(src, act, coef, first, wide, tile, width):
+def activate(src, act, coef, first, wide, row, count, width):
     cols = pl.ds(first, wide)
-    half = src[tile_rows(tile), cols].astype(F32) * coef[0:1, cols] + coef[1:2, cols]
+    half = src[pl.ds(pl.multiple_of(row, width), count), cols].astype(F32) * coef[0:1, cols] + coef[1:2, cols]
     vals = half + half * jnp.tanh(half)
-    column = lax.rem(lax.broadcasted_iota(jnp.int32, (TM, wide), 0), width)
-    put = tile_rows(tile, width)
+    column = lax.rem(lax.broadcasted_iota(jnp.int32, (count, wide), 0), width)
+    put = pl.ds(pl.multiple_of(row + width, width), count)
     act[0, put, cols] = jnp.where(column == 0, 0.0, pltpu.roll(vals, 1, 0)).astype(BF16)
     act[1, put, cols] = vals.astype(BF16)
-    act[2, put, cols] = jnp.where(column == width - 1, 0.0, pltpu.roll(vals, TM - 1, 0)).astype(BF16)
+    act[2, put, cols] = jnp.where(column == width - 1, 0.0, pltpu.roll(vals, count - 1, 0)).astype(BF16)
 
 
 def clear_edges(act, width):
@@ -175,7 +176,7 @@
     acc[...] = jnp.zeros_like(acc)
 
     def build(chunk, tile):
-        activate(src, act, coef, pl.multiple_of(chunk * CK, CK), CK, tile, width)
+        activate(src, act, coef, pl.multiple_of(chunk * CK, CK), CK, tile * TM, TM, width)
 
     @pl.loop(0, tokens // TM)
     def _(tile):
@@ -199,12 +200,11 @@
     @pl.loop(0, acc.shape[0] // 64)
     def _(idx):
         rows = pl.ds(pl.multiple_of(idx * 64, 64), 64)
-        dst[rows, :] = ((other if other.shape[0] == 1 else other[rows, :].astype(F32)) + acc[rows, :]).astype(BF16)
+        dst[rows, :] = (other[rows, :].astype(F32) + acc[rows, :]).astype(BF16)
 
 
 def time_copy(res_time, which, wbuf, sem):
-    depth = res_time.shape[1]
-    return pltpu.make_async_copy(res_time.at[which], wbuf.at[1, pl.ds(0, depth), :], sem)
+    return pltpu.make_async_copy(res_time.at[which], wbuf.at[1, pl.ds(0, res_time.shape[1]), :], sem)
 
 
 def time_row(time_ref, wbuf, tproj, image):
@@ -214,13 +214,42 @@
     return tproj[pl.ds(image, 1), :]
 
 
+def widen(param, chans):
+    groups, width = param.shape
+    group = lax.broadcasted_iota(jnp.int32, (groups, chans), 0) * width
+    chan = lax.broadcasted_iota(jnp.int32, (groups, chans), 1)
+    spread = jnp.where((chan >= group) & (chan < group + width), 1.0, 0.0).astype(BF16)
+    wide = lax.dot_general(param, spread, (((0,), (0,)), ((), ())), preferred_element_type=F32)
+    place = lax.broadcasted_iota(jnp.int32, (width, chans), 0)
+    inside = lax.rem(lax.broadcasted_iota(jnp.int32, (width, chans), 1), width)
+    return jnp.sum(jnp.where(place == inside, wide, 0.0), axis=0, keepdims=True)
+
+
 def norm_from(src, member, norm_ref, row, count, coef):
     tot, sqr = channel_sums(src, src.shape[0], src.shape[1])
     group_affine(group_sums(two_rows(tot, sqr), member), norm_ref[row:row + 1], norm_ref[row + 1:row + 2], member, count, coef, 0.5)
 
 
-def res_block_in(latent, time_emb, res_conv, res_time, norms, which, width, groups):
+def add_and_norm(mid, acc, bias, member, norm_ref, row, count, coef):
+    def step(idx, carry):
+        rows = pl.ds(pl.multiple_of(idx * 64, 64), 64)
+        rounded = (acc[rows, :] + bias).astype(BF16)
+        mid[rows, :] = rounded
+        vals = rounded.astype(F32).reshape(8, 8, acc.shape[1])
+        return carry[0] + jnp.sum(vals, axis=0), carry[1] + jnp.sum(vals * vals, axis=0)
+
+    zero = jnp.zeros((8, acc.shape[1]), F32)
+    tot, sqr = lax.fori_loop(0, acc.shape[0] // 64, step, (zero, zero))
+    group_affine(group_sums(two_rows(tot, sqr), member), norm_ref[row:row + 1], norm_ref[row + 1:row + 2], member, count, coef, 0.5)
+
+
+def res_block_in(latent, time_emb, context, res_conv, res_time, res_norm, attn_norm, cross_kv, text, width):
+    which, other = 0, 1
     peers, band, chans = latent.shape
+    groups = res_norm.shape[1]
+    text_dim = context.shape[1]
+    text_rows = -(-text // 16) * 16
+    block_norms = res_norm.shape[0]
     tokens = peers * band
     last = chans // CK - 1
     half = CK // 2
@@ -228,14 +257,20 @@
     count = float(tokens * (chans // groups))
     tiles = tokens // TM
 
-    def kernel(lat, time_ref, kern, wtime, norm_ref, out_ref, own, image, mid, act, wbuf, acc, tproj, rows, mine, stats, coef,
-               wsem, tsem, own_sem, send_sem, recv_sem, stat_send, stat_recv):
+    def kernel(lat, time_hbm, ctx_hbm, kern, wtime, norm_hbm, attn_hbm, ckv, out_ref, norm_ref, bias_ref, ctx_k, ctx_v,
+               image, own, act, wbuf, acc, time_ref, tproj, rows, mine, stats, coef, norm_raw, attn_raw, ctx_raw, ctx_mine, ckv_buf,
+               wsem, tsem, own_sem, small_sem, ctx_sem, send_sem, recv_sem, stat_send, stat_recv):
         me = lax.axis_index('sp')
-        load = pltpu.make_async_copy(lat, own, own_sem)
-        load.start()
-        start_all(fetch_rows(kern, which, 0, 0, wbuf, wsem))
+        mid = own
+        load = [pltpu.make_async_copy(lat.at[peer], own.at[pl.ds(peer * band, band), :], own_sem) for peer in range(peers)]
+        start_all(load)
+        small = [pltpu.make_async_copy(src, dst, small_sem.at[index]) for index, (src, dst) in enumerate(((time_hbm, time_ref), (norm_hbm, norm_raw), (attn_hbm, attn_raw)))]
+        start_all(small)
         weight = time_copy(wtime, which, wbuf, tsem)
         weight.start()
+        start_all(fetch_rows(kern, which, 0, 0, wbuf, wsem))
+        ctx_copies = [pltpu.make_async_copy(ctx_hbm, ctx_raw, ctx_sem.at[0]), pltpu.make_async_copy(ckv, ckv_buf, ctx_sem.at[1])]
+        start_all(ctx_copies)
         meet(peers, me)
         clear_edges(act, width)
         member = members(chans, groups)
@@ -251,11 +286,11 @@
                 remote(lat.at[peer, :, pl.ds(first, wide)], image.at[own_rows, pl.ds(first, wide)], send_sem.at[index], recv_sem.at[index], peer).start()
 
         send(0)
-        load.wait()
+        wait_all(load)
 
         @pl.loop(0, peers)
         def _(peer):
-            vals = own[peer].astype(F32).reshape(band // 8, 8, chans)
+            vals = own[pl.ds(pl.multiple_of(peer * band, band), band), :].astype(F32).reshape(band // 8, 8, chans)
             rows[pl.ds(peer, 1), :] = jnp.sum(jnp.sum(vals, axis=0), axis=0, keepdims=True)
             rows[pl.ds(peers + peer, 1), :] = jnp.sum(jnp.sum(vals * vals, axis=0), axis=0, keepdims=True)
 
@@ -271,11 +306,33 @@
 
         for index in range(1, len(pieces)):
             send(index)
-        image[own_rows, :] = own[me]
+        image[own_rows, :] = own[own_rows, :]
         stats[me] = mine[me]
+        wait_all(small)
+        for index in range(block_norms):
+            norm_ref[index:index + 1, :] = widen(norm_raw[index], chans)
+        for index in range(2):
+            norm_ref[block_norms + index:block_norms + index + 1, :] = widen(attn_raw[index], chans)
         weight.wait()
-        bias = time_row(time_ref, wbuf, tproj, me)
+        rows[0:1, :] = time_row(time_ref, wbuf, tproj, me)
+        weight = time_copy(wtime, other, wbuf, tsem)
+        weight.start()
         acc[...] = jnp.zeros_like(acc)
+        ctx_copies[0].wait()
+        place = (text_rows, text * peers)
+        wanted = lax.broadcasted_iota(jnp.int32, place, 0) * peers + me
+        pick = jnp.where(lax.broadcasted_iota(jnp.int32, place, 1) == wanted, 1.0, 0.0).astype(BF16)
+        ctx_mine[...] = nn(pick, ctx_raw[...]).astype(BF16)
+        ctx_copies[1].wait()
+        ctx_k[...] = nt(ctx_mine[...], ckv_buf[0]).astype(BF16)
+
+        @pl.loop(0, chans // 256)
+        def _(part):
+            part_rows = pl.ds(pl.multiple_of(part * 256, 256), 256)
+            ctx_v[part_rows, :] = nt(ckv_buf[1, part_rows, :], ctx_mine[...]).astype(BF16)
+
+        weight.wait()
+        bias_ref[...] = time_row(time_ref, wbuf, tproj, me)
         drain(stats.at[pl.ds(0, peers - 1)], stat_recv)
         drain(stats.at[pl.ds(0, peers - 1)], stat_send)
         row = 4 * which
@@ -300,7 +357,7 @@
 
             @pl.loop(0, tiles)
             def _(tile):
-                activate(image, act, coef, pl.multiple_of(chunk * CK, CK), CK, tile, width)
+                activate(image, act, coef, pl.multiple_of(chunk * CK, CK), CK, tile * TM, TM, width)
 
             @pl.loop(0, tiles)
             def _(tile):
@@ -315,15 +372,14 @@
 
             @pl.loop(0, tiles)
             def _(tile):
-                activate(image, act, coef, first, half, tile, width)
+                activate(image, act, coef, first, half, tile * TM, TM, width)
 
             @pl.loop(0, tiles)
             def _(tile):
                 acc[tile_rows(tile), :] += half_product(act, wbuf, last % 2, first, part, tile, width)
 
         start_all(fetch_rows(kern, which, 1, 0, wbuf, wsem))
-        add_rows(mid, acc, bias)
-        norm_from(mid, member, norm_ref, row + 2, count, coef)
+        add_and_norm(mid, acc, rows[0:1, :], member, norm_ref, row + 2, count, coef)
         conv_rows(lambda chunk: fetch_rows(kern, which, 1, chunk, wbuf, wsem), mid, act, wbuf, coef, acc, width)
         add_rows(out_ref, acc, image)
         for index in range(len(pieces)):
@@ -334,30 +390,42 @@
     dma = pltpu.SemaphoreType.DMA
     return pl.pallas_call(
         kernel,
-        out_shape=jax.ShapeDtypeStruct((tokens, chans), BF16),
-        in_specs=[hbm, vmem, hbm, hbm, vmem],
-        out_specs=vmem,
+        out_shape=[
+            jax.ShapeDtypeStruct((tokens, chans), BF16),
+            jax.ShapeDtypeStruct((block_norms + 8, chans), F32),
+            jax.ShapeDtypeStruct((1, chans), F32),
+            jax.ShapeDtypeStruct((text_rows, chans), BF16),
+            jax.ShapeDtypeStruct((chans, text_rows), BF16),
+        ],
+        in_specs=[hbm] * 8,
+        out_specs=[vmem] * 5,
         scratch_shapes=[
-            pltpu.VMEM(latent.shape, BF16),
             pltpu.VMEM((tokens, chans), BF16),
             pltpu.VMEM((tokens, chans), BF16),
             pltpu.VMEM((3, tokens + 2 * width, chans), BF16),
             pltpu.VMEM((2, len(taps()) * CK, chans), BF16),
             pltpu.VMEM((tokens, chans), F32),
+            pltpu.VMEM(time_emb.shape, BF16),
             pltpu.VMEM((peers, chans), F32),
             pltpu.VMEM((2 * peers, chans), F32),
             pltpu.VMEM((peers, 8, 128), F32),
             pltpu.VMEM((peers, 8, 128), F32),
             pltpu.VMEM((8, chans), F32),
-            dma((2,)), dma, dma, dma((len(pieces),)), dma((len(pieces),)), dma, dma,
+            pltpu.VMEM(res_norm.shape, BF16),
+            pltpu.VMEM(attn_norm.shape, BF16),
+            pltpu.VMEM(context.shape, BF16),
+            pltpu.VMEM((text_rows, text_dim), BF16),
+            pltpu.VMEM(cross_kv.shape, BF16),
+            dma((2,)), dma, dma, dma((3,)), dma((2,)), dma((len(pieces),)), dma((len(pieces),)), dma, dma,
         ],
-        compiler_params=pltpu.CompilerParams(vmem_limit_bytes=52000000, collective_id=0, has_side_effects=True),
+        compiler_params=pltpu.CompilerParams(vmem_limit_bytes=53000000, collective_id=0, has_side_effects=True),
         cost_estimate=cost_of(36 * tokens * chans * chans, 36 * chans * chans),
         name='res_block_in',
-    )(latent, time_emb, res_conv, res_time, norms)
-
-
-def res_block_out(hidden, time_emb, res_conv, res_time, norms, which, width, groups, peers):
+    )(latent, time_emb, context, res_conv, res_time, res_norm, attn_norm, cross_kv)
+
+
+def res_block_out(hidden, bias, res_conv, norms, width, groups, peers):
+    which = 1
     tokens, chans = hidden.shape
     band = tokens // peers
     chunks = chans // CK
@@ -365,32 +433,38 @@
     per_tile = TM // band
     count = float(tokens * (chans // groups))
 
-    def kernel(x_ref, time_ref, kern, wtime, norm_ref, out_ref, mid, act, wbuf, cbuf, acc, tproj, coef, wsem, csem, tsem, send_sem, recv_sem):
+    def kernel(x_ref, bias_ref, kern, norm_ref, out_ref, mid, result, act, wbuf, cbuf, acc, coef, wsem, csem, send_sem, recv_sem):
         me = lax.axis_index('sp')
         start_all(fetch_rows(kern, which, 0, 0, wbuf, wsem))
-        weight = time_copy(wtime, which, wbuf, tsem)
-        weight.start()
         meet(peers, me)
         clear_edges(act, width)
         member = members(chans, groups)
         row = 4 * which
         norm_from(x_ref, member, norm_ref, row, count, coef)
-        weight.wait()
-        bias = time_row(time_ref, wbuf, tproj, me)
         conv_rows(lambda chunk: fetch_rows(kern, which, 0, chunk, wbuf, wsem), x_ref, act, wbuf, coef, acc, width)
         start_all(fetch_cols(kern, which, 1, 0, cbuf, csem))
-        add_rows(mid, acc, bias)
-        norm_from(mid, member, norm_ref, row + 2, count, coef)
-
-        @pl.loop(0, chunks)
-        def _(chunk):
-            @pl.loop(0, tiles)
-            def _(tile):
-                activate(mid, act, coef, pl.multiple_of(chunk * CK, CK), CK, tile, width)
+        add_and_norm(mid, acc, bias_ref[...], member, norm_ref, row + 2, count, coef)
+
+        def build(row, rows):
+            @pl.loop(0, chunks)
+            def _(chunk):
+                activate(mid, act, coef, pl.multiple_of(chunk * CK, CK), CK, row, rows, width)
+
+        def build_tile(tile):
+            build(tile * TM, TM)
+
+            @pl.when(tile + 1 < tiles)
+            def _():
+                build((tile + 1) * TM, width)
+
+        turn = lax.rem(lax.div(me, per_tile) + tiles // 2, tiles)
+        build_tile(turn)
+
+        @pl.when(turn > 0)
+        def _():
+            build(turn * TM - width, width)
 
         await_peers(peers)
-        turn = lax.div(me, per_tile) + tiles // 2
-        result = mid
 
         @pl.loop(0, chunks)
         def _(chunk):
@@ -421,6 +495,10 @@
                     def _():
                         remote(block, out_ref.at[me, :, cols], send_sem, recv_sem, peer).start()
 
+                @pl.when((chunk == 0) & (step + 1 < tiles))
+                def _():
+                    build_tile(lax.rem(step + 1 + turn, tiles))
+
         others = out_ref.at[pl.ds(0, peers - 1)]
         drain(others, send_sem)
         drain(others, recv_sem)
@@ -431,60 +509,51 @@
     return pl.pallas_call(
         kernel,
         out_shape=jax.ShapeDtypeStruct((peers, band, chans), BF16),
-        in_specs=[vmem, vmem, hbm, hbm, vmem],
+        in_specs=[vmem, vmem, hbm, vmem],
         out_specs=vmem,
         scratch_shapes=[
+            pltpu.VMEM((tokens, chans), BF16),
             pltpu.VMEM((tokens, chans), BF16),
             pltpu.VMEM((3, tokens + 2 * width, chans), BF16),
             pltpu.VMEM((2, len(taps()) * CK, chans), BF16),
             pltpu.VMEM((2, len(taps()), chans, CK), BF16),
             pltpu.VMEM((tokens, chans), F32),
-            pltpu.VMEM((peers, chans), F32),
             pltpu.VMEM((8, chans), F32),
-            dma((2,)), dma((2,)), dma, dma, dma,
+            dma((2,)), dma((2,)), dma, dma,
         ],
-        compiler_params=pltpu.CompilerParams(vmem_limit_bytes=49000000, collective_id=1, has_side_effects=True),
+        compiler_params=pltpu.CompilerParams(vmem_limit_bytes=48000000, collective_id=1, has_side_effects=True),
         cost_estimate=cost_of(36 * tokens * chans * chans, 36 * chans * chans),
         name='res_block_out',
-    )(hidden, time_emb, res_conv, res_time, norms)
+    )(hidden, bias, res_conv, norms)
 
 
 def cost_of(flops, nbytes):
     return pl.CostEstimate(flops=flops, bytes_accessed=nbytes, transcendentals=0)
 
 
-def transformer(hidden, context, norms, norm_row, proj_inout, qkv_t, self_out, cross_q_t, cross_kv_t, cross_out, ff_in, ff_out, groups, heads, text):
+def transformer(hidden, ctx_keys, ctx_vals, norms, norm_row, proj_inout, qkv_t, self_out, cross_q_t, cross_out, ff_in, ff_out, groups, heads, text):
     tokens, chans = hidden.shape
-    text_dim = context.shape[1]
-    images = context.shape[0] // text
-    text_rows = -(-text // 16) * 16
+    text_rows = ctx_keys.shape[0]
     head_dim = chans // heads
     pairs = heads // 2
     pair = 2 * head_dim
     count = float(tokens * (chans // groups))
     tiles = tokens // TM
     ff_steps = ff_out.shape[0] // chans
-    ctx_half = text_dim // 2
     qw = 512 if chans >= 1024 else 256
     kb = 256
     scale = head_dim ** -0.5
     half = chans // 2
 
-    def kernel(h_ref, ctx_ref, norm_ref, pio, wqkv, wo, cq, ckv, co, f1, f2, out_ref,
-               ring, tok, aux, q_t, keys, v_t, acc, ctx_mine, ctx_k, ctx_v, coef, rsem):
+    def kernel(h_ref, ctx_k, ctx_v, norm_ref, pio, wqkv, wo, cq, co, f1, f2, out_ref, ring, tok, aux, both, keys, acc, coef, rsem):
         units = {
             'in': (pio.at[0], 0, 0), 'q': (wqkv.at[0], 0, 1), 'k': (wqkv.at[1], 1, 0), 'v': (wqkv.at[2], 1, 1),
-            'ck0': (ckv.at[0, :, 0:ctx_half], 1, 2), 'ck1': (ckv.at[0, :, ctx_half:text_dim], 0, 2),
-            'cv0': (ckv.at[1, :, 0:ctx_half], 0, 0), 'cv1': (ckv.at[1, :, ctx_half:text_dim], 0, 1),
             'o': (wo, 1, 0), 'cq': (cq, 1, 1), 'co': (co, 1, 2), 'out': (pio.at[1], 0, 0),
         }
 
-        def spot(group, place, wide):
-            return ring.at[group, place] if wide == chans else ring.at[group, place, :, 0:wide]
-
         def copy_of(name):
             src, group, place = units[name]
-            return pltpu.make_async_copy(src, spot(group, place, src.shape[1]), rsem.at[group, place])
+            return pltpu.make_async_copy(src, ring.at[group, place], rsem.at[group, place])
 
         def start(*names):
             for name in names:
@@ -492,8 +561,8 @@
 
         def take(name):
             copy_of(name).wait()
-            src, group, place = units[name]
-            return spot(group, place, src.shape[1])
+            _, group, place = units[name]
+            return ring.at[group, place]
 
         def ff_copies(step, group):
             cols = pl.multiple_of(step * chans, chans)
@@ -503,15 +572,7 @@
                 pltpu.make_async_copy(f2.at[pl.ds(cols, chans), :], ring.at[group, 2], rsem.at[group, 2]),
             ]
 
-        me = lax.axis_index('sp')
-        ctx_rows = text * images
-        assert ctx_rows <= chans and ctx_half <= chans
-        ctx_copies = [
-            pltpu.make_async_copy(ctx_ref.at[:, pl.ds(part * ctx_half, ctx_half)], ring.at[1 - part, 2, 0:ctx_rows, 0:ctx_half], rsem.at[1 - part, 2])
-            for part in range(2)
-        ]
-        start_all(ctx_copies)
-        start('in', 'q', 'k', 'v')
+        start('in', 'q', 'k', 'v', 'co')
 
         tot, sqr = channel_sums(h_ref, tokens, chans)
         member = members(chans, groups)
@@ -531,24 +592,16 @@
 
             norm_tile(tiles - 1)
 
-        place = (text_rows, ctx_rows)
-        wanted = lax.broadcasted_iota(jnp.int32, place, 0) * images + me
-        pick = jnp.where(lax.broadcasted_iota(jnp.int32, place, 1) == wanted, 1.0, 0.0).astype(BF16)
-        wait_all(ctx_copies)
-        for part in range(2):
-            ctx_mine[part] = nn(pick, ring[1 - part, 2, 0:ctx_rows, 0:ctx_half]).astype(BF16)
-        start('ck0', 'ck1')
         project_rows(take('in'), lambda rows: (h_ref[rows, :].astype(F32) * coef[0:1] + coef[1:2]).astype(BF16), lambda rows: 0.0, aux)
-        start('cv0')
+
+        q_t, v_t = both.at[0], both.at[1]
 
         def transposed(weight, src, dst, factor):
             @pl.loop(0, 2)
             def _(part):
                 rows = pl.ds(pl.multiple_of(part * half, half), half)
-                dst[rows, :] = (nt(weight[rows, :], src[...]).astype(BF16) * factor).astype(BF16) if factor != 1.0 else nt(weight[rows, :], src[...]).astype(BF16)
-
-        transposed(take('q'), aux, q_t, scale)
-        start('cv1')
+                dst[rows, :] = (nt(weight[rows, :], src[...]).astype(BF16) * factor).astype(BF16)
+
         w_key = take('k')
 
         @pl.loop(0, tokens // 512)
@@ -556,18 +609,12 @@
             rows = pl.ds(pl.multiple_of(part * 512, 512), 512)
             keys[rows, :] = nt(aux[rows, :], w_key[...]).astype(BF16)
         start('o')
-        transposed(take('v'), aux, v_t, 1.0)
+
+        @pl.loop(0, 2)
+        def _(which):
+            pltpu.make_async_copy(wqkv.at[2 * which], ring.at[which, 1], rsem.at[which, 1]).wait()
+            transposed(ring.at[which, 1], aux, both.at[which], jnp.where(which == 0, scale, 1.0))
         start('cq')
-        w_ck = take('ck0'), take('ck1')
-        ctx_k[...] = (nt(ctx_mine[0], w_ck[0][...]) + nt(ctx_mine[1], w_ck[1][...])).astype(BF16)
-        start('co')
-        w_cv = take('cv0'), take('cv1')
-
-        @pl.loop(0, chans // 256)
-        def _(part):
-            rows = pl.ds(pl.multiple_of(part * 256, 256), 256)
-            ctx_v[rows, :] = (nt(w_cv[0][rows, :], ctx_mine[0]) + nt(w_cv[1][rows, :], ctx_mine[1])).astype(BF16)
-
         for copy in ff_copies(0, 0):
             copy.start()
 
@@ -655,10 +702,12 @@
 
         text_valid = lax.broadcasted_iota(jnp.int32, (text_rows, 1), 0) < text
 
-        @pl.loop(0, pairs // 2)
+        wide_step = max(count for count in (CROSS_PAIRS, 2, 1) if pairs % count == 0)
+
+        @pl.loop(0, pairs // wide_step)
         def _(step):
-            for sub in range(2):
-                hp = step * 2 + sub
+            for sub in range(wide_step):
+                hp = step * wide_step + sub
                 outs = []
                 for head in range(2):
                     vals = nn(ctx_k[:, pair_cols(hp)], query_of(hp, 0, tokens, head))
@@ -712,26 +761,22 @@
     return pl.pallas_call(
         kernel,
         out_shape=jax.ShapeDtypeStruct(hidden.shape, BF16),
-        in_specs=[vmem, hbm, vmem] + [hbm] * 8,
+        in_specs=[vmem] * 4 + [hbm] * 7,
         out_specs=vmem,
         scratch_shapes=[
             pltpu.VMEM((2, 3, chans, chans), BF16),
             pltpu.VMEM((tokens, chans), BF16),
             pltpu.VMEM((tokens, chans), BF16),
-            pltpu.VMEM((chans, tokens), BF16),
+            pltpu.VMEM((2, chans, tokens), BF16),
             pltpu.VMEM((tokens, chans), BF16),
-            pltpu.VMEM((chans, tokens), BF16),
             pltpu.VMEM((tokens, chans), F32),
-            pltpu.VMEM((2, text_rows, ctx_half), BF16),
-            pltpu.VMEM((text_rows, chans), BF16),
-            pltpu.VMEM((chans, text_rows), BF16),
             pltpu.VMEM((8, chans), F32),
             pltpu.SemaphoreType.DMA((2, 3)),
         ],
         compiler_params=pltpu.CompilerParams(vmem_limit_bytes=49000000),
         cost_estimate=cost_of(flops, 50 * chans * chans),
         name='transformer',
-    )(hidden, context, norms, proj_inout, qkv_t, self_out, cross_q_t, cross_kv_t, cross_out, ff_in, ff_out)
+    )(hidden, ctx_keys, ctx_vals, norms, proj_inout, qkv_t, self_out, cross_q_t, cross_out, ff_in, ff_out)
 
 
 def solution(mesh):
@@ -744,16 +789,17 @@
         heads, head_dim = self_out.shape[:2]
         groups = res_norm.shape[3]
         text, text_dim = context.shape[1:]
-        norms = jnp.concatenate([res_norm.reshape(8, chans), attn_norm.reshape(2, chans)], axis=0).astype(F32)
-        first = res_block_in(latent.reshape(images, band, chans), time_emb, res_conv, res_time, norms, 0, width, groups)
+        flat_kv = jnp.transpose(cross_kv, (0, 2, 3, 1)).reshape(2, chans, text_dim)
+        first, norms, bias, ctx_keys, ctx_vals = res_block_in(
+            latent.reshape(images, band, chans), time_emb, jnp.transpose(context, (1, 0, 2)).reshape(text * images, text_dim), res_conv, res_time,
+            res_norm.reshape((-1,) + res_norm.shape[3:]), attn_norm, flat_kv, text, width)
         middle = transformer(
-            first, jnp.transpose(context, (1, 0, 2)).reshape(text * images, text_dim), norms, 8, proj_inout,
+            first, ctx_keys, ctx_vals, norms, res_norm.shape[0] * res_norm.shape[1] * res_norm.shape[2], proj_inout,
             jnp.transpose(self_qkv, (0, 2, 3, 1)).reshape(3, chans, chans),
             self_out.reshape(chans, chans),
             jnp.transpose(cross_q, (1, 2, 0)).reshape(chans, chans),
-            jnp.transpose(cross_kv, (0, 2, 3, 1)).reshape(2, chans, text_dim),
             cross_out.reshape(chans, chans), ff_in, ff_out, groups, heads, text)
-        out = res_block_out(middle, time_emb, res_conv, res_time, norms, 1, width, groups, num_bands)
+        out = res_block_out(middle, bias, res_conv, norms, width, groups, num_bands)
         return out.reshape(latent.shape)
 
     band_spec = P('dp', 'sp', None, None)

time: 343 us -> 334 us (0.974)
  Pallas kernels: 337 us -> 328 us
    pallas_call x1, Pallas kernels: 120 us -> 114 us  [transformer(): pl.pallas_call(kernel, out_shape=jax.ShapeDtypeStruct(hidden.shape, BF16)...]
where the time goes in v6:
time: 334 us; the launch traced here: 332 us
  Pallas kernels  328 us (98%)
  local copies, waits for them, and re-layouts  3.83 us (1%)
    pallas_call x1, Pallas kernels, transformer(): pl.pallas_call(kernel, out_shape=jax.ShapeDtypeStruct(hidden.shape, BF16)...  114 us
    pallas_call x1, Pallas kernels, res_block_in(): pl.pallas_call(kernel, out_shape=[jax.ShapeDtypeStruct((tokens, chans), B...  112 us
    pallas_call x1, Pallas kernels, res_block_out(): pl.pallas_call(kernel, out_shape=jax.ShapeDtypeStruct((peers, band, chans...  102 us

profile of v6, /device:TPU:30, one launch (start us, length us, event | category | flops | bytes accessed | tf_op | source)
XLA Modules:
  0.0 331.6 jit_solution(10282729505696996958)
XLA Ops:
  0.0 0.0 copy-start
  0.0 0.8 copy-done
  0.8 0.0 copy-start.1
  0.8 0.8 copy-done.1
  1.6 0.0 copy-start.2
  1.6 0.7 copy-done.2
  2.3 112.0 %res_block_in.1 = (bf16[1024,1280]{1,0:T(8,128)(2,1)S(1)}, f32[16,1280]{1,0:T(8,128)S(1)}, f32[1,1280]{1,0:T(1,128)S(1)}, bf16[80,1280]{1,0:T(8,128)(2,1)S(1)}, bf16[1280,80]{1,0:T(8,128)(2,1)S(1)}) custom-call(bf16[16,64,1280]{2,1,0:T(8,128)(2,1)} %bitcast.25, bf16[16,1280]{1,0:T(8,128)(2,1)S(1)} %copy-done.1, bf16[1232,2048]{1,0:T(8,128)(2,1)} %bitcast.21, ...), custom_call_target="tpu_custom_call" | custom-call | flops 60397977600 | bytes 58982400 | tf_op jit(solution)/shard_map/res_block_in/pallas_call | solution.py:391
  114.3 113.5 %transformer.1.x_ref = bf16[1024,1280]{1,0:T(8,128)(2,1)S(1)} custom-call(bf16[1024,1280]{1,0:T(8,128)(2,1)S(1)} %get-tuple-element.10.h_ref, bf16[80,1280]{1,0:T(8,128)(2,1)S(1)} %get-tuple-element.11.ctx_k, bf16[1280,80]{1,0:T(8,128)(2,1)S(1)} %get-tuple-element.12.ctx_v, f32[16,1280]{1,0:T(8,128)S(1)} %get-tuple-element.13.norm_ref, ...), custom_call_target="tpu_custom_call" | custom-call | flops 72477573120 | bytes 81920000 | tf_op jit(solution)/shard_map/transformer/pallas_call | solution.py:761
  227.8 102.3 %res_block_out.1 = bf16[16,64,1280]{2,1,0:T(8,128)(2,1)S(1)} custom-call(bf16[1024,1280]{1,0:T(8,128)(2,1)S(1)} %transformer.1.x_ref, f32[1,1280]{1,0:T(1,128)S(1)} %get-tuple-element.14.bias_ref, bf16[2,2,3,3,1280,1280]{5,4,3,2,1,0:T(8,128)(2,1)} %kern.3, f32[16,1280]{1,0:T(8,128)S(1)} %get-tuple-element.13.norm_ref), custom_call_target="tpu_custom_call" | custom-call | flops 60397977600 | bytes 58982400 | tf_op jit(solution)/shard_map/res_block_out/pallas_call | solution.py:509
  330.2 1.5 copy.17
Async XLA Ops:
  0.0 0.8 copy-start
  0.8 0.8 copy-start.1
  1.6 0.7 copy-start.2

commit v7 on v6

v7 whole, which is shorter than its diff:
```python
import functools

import jax
import jax.numpy as jnp
from jax import lax
from jax.experimental import pallas as pl
from jax.experimental.pallas import tpu as pltpu
from jax.sharding import PartitionSpec as P

BF16 = jnp.bfloat16
F32 = jnp.float32
MESH = pl.DeviceIdType.MESH
GN_EPS = 1e-6
LN_EPS = 1e-5
TM = 256
CK = 256
LANES = 128
ROWS = 8
STEP = 64
CROSS_PAIRS = 5
VMEM_LIMIT = 67_000_000


def loop(stop, **options):
    return pl.loop(0, stop, **options)


def one_hot(mask):
    return mask.astype(F32).astype(BF16)


def nn(lhs, rhs):
    return jnp.dot(lhs, rhs, preferred_element_type=F32)


def nt(lhs, rhs):
    return lax.dot_general(lhs, rhs, (((1,), (1,)), ((), ())), preferred_element_type=F32)


def split3(vals):
    high = vals.astype(BF16).astype(F32)
    rest = vals - high
    mid = rest.astype(BF16).astype(F32)
    return [high, mid, rest - mid]


def channel_sums(src, rows, chans):
    def step(idx, carry):
        tot, sqr = carry
        vals = src[pl.ds(pl.multiple_of(idx * STEP, STEP), STEP), :].astype(F32).reshape(ROWS, ROWS, chans)
        return tot + jnp.sum(vals, axis=0), sqr + jnp.sum(vals * vals, axis=0)

    zero = jnp.zeros((ROWS, chans), F32)
    return lax.fori_loop(0, rows // STEP, step, (zero, zero))


def layer_norm(tokens):
    centred = tokens - jnp.mean(tokens, axis=-1, keepdims=True)
    return (centred * lax.rsqrt(jnp.mean(centred * centred, axis=-1, keepdims=True) + LN_EPS)).astype(BF16)


def meet(peers, me):
    barrier = pltpu.get_barrier_semaphore()

    @pl.loop(1, peers)
    def _(step):
        pl.semaphore_signal(barrier, inc=1, device_id={'sp': lax.rem(me + step, peers)}, device_id_type=MESH)


def await_peers(peers):
    pl.semaphore_wait(pltpu.get_barrier_semaphore(), peers - 1)


def drain(ref, sem):
    pltpu.make_async_copy(ref, ref, sem).wait()


def remote(src, dst, send_sem, recv_sem, peer):
    return pltpu.make_async_remote_copy(src, dst, send_sem, recv_sem, device_id={'sp': peer}, device_id_type=MESH)


def chunk_cols(chunk):
    return pl.ds(pl.multiple_of(chunk * CK, CK), CK)


def tile_rows(tile, first=0):
    return pl.ds(pl.multiple_of(first + tile * TM, 32), TM)


def members(chans, groups, offset=0):
    width = chans // groups
    chan = lax.broadcasted_iota(jnp.int32, (chans, LANES), 0)
    low = (lax.broadcasted_iota(jnp.int32, (chans, LANES), 1) - offset) * width
    return one_hot((chan >= low) & (chan < low + width))


def group_sums(rows, member):
    count = rows.shape[0]
    high, mid, low = split3(rows)
    sums = nn(jnp.concatenate([high, mid, low], axis=0).astype(BF16), member)
    return sums[0:count] + sums[count:2 * count] + sums[2 * count:3 * count]


def group_affine(sums, gain, shift, member, count, coef, factor):
    mean = sums[0:1] / count
    rstd = lax.rsqrt(sums[1:2] / count - mean * mean + GN_EPS)
    back = jnp.concatenate(split3(mean) + split3(rstd) + [jnp.zeros((2, LANES), F32)], axis=0).astype(BF16)
    wide = nt(back, member)
    scale = jnp.sum(wide[3:6], axis=0, keepdims=True) * gain
    coef[0:1, :] = factor * scale
    coef[1:2, :] = factor * (shift - jnp.sum(wide[:3], axis=0, keepdims=True) * scale)


def row_sums(tot, sqr):
    return [jnp.sum(tot, axis=0, keepdims=True), jnp.sum(sqr, axis=0, keepdims=True)]


def eight_rows(rows):
    return jnp.concatenate(rows + [jnp.zeros((ROWS - len(rows), rows[0].shape[1]), F32)], axis=0)


class Pair:
    def __init__(self, peers, band, width):
        self.chips, self.band, self.width = peers // 2, band, width
        self.half, self.sub = self.chips // 2, 2 * band
        self.rows = self.half * self.sub
        self.me = lax.axis_index('sp')
        self.chip, self.core = lax.div(self.me, 2), lax.rem(self.me, 2)
        self.base, self.side, _ = self.seat(self.me)
        self.partner = self.device(self.base, 1 - self.side, self.core)
        self.owners = [self.device(self.base, slot, self.core) for slot in range(2)]

    def seat(self, device):
        chip, core = lax.div(device, 2), lax.rem(device, 2)
        side = lax.div(lax.rem(chip + self.chips - 2 * core, 4), 2)
        return lax.rem(chip - 2 * side + self.chips, self.chips), side, core

    def device(self, base, side, core):
        return 2 * lax.rem(base + 2 * side, self.chips) + core

    def first_chip(self, base, slot, side):
        return lax.rem(base + slot + 1 + (side + 1) * self.half, self.chips)

    def block_chip(self, slot, index, side=None):
        return lax.rem(self.first_chip(self.base, slot, self.side if side is None else side) + index, self.chips)

    def block_rows(self, index):
        return pl.ds(pl.multiple_of(self.width + index * self.sub, self.width), self.sub)

    def border(self, slot):
        return lax.rem(self.chips - self.block_chip(slot, 0), self.chips)

    def spot(self, slot, index):
        return self.width + index * self.sub + jnp.where(index >= self.border(slot), self.width, 0)

    def last_spot(self, slot):
        return self.width + self.rows + jnp.where(self.half >= self.border(slot), self.width, 0)

    def act_shape(self, chans):
        return (2, 3, self.rows + 3 * self.width, chans)

    def clear_border(self, act):
        for slot in range(2):
            @pl.when(self.half >= self.border(slot))
            def _():
                row = pl.ds(pl.multiple_of(self.width + self.border(slot) * self.sub, self.width), self.width)
                act[slot, :, row, :] = jnp.zeros((3, self.width, act.shape[3]), BF16)

    def build(self, src, act, coef, slot, first):
        def part(row, put, count):
            activate(src.at[slot], act.at[slot], coef.at[slot], pl.ds(first, CK), row, put, count, self.width)

        part(0, 0, self.width)
        part(self.width + self.rows, self.last_spot(slot), self.width)

        @loop(self.half)
        def _(index):
            part(self.width + index * self.sub, self.spot(slot, index), self.sub)

    def build_all(self, src, act, coef, slot):
        @loop(act.shape[3] // CK)
        def _(chunk):
            self.build(src, act, coef, slot, pl.multiple_of(chunk * CK, CK))

    def shifted(self, act, slot, tile, dy, dx, cols):
        blocks = TM // self.sub
        rows = [self.spot(slot, blocks * tile + index) + (dy - 1) * self.width for index in range(blocks)]
        return jnp.concatenate([act[slot, dx, pl.ds(pl.multiple_of(row, self.width), self.sub), cols] for row in rows], axis=0)

    def tiles(self, body, order=None):
        per = self.rows // TM

        @loop(2 * per if order is None else per)
        def _(step):
            body(lax.div(step, per) if order is None else order, lax.rem(step, per))

    def acc_rows(self, slot, tile):
        return pl.ds(pl.multiple_of(slot * self.rows + tile * TM, TM), TM)

    def swap_norm(self, mid, acc, bias, sums, member, norm_ref, row, count, coef, send_sem, recv_sem):
        copies, rows = [], []
        for slot in range(2):
            def step(idx, carry):
                first = pl.multiple_of(idx * STEP, STEP)
                rounded = (acc[pl.ds(first + slot * self.rows, STEP), :] + bias[slot:slot + 1, :]).astype(BF16)
                mid[slot, pl.ds(first + self.width, STEP), :] = rounded
                vals = rounded.astype(F32).reshape(ROWS, ROWS, acc.shape[1])
                return carry[0] + jnp.sum(vals, axis=0), carry[1] + jnp.sum(vals * vals, axis=0)

            zero = jnp.zeros((ROWS, acc.shape[1]), F32)
            rows += row_sums(*lax.fori_loop(0, self.rows // STEP, step, (zero, zero)))
            for here, there in ((self.width, self.width + self.rows), (self.rows, 0)):
                index = len(copies)
                copies.append(remote(mid.at[slot, pl.ds(here, self.width), :], mid.at[slot, pl.ds(there, self.width), :], send_sem.at[index], recv_sem.at[index], self.partner))
                copies[-1].start()
        sums[0] = group_sums(eight_rows(rows), member)
        copies.append(remote(sums.at[0], sums.at[1], send_sem.at[len(copies)], recv_sem.at[len(copies)], self.partner))
        copies[-1].start()
        wait_all(copies)
        total = sums[0] + sums[1]
        for slot in range(2):
            group_affine(total[2 * slot:2 * slot + 2], norm_ref[row:row + 1], norm_ref[row + 1:row + 2], member, count, coef.at[slot], 0.5)


def activate(src, act, coef, cols, row, put, count, width):
    half = src[pl.ds(pl.multiple_of(row, width), count), cols].astype(F32) * coef[0:1, cols] + coef[1:2, cols]
    vals = half + half * jnp.tanh(half)
    column = lax.rem(lax.broadcasted_iota(jnp.int32, vals.shape, 0), width)
    rows = pl.ds(pl.multiple_of(put, width), count)
    act[0, rows, cols] = jnp.where(column == 0, 0.0, pltpu.roll(vals, 1, 0)).astype(BF16)
    act[1, rows, cols] = vals.astype(BF16)
    act[2, rows, cols] = jnp.where(column == width - 1, 0.0, pltpu.roll(vals, count - 1, 0)).astype(BF16)


def taps():
    return [(dy, dx) for dy in range(3) for dx in range(3)]


def fetch_rows(kern, which, conv, chunk, wbuf, sem):
    slot = lax.rem(chunk, 2)
    return [pltpu.make_async_copy(kern.at[which, conv, dy, dx, chunk_cols(chunk), :], wbuf.at[slot, pl.ds(tap * CK, CK), :], sem.at[slot])
            for tap, (dy, dx) in enumerate(taps())]


def fetch_cols(kern, which, conv, chunk, wbuf, sem):
    slot = lax.rem(chunk, 2)
    return [pltpu.make_async_copy(kern.at[which, conv, dy, dx, :, chunk_cols(chunk)], wbuf.at[slot, tap], sem.at[slot])
            for tap, (dy, dx) in enumerate(taps())]


def start_all(copies):
    for copy in copies:
        copy.start()


def wait_all(copies):
    for copy in copies:
        copy.wait()


def chunk_product(pair, act, wbuf, chunk, slot, tile):
    cols = chunk_cols(chunk)
    return sum(nn(pair.shifted(act, slot, tile, dy, dx, cols), wbuf[lax.rem(chunk, 2), tap * CK:(tap + 1) * CK, :]) for tap, (dy, dx) in enumerate(taps()))


def column_product(pair, act, cbuf, chunk, slot, tile):
    return sum(nn(pair.shifted(act, slot, tile, dy, dx, slice(None)), cbuf[lax.rem(chunk, 2), tap]) for tap, (dy, dx) in enumerate(taps()))


def conv_columns(pair, kern, which, image, mid, act, cbuf, csem, coef, lead, emit):
    chunks = act.shape[3] // CK
    pair.build_all(mid, act, coef, lead)

    @loop(chunks)
    def _(chunk):
        @pl.when(chunk + 1 < chunks)
        def _():
            start_all(fetch_cols(kern, which, 1, chunk + 1, cbuf, csem))

        wait_all(fetch_cols(kern, which, 1, chunk, cbuf, csem))
        cols = chunk_cols(chunk)

        @loop(2)
        def _(turn):
            slot = lax.rem(lead + turn, 2)

            @pl.when((chunk == 0) & (turn == 1))
            def _():
                pair.build_all(mid, act, coef, slot)

            def body(slot, tile):
                rows = pl.ds(pl.multiple_of(pair.width + tile * TM, pair.width), TM)
                emit(slot, tile, rows, cols, (image[slot, rows, cols].astype(F32) + column_product(pair, act, cbuf, chunk, slot, tile)).astype(BF16))

            pair.tiles(body, slot)


def time_copy(res_time, which, wbuf, sem):
    return pltpu.make_async_copy(res_time.at[which], wbuf.at[1, pl.ds(0, res_time.shape[1]), :], sem)


def time_project(time_ref, wbuf, tproj):
    emb = time_ref[...].astype(F32)
    act = (emb / (1.0 + jnp.exp(-emb))).astype(BF16)
    tproj[...] = nn(act, wbuf[1, 0:act.shape[1], :])


def widen(param, chans):
    groups, width = param.shape
    group = lax.broadcasted_iota(jnp.int32, (groups, chans), 0) * width
    chan = lax.broadcasted_iota(jnp.int32, (groups, chans), 1)
    spread = one_hot((chan >= group) & (chan < group + width))
    wide = lax.dot_general(param, spread, (((0,), (0,)), ((), ())), preferred_element_type=F32)
    place = lax.broadcasted_iota(jnp.int32, (width, chans), 0)
    inside = lax.rem(lax.broadcasted_iota(jnp.int32, (width, chans), 1), width)
    return jnp.sum(jnp.where(place == inside, wide, 0.0), axis=0, keepdims=True)


def res_block_in(latent, time_emb, context, res_conv, res_time, res_norm, attn_norm, cross_kv, text, width):
    which, other = 0, 1
    peers, band, chans = latent.shape
    groups = res_norm.shape[1]
    text_dim = context.shape[1]
    text_rows = -(-text // 16) * 16
    block_norms = res_norm.shape[0]
    tokens = peers * band
    chunks = chans // CK
    count = float(tokens * (chans // groups))
    ctx_half = text_dim // 2

    def kernel(lat, time_hbm, ctx_hbm, kern, wtime, norm_hbm, attn_hbm, ckv, out_ref, norm_ref, bias_ref, ctx_k, ctx_v,
               image, mid, act, wbuf, cbuf, acc, time_ref, tproj, rows, bias, mine, stats, sums, coef, norm_raw, attn_raw, ctx_mine,
               wsem, csem, tsem, own_sem, small_sem, ctx_sem, send_sem, side_sem, recv_sem, stat_send, stat_recv, swap_send, swap_recv, give_send, give_recv):
        pair = Pair(peers, band, width)
        me = pair.me

        def own_rows(peer):
            return mid.at[lax.div(peer, pair.chips), pl.ds(pl.multiple_of(lax.rem(peer, pair.chips) * band, band), band), :]

        def load(peer):
            return pltpu.make_async_copy(lat.at[peer], own_rows(peer), own_sem)

        loop(peers)(lambda peer: load(peer).start())
        small = [pltpu.make_async_copy(src, dst, small_sem.at[index]) for index, (src, dst) in enumerate(((time_hbm, time_ref), (norm_hbm, norm_raw), (attn_hbm, attn_raw)))]
        start_all(small)
        weight = time_copy(wtime, which, wbuf, tsem)
        weight.start()
        start_all(fetch_rows(kern, which, 0, 0, wbuf, wsem))
        depth = act.shape[2]
        ctx_parts = [(part, piece, first, min(depth, text * peers - first)) for part in range(2) for piece, first in enumerate(range(0, text * peers, depth))]
        load_ctx = [pltpu.make_async_copy(ctx_hbm.at[pl.ds(first, size), pl.ds(part * ctx_half, ctx_half)], act.at[part, piece, pl.ds(0, size), pl.ds(0, ctx_half)], ctx_sem.at[0])
                    for part, piece, first, size in ctx_parts]
        start_all(load_ctx)
        load_kv = [pltpu.make_async_copy(ckv.at[index, :, pl.ds(part * CK, CK)], cbuf.at[index, part], ctx_sem.at[1]) for index in range(2) for part in range(text_dim // CK)]
        start_all(load_kv)
        meet(peers, me)
        member = members(chans, groups)
        await_peers(peers)

        def send(index):
            cols = chunk_cols(index)

            @loop(peers)
            def _(step):
                owner = lax.rem(me + step, peers)
                base, slot, core = pair.seat(owner)
                place = lax.rem(pair.chip - pair.first_chip(base, slot, 0) + pair.chips, pair.chips)
                side = lax.div(place, pair.half)
                place = place - side * pair.half
                near, far = pair.device(base, side, core), pair.device(base, 1 - side, core)
                src = lat.at[owner, :, cols]
                dst = image.at[slot, pl.ds(pl.multiple_of(width + place * pair.sub + pair.core * band, width), band), cols]

                @pl.when(near == me)
                def _():
                    pltpu.make_async_copy(src, dst, recv_sem.at[index]).start()

                @pl.when(near != me)
                def _():
                    remote(src, dst, send_sem, recv_sem.at[index], near).start()

                @pl.when((pair.core == 1) & (place == pair.half - 1))
                def _():
                    remote(lat.at[owner, pl.ds(band - width, width), cols], image.at[slot, pl.ds(0, width), cols], side_sem, recv_sem.at[index], far).start()

                @pl.when((pair.core == 0) & (place == 0))
                def _():
                    remote(lat.at[owner, pl.ds(0, width), cols], image.at[slot, pl.ds(width + pair.rows, width), cols], side_sem, recv_sem.at[index], far).start()

        send(0)
        loop(peers)(lambda peer: load(peer).wait())

        @loop(peers)
        def _(peer):
            vals = own_rows(peer)[...].astype(F32).reshape(band // ROWS, ROWS, chans)
            for part, total in enumerate((vals, vals * vals)):
                rows[pl.ds(part * peers + peer, 1), :] = jnp.sum(jnp.sum(total, axis=0), axis=0, keepdims=True)

        found = group_sums(rows[...], member)
        for peer in range(peers):
            mine[peer, 0:1, :] = found[peer:peer + 1]
            mine[peer, 1:2, :] = found[peers + peer:peers + peer + 1]

        @pl.loop(1, peers)
        def _(step):
            peer = lax.rem(me + step, peers)
            base, _, core = pair.seat(peer)
            for slot in range(2):
                remote(mine.at[pair.device(base, slot, core)], stats.at[me, slot], stat_send, stat_recv, peer).start()

        pl.loop(1, chunks)(send)
        for slot in range(2):
            stats[me, slot] = mine[pair.owners[slot]]
        wait_all(small)
        for index in range(block_norms):
            norm_ref[index:index + 1, :] = widen(norm_raw[index], chans)
        for index in range(2):
            norm_ref[block_norms + index:block_norms + index + 1, :] = widen(attn_raw[index], chans)

        def time_rows(dst, copy):
            copy.wait()
            time_project(time_ref, wbuf, tproj)
            for slot in range(2):
                dst[slot:slot + 1, :] = tproj[pl.ds(pair.owners[slot], 1), :]

        time_rows(bias, weight)
        weight = time_copy(wtime, other, wbuf, tsem)
        weight.start()
        acc[...] = jnp.zeros_like(acc)
        wait_all(load_ctx)
        for part in range(2):
            total = 0.0
            for this, piece, first, size in ctx_parts:
                if this == part:
                    place = (text_rows, size)
                    wanted = lax.broadcasted_iota(jnp.int32, place, 0) * peers + (me - first)
                    pick = one_hot(lax.broadcasted_iota(jnp.int32, place, 1) == wanted)
                    total += nn(pick, act[part, piece, 0:size, 0:ctx_half])
            ctx_mine[:, part * ctx_half:(part + 1) * ctx_half] = total.astype(BF16)
        wait_all(load_kv)
        ctx_k[...] = sum(nt(ctx_mine[:, part * CK:(part + 1) * CK], cbuf[0, part]) for part in range(text_dim // CK)).astype(BF16)

        @loop(chans // CK)
        def _(block):
            part_rows = pl.ds(pl.multiple_of(block * CK, CK), CK)
            ctx_v[part_rows, :] = sum(nt(cbuf[1, part, part_rows, :], ctx_mine[:, part * CK:(part + 1) * CK]) for part in range(text_dim // CK)).astype(BF16)

        time_rows(bias_ref, weight)
        pair.clear_border(act)
        others = stats.at[pl.ds(0, peers - 1)]
        drain(others, stat_recv)
        drain(others, stat_send)
        row = 4 * which
        for slot in range(2):
            group_affine(jnp.sum(stats[:, slot], axis=0), norm_ref[row:row + 1], norm_ref[row + 1:row + 2], member, count, coef.at[slot], 0.5)

        @loop(chunks)
        def _(chunk):
            @pl.when(chunk + 1 < chunks)
            def _():
                start_all(fetch_rows(kern, which, 0, chunk + 1, wbuf, wsem))

            wait_all(fetch_rows(kern, which, 0, chunk, wbuf, wsem))
            drain(image.at[:, :, chunk_cols(chunk)], recv_sem.at[chunk])

            @loop(2)
            def _(slot):
                pair.build(image, act, coef, slot, pl.multiple_of(chunk * CK, CK))

            def body(slot, tile):
                acc[pair.acc_rows(slot, tile), :] += chunk_product(pair, act, wbuf, chunk, slot, tile)

            pair.tiles(body)

        start_all(fetch_cols(kern, which, 1, 0, cbuf, csem))
        pair.swap_norm(mid, acc, bias, sums, member, norm_ref, row + 2, count, coef, swap_send, swap_recv)
        give = 1 - pair.side

        def emit(slot, tile, place, cols, vals):
            blocks = TM // pair.sub
            spots = [pl.ds(pl.multiple_of(pair.block_chip(slot, blocks * tile + index) * pair.sub, pair.sub), pair.sub) for index in range(blocks)]

            @pl.when(slot == give)
            def _():
                image[slot, place, cols] = vals
                for index, spot in enumerate(spots):
                    remote(image.at[slot, pair.block_rows(blocks * tile + index), cols], out_ref.at[spot, cols], give_send, give_recv, pair.partner).start()

            @pl.when(slot != give)
            def _():
                for index, spot in enumerate(spots):
                    out_ref[spot, cols] = vals[index * pair.sub:(index + 1) * pair.sub]

        conv_columns(pair, kern, which, image, mid, act, cbuf, csem, coef, give, emit)
        for sem in (give_send, give_recv):
            drain(out_ref.at[pl.ds(0, pair.rows)], sem)
        drain(lat.at[pl.ds(0, peers - 2)], send_sem)
        drain(lat.at[0:2], side_sem)

    vmem = pl.BlockSpec(memory_space=pltpu.VMEM)
    hbm = pl.BlockSpec(memory_space=pl.ANY)
    dma = pltpu.SemaphoreType.DMA
    rows = tokens // 2
    return pl.pallas_call(
        kernel,
        out_shape=[
            jax.ShapeDtypeStruct((tokens, chans), BF16),
            jax.ShapeDtypeStruct((block_norms + ROWS, chans), F32),
            jax.ShapeDtypeStruct((2, chans), F32),
            jax.ShapeDtypeStruct((text_rows, chans), BF16),
            jax.ShapeDtypeStruct((chans, text_rows), BF16),
        ],
        in_specs=[hbm] * ROWS,
        out_specs=[vmem] * 5,
        scratch_shapes=shared_scratch(rows, width, chans) + [
            pltpu.VMEM(time_emb.shape, BF16),
            pltpu.VMEM((peers, chans), F32),
            pltpu.VMEM((2 * peers, chans), F32),
            pltpu.VMEM((2, chans), F32),
            pltpu.VMEM((peers, 2, LANES), F32),
            pltpu.VMEM((peers, 2, 2, LANES), F32),
            pltpu.VMEM((2, ROWS, LANES), F32),
            pltpu.VMEM((2, ROWS, chans), F32),
            pltpu.VMEM(res_norm.shape, BF16),
            pltpu.VMEM(attn_norm.shape, BF16),
            pltpu.VMEM((text_rows, text_dim), BF16),
            dma((2,)), dma((2,)), dma, dma, dma((3,)), dma((2,)), dma, dma, dma((chunks,)), dma, dma, dma((5,)), dma((5,)), dma, dma,
        ],
        compiler_params=pltpu.CompilerParams(vmem_limit_bytes=53000000, collective_id=0, has_side_effects=True),
        cost_estimate=cost_of(36 * tokens * chans * chans, 36 * chans * chans),
        name='res_block_in',
    )(latent, time_emb, context, res_conv, res_time, res_norm, attn_norm, cross_kv)


def shared_scratch(rows, width, chans):
    beside = rows + 2 * width
    return [
        pltpu.VMEM((2, beside, chans), BF16),
        pltpu.VMEM((2, beside, chans), BF16),
        pltpu.VMEM((2, 3, beside + width, chans), BF16),
        pltpu.VMEM((2, len(taps()) * CK, chans), BF16),
        pltpu.VMEM((2, len(taps()), chans, CK), BF16),
        pltpu.VMEM((2 * rows, chans), F32),
    ]


def res_block_out(hidden, bias, res_conv, norms, width, groups, peers):
    which = 1
    tokens, chans = hidden.shape
    band = tokens // peers
    chunks = chans // CK
    count = float(tokens * (chans // groups))

    def kernel(hid, bias_ref, kern, norm_ref, out_ref, image, mid, act, wbuf, cbuf, acc, owned, sums, coef,
               wsem, csem, give_send, give_recv, tell_send, tell_recv, swap_send, swap_recv, send_sem, recv_sem):
        pair = Pair(peers, band, width)
        me, side = pair.me, pair.side
        start_all(fetch_rows(kern, which, 0, 0, wbuf, wsem))
        meet(peers, me)
        pair.clear_border(act)
        member = members(chans, groups)

        def pieces(holder):
            def image_rows(index, offset, size):
                return pl.ds(pl.multiple_of(lax.rem(pair.block_chip(side, index, holder) * pair.sub + offset, tokens), width), size)

            return [(image_rows(index, 0, pair.sub), pair.block_rows(index)) for index in range(pair.half)] + [
                (image_rows(0, tokens - width, width), pl.ds(0, width)), (image_rows(pair.half, 0, width), pl.ds(width + pair.rows, width))]

        await_peers(peers)

        @loop(chunks)
        def _(chunk):
            cols = chunk_cols(chunk)
            for src, dst in pieces(1 - side):
                remote(hid.at[src, cols], image.at[side, dst, cols], give_send, give_recv.at[chunk], pair.partner).start()

        owned[side] = group_sums(eight_rows(row_sums(*channel_sums(hid, tokens, chans))), member)
        tell = remote(owned.at[side], owned.at[side], tell_send, tell_recv, pair.partner)
        tell.start()
        for src, dst in pieces(side):
            image[side, dst, :] = hid[src, :]
        acc[...] = jnp.zeros_like(acc)
        tell.wait()
        row = 4 * which
        for slot in range(2):
            group_affine(owned[slot, 0:2], norm_ref[row:row + 1], norm_ref[row + 1:row + 2], member, count, coef.at[slot], 0.5)

        @loop(chunks)
        def _(chunk):
            @pl.when(chunk + 1 < chunks)
            def _():
                start_all(fetch_rows(kern, which, 0, chunk + 1, wbuf, wsem))

            wait_all(fetch_rows(kern, which, 0, chunk, wbuf, wsem))

            @loop(2)
            def _(turn):
                slot = lax.rem(side + turn, 2)

                @pl.when(turn == 1)
                def _():
                    drain(image.at[1 - side, :, chunk_cols(chunk)], give_recv.at[chunk])

                pair.build(image, act, coef, slot, pl.multiple_of(chunk * CK, CK))

                def body(slot, tile):
                    acc[pair.acc_rows(slot, tile), :] += chunk_product(pair, act, wbuf, chunk, slot, tile)

                pair.tiles(body, slot)

        start_all(fetch_cols(kern, which, 1, 0, cbuf, csem))
        pair.swap_norm(mid, acc, bias_ref, sums, member, norm_ref, row + 2, count, coef, swap_send, swap_recv)

        def emit(slot, tile, place, cols, vals):
            image[slot, place, cols] = vals
            slab = pair.device(pair.base, slot, pair.core)
            blocks = TM // pair.sub
            for index in range(blocks):
                block = blocks * tile + index
                for core in range(2):
                    peer = 2 * pair.block_chip(slot, block) + core
                    src = image.at[slot, pl.ds(pl.multiple_of(width + block * pair.sub + core * band, width), band), cols]

                    @pl.when(peer == me)
                    def _():
                        out_ref[slab, :, cols] = src[...]

                    @pl.when(peer != me)
                    def _():
                        remote(src, out_ref.at[slab, :, cols], send_sem, recv_sem, peer).start()

        conv_columns(pair, kern, which, image, mid, act, cbuf, csem, coef, side, emit)
        drain(image.at[0], give_send)
        others = out_ref.at[pl.ds(0, peers - 2)]
        drain(others, send_sem)
        drain(others, recv_sem)

    vmem = pl.BlockSpec(memory_space=pltpu.VMEM)
    hbm = pl.BlockSpec(memory_space=pl.ANY)
    dma = pltpu.SemaphoreType.DMA
    return pl.pallas_call(
        kernel,
        out_shape=jax.ShapeDtypeStruct((peers, band, chans), BF16),
        in_specs=[vmem, vmem, hbm, vmem],
        out_specs=vmem,
        scratch_shapes=shared_scratch(tokens // 2, width, chans) + [
            pltpu.VMEM((2, ROWS, LANES), F32),
            pltpu.VMEM((2, ROWS, LANES), F32),
            pltpu.VMEM((2, ROWS, chans), F32),
            dma((2,)), dma((2,)), dma, dma((chunks,)), dma, dma, dma((5,)), dma((5,)), dma, dma,
        ],
        compiler_params=pltpu.CompilerParams(vmem_limit_bytes=48000000, collective_id=1, has_side_effects=True),
        cost_estimate=cost_of(36 * tokens * chans * chans, 36 * chans * chans),
        name='res_block_out',
    )(hidden, bias, res_conv, norms)


def in_hbm(array):
    return pltpu.with_memory_space_constraint(array, pltpu.HBM)


def cost_of(flops, nbytes):
    return pl.CostEstimate(flops=flops, bytes_accessed=nbytes, transcendentals=0)


def transformer(hidden, ctx_keys, ctx_vals, norms, norm_row, proj_inout, qkv_t, self_out, cross_q_t, cross_out, ff_in, ff_out, groups, heads, text):
    tokens, chans = hidden.shape
    text_rows = ctx_keys.shape[0]
    head_dim = chans // heads
    pairs = heads // 2
    pair = 2 * head_dim
    count = float(tokens * (chans // groups))
    tiles = tokens // TM
    ff_steps = ff_out.shape[0] // chans
    qw = 512 if chans >= 1024 else CK
    kb = CK
    scale = head_dim ** -0.5
    half = chans // 2

    def kernel(h_ref, ctx_k, ctx_v, norm_ref, pio, wqkv, wo, cq, co, f1, f2, out_ref, ring, tok, aux, both, keys, acc, coef, rsem):
        units = {
            'in': (pio.at[0], 0, 0), 'q': (wqkv.at[0], 0, 1), 'k': (wqkv.at[1], 1, 0), 'v': (wqkv.at[2], 1, 1),
            'o': (wo, 1, 0), 'cq': (cq, 1, 1), 'co': (co, 1, 2), 'out': (pio.at[1], 0, 0),
        }

        def copy_of(name):
            src, group, place = units[name]
            return pltpu.make_async_copy(src, ring.at[group, place], rsem.at[group, place])

        def start(*names):
            for name in names:
                copy_of(name).start()

        def take(name):
            copy_of(name).wait()
            _, group, place = units[name]
            return ring.at[group, place]

        def ff_copies(step, group):
            cols = pl.multiple_of(step * chans, chans)
            return [
                pltpu.make_async_copy(f1.at[:, pl.ds(cols, chans)], ring.at[group, 0], rsem.at[group, 0]),
                pltpu.make_async_copy(f1.at[:, pl.ds(cols + ff_steps * chans, chans)], ring.at[group, 1], rsem.at[group, 1]),
                pltpu.make_async_copy(f2.at[pl.ds(cols, chans), :], ring.at[group, 2], rsem.at[group, 2]),
            ]

        start('in', 'q', 'k', 'v', 'co')

        tot, sqr = channel_sums(h_ref, tokens, chans)
        member = members(chans, groups)
        sums = group_sums(eight_rows(row_sums(tot, sqr)), member)
        group_affine(sums, norm_ref[norm_row:norm_row + 1], norm_ref[norm_row + 1:norm_row + 2], member, count, coef, 1.0)

        def project_rows(weight, src, base, normed_to):
            def norm_tile(tile):
                rows = tile_rows(tile)
                normed_to[rows, :] = layer_norm(tok[rows, :].astype(F32))

            @loop(tiles)
            def _(tile):
                norm_tile(jnp.maximum(tile - 1, 0))
                rows = tile_rows(tile)
                tok[rows, :] = (base(rows) + nn(src(rows), weight[...])).astype(BF16)

            norm_tile(tiles - 1)

        project_rows(take('in'), lambda rows: (h_ref[rows, :].astype(F32) * coef[0:1] + coef[1:2]).astype(BF16), lambda rows: 0.0, aux)

        q_t, v_t = both.at[0], both.at[1]

        def transposed(weight, src, dst, factor):
            @loop(2)
            def _(part):
                rows = pl.ds(pl.multiple_of(part * half, half), half)
                dst[rows, :] = (nt(weight[rows, :], src[...]).astype(BF16) * factor).astype(BF16)

        w_key = take('k')

        @loop(tokens // 512)
        def _(part):
            rows = pl.ds(pl.multiple_of(part * 512, 512), 512)
            keys[rows, :] = nt(aux[rows, :], w_key[...]).astype(BF16)
        start('o')

        @loop(2)
        def _(which):
            pltpu.make_async_copy(wqkv.at[2 * which], ring.at[which, 1], rsem.at[which, 1]).wait()
            transposed(ring.at[which, 1], aux, both.at[which], jnp.where(which == 0, scale, 1.0))
        start('cq')
        for copy in ff_copies(0, 0):
            copy.start()

        row_head = lax.broadcasted_iota(jnp.int32, (pair, 1), 0) < head_dim

        def query_of(hp, first, wide, head):
            both = q_t[pl.ds(pl.multiple_of(hp * pair, pair), pair), pl.ds(first, wide)]
            keep = row_head if head == 0 else jnp.logical_not(row_head)
            return jnp.where(keep, both, jnp.zeros_like(both))

        def pair_cols(hp):
            return pl.ds(pl.multiple_of(hp * pair, pair), pair)

        halves = tokens // qw
        blocks = pairs * halves
        scores = [acc.at[:, pl.ds(h * qw, qw)] for h in range(2)]
        probs = [out_ref.at[:, pl.ds(h * qw, qw)] for h in range(2)]
        parts = tokens // kb

        def place(block):
            hp = lax.div(block, halves)
            return hp, pl.multiple_of((block - hp * halves) * qw, qw)

        def fold(vals, func):
            return func(vals.reshape(-1, ROWS, vals.shape[-1]), axis=0)

        def score_part(block, query, head, part):
            hp, _ = place(block)
            vals = nn(keys[part * kb:(part + 1) * kb, pair_cols(hp)], query)
            scores[head][part * kb:(part + 1) * kb, :] = vals
            return fold(vals, jnp.max)

        def exp_part(head, part, top):
            vals = jnp.exp(scores[head][part * kb:(part + 1) * kb, :] - top)
            probs[head][part * kb:(part + 1) * kb, :] = vals.astype(BF16)
            return fold(vals, jnp.sum)

        def value_of(block, head, denom):
            hp, _ = place(block)
            vals = v_t[pl.ds(pl.multiple_of(hp * pair + head * head_dim, head_dim), head_dim), :]
            return nn(vals, probs[head][...]) * (1.0 / denom)

        def block_query(block, head):
            hp, first = place(block)
            return query_of(hp, first, qw, head)

        def softmax_stage(score_block, score_head, exp_head, top):
            tops, sums = [], []
            query = block_query(score_block, score_head)
            for part in range(parts):
                tops.append(score_part(score_block, query, score_head, part))
                sums.append(exp_part(exp_head, part, top))
            new_top = jnp.max(functools.reduce(jnp.maximum, tops), axis=0, keepdims=True)
            return new_top, jnp.sum(functools.reduce(jnp.add, sums), axis=0, keepdims=True)

        def emit(block, low, high):
            hp, first = place(block)
            aux[pl.ds(first, qw), pair_cols(hp)] = jnp.concatenate([low, high], axis=0).T.astype(BF16)

        top_first = jnp.max(functools.reduce(jnp.maximum, [score_part(0, block_query(0, 0), 0, part) for part in range(parts)]), axis=0, keepdims=True)
        zero_row = jnp.ones((1, qw), F32)
        zero_out = jnp.zeros((head_dim, qw), F32)

        def attend_block(block, carry):
            top0, denom1, low = carry
            before = jnp.maximum(block - 1, 0)
            high = value_of(before, 1, denom1)
            emit(before, low, high)
            top1, denom0 = softmax_stage(block, 1, 0, top0)
            after = jnp.minimum(block + 1, blocks - 1)
            low = value_of(block, 0, denom0)
            top0, denom1 = softmax_stage(after, 0, 1, top1)
            return top0, denom1, low

        def attend_blocks(step, carry):
            for sub in range(4):
                carry = attend_block(step * 4 + sub, carry)
            return carry

        _, denom1, low = lax.fori_loop(0, blocks // 4, attend_blocks, (top_first, zero_row, zero_out))
        emit(blocks - 1, low, value_of(blocks - 1, 1, denom1))

        project_rows(take('o'), lambda rows: aux[rows, :], lambda rows: tok[rows, :].astype(F32), keys)
        transposed(take('cq'), keys, q_t, scale)

        text_valid = lax.broadcasted_iota(jnp.int32, (text_rows, 1), 0) < text

        wide_step = max(count for count in (CROSS_PAIRS, 2, 1) if pairs % count == 0)

        @loop(pairs // wide_step)
        def _(step):
            for sub in range(wide_step):
                hp = step * wide_step + sub
                outs = []
                for head in range(2):
                    vals = nn(ctx_k[:, pair_cols(hp)], query_of(hp, 0, tokens, head))
                    vals = jnp.where(text_valid, vals, -jnp.inf)
                    weights = jnp.exp(vals - jnp.max(vals, axis=0, keepdims=True))
                    denom = jnp.sum(weights, axis=0, keepdims=True)
                    text_vals = ctx_v[pl.ds(pl.multiple_of(hp * pair + head * head_dim, head_dim), head_dim), :]
                    outs.append(nn(text_vals, weights.astype(BF16)) * (1.0 / denom))
                aux[:, pair_cols(hp)] = jnp.concatenate(outs, axis=0).T.astype(BF16)

        project_rows(take('co'), lambda rows: aux[rows, :], lambda rows: tok[rows, :].astype(F32), keys)
        for copy in ff_copies(1, 1):
            copy.start()
        acc[...] = jnp.zeros_like(acc)

        @loop(ff_steps)
        def _(step):
            group = lax.rem(step, 2)
            for copy in ff_copies(step, group):
                copy.wait()

            @loop(tiles, unroll=2)
            def _(tile):
                rows = tile_rows(tile)
                src = keys[rows, :]
                value = nn(src, ring[group, 0])
                gate = nn(src, ring[group, 1])
                gated = (value * (0.5 * gate * (1.0 + lax.erf(gate * (0.5 ** 0.5))))).astype(BF16)
                acc[rows, :] += nn(gated, ring[group, 2])

            @pl.when(step + 2 < ff_steps)
            def _():
                for copy in ff_copies(step + 2, group):
                    copy.start()

            @pl.when(step == ff_steps - 2)
            def _():
                start('out')

        w_fin = take('out')

        @loop(tiles)
        def _(tile):
            rows = tile_rows(tile)
            t = (tok[rows, :].astype(F32) + acc[rows, :]).astype(BF16)
            out_ref[rows, :] = (h_ref[rows, :].astype(F32) + nn(t, w_fin[...])).astype(BF16)

    vmem = pl.BlockSpec(memory_space=pltpu.VMEM)
    hbm = pl.BlockSpec(memory_space=pl.ANY)
    flops = 2 * tokens * chans * chans * (ROWS + 3 * ff_steps) + 4 * tokens * tokens * chans
    return pl.pallas_call(
        kernel,
        out_shape=jax.ShapeDtypeStruct(hidden.shape, BF16),
        in_specs=[vmem] * 4 + [hbm] * 7,
        out_specs=vmem,
        scratch_shapes=[
            pltpu.VMEM((2, 3, chans, chans), BF16),
            pltpu.VMEM((tokens, chans), BF16),
            pltpu.VMEM((tokens, chans), BF16),
            pltpu.VMEM((2, chans, tokens), BF16),
            pltpu.VMEM((tokens, chans), BF16),
            pltpu.VMEM((tokens, chans), F32),
            pltpu.VMEM((ROWS, chans), F32),
            pltpu.SemaphoreType.DMA((2, 3)),
        ],
        compiler_params=pltpu.CompilerParams(vmem_limit_bytes=50000000),
        cost_estimate=cost_of(flops, 50 * chans * chans),
        name='transformer',
    )(hidden, ctx_keys, ctx_vals, norms, proj_inout, qkv_t, self_out, cross_q_t, cross_out, ff_in, ff_out)


def solution(mesh):
    num_bands = mesh.shape['sp']

    def local_stage(latent, time_emb, context, res_conv, res_time, res_norm, attn_norm, proj_inout, self_qkv, self_out, cross_q, cross_kv, cross_out, ff_in, ff_out):
        images, band_rows, width, chans = latent.shape
        assert images == num_bands
        band = band_rows * width
        heads, head_dim = self_out.shape[:2]
        groups = res_norm.shape[3]
        text, text_dim = context.shape[1:]
        flat_kv = jnp.transpose(cross_kv, (0, 2, 3, 1)).reshape(2, chans, text_dim)
        first, norms, bias, ctx_keys, ctx_vals = res_block_in(
            latent.reshape(images, band, chans), in_hbm(time_emb), jnp.transpose(context, (1, 0, 2)).reshape(text * images, text_dim), res_conv, res_time,
            in_hbm(res_norm.reshape((-1,) + res_norm.shape[3:])), in_hbm(attn_norm), flat_kv, text, width)
        middle = transformer(
            first, ctx_keys, ctx_vals, norms, res_norm.shape[0] * res_norm.shape[1] * res_norm.shape[2], proj_inout,
            jnp.transpose(self_qkv, (0, 2, 3, 1)).reshape(3, chans, chans),
            self_out.reshape(chans, chans),
            jnp.transpose(cross_q, (1, 2, 0)).reshape(chans, chans),
            cross_out.reshape(chans, chans), ff_in, ff_out, groups, heads, text)
        out = res_block_out(middle, bias, res_conv, norms, width, groups, num_bands)
        return out.reshape(latent.shape)

    band_spec = P('dp', 'sp', None, None)
    shared = P()
    in_specs = (band_spec, P('dp', None), P('dp', None, None)) + (shared,) * 12
    return jax.shard_map(local_stage, mesh=mesh, in_specs=in_specs, out_specs=band_spec, check_vma=False)
```

time: 334 us -> 365 us (1.093)
  Pallas kernels: 328 us -> 362 us
    pallas_call x1, Pallas kernels: 102 us -> 131 us  [res_block_out(): pl.pallas_call(kernel, out_shape=jax.ShapeDtypeStruct((peers, band, chans...]
    pallas_call x1, Pallas kernels: 112 us -> 117 us  [res_block_in(): pl.pallas_call(kernel, out_shape=[jax.ShapeDtypeStruct((tokens, chans), B...]
where the time goes in v7:
time: 365 us; the launch traced here: 363 us
  Pallas kernels  362 us (99%)
    pallas_call x1, Pallas kernels, res_block_out(): pl.pallas_call(kernel, out_shape=jax.ShapeDtypeStruct((peers, band, chans...  131 us
    pallas_call x1, Pallas kernels, res_block_in(): pl.pallas_call(kernel, out_shape=[jax.ShapeDtypeStruct((tokens, chans), B...  117 us
    pallas_call x1, Pallas kernels, transformer(): pl.pallas_call(kernel, out_shape=jax.ShapeDtypeStruct(hidden.shape, BF16)...  114 us

profile of v7, /device:TPU:30, one launch (start us, length us, event | category | flops | bytes accessed | tf_op | source)
XLA Modules:
  0.0 363.3 jit_solution(2235070863585398200)
XLA Ops:
  0.0 116.8 %res_block_in.1 = (bf16[1024,1280]{1,0:T(8,128)(2,1)S(1)}, f32[16,1280]{1,0:T(8,128)S(1)}, f32[2,1280]{1,0:T(2,128)S(1)}, bf16[80,1280]{1,0:T(8,128)(2,1)S(1)}, bf16[1280,80]{1,0:T(8,128)(2,1)S(1)}) custom-call(bf16[16,64,1280]{2,1,0:T(8,128)(2,1)} %bitcast.24, bf16[16,1280]{1,0:T(8,128)(2,1)} %time_hbm.1, bf16[1232,2048]{1,0:T(8,128)(2,1)} %bitcast.20, ...), custom_call_target="tpu_custom_call" | custom-call | flops 60397977600 | bytes 58982400 | tf_op jit(solution)/shard_map/res_block_in/pallas_call | solution.py:504
  116.8 113.6 %transformer.1.hid = bf16[1024,1280]{1,0:T(8,128)(2,1)S(1)} custom-call(bf16[1024,1280]{1,0:T(8,128)(2,1)S(1)} %get-tuple-element.10.h_ref, bf16[80,1280]{1,0:T(8,128)(2,1)S(1)} %get-tuple-element.11.ctx_k, bf16[1280,80]{1,0:T(8,128)(2,1)S(1)} %get-tuple-element.12.ctx_v, f32[16,1280]{1,0:T(8,128)S(1)} %get-tuple-element.13.norm_ref, ...), custom_call_target="tpu_custom_call" | custom-call | flops 72477573120 | bytes 81920000 | tf_op jit(solution)/shard_map/transformer/pallas_call | solution.py:894
  230.4 131.5 %res_block_out.1 = bf16[16,64,1280]{2,1,0:T(8,128)(2,1)S(1)} custom-call(bf16[1024,1280]{1,0:T(8,128)(2,1)S(1)} %transformer.1.hid, f32[2,1280]{1,0:T(2,128)S(1)} %get-tuple-element.14.bias_ref, bf16[2,2,3,3,1280,1280]{5,4,3,2,1,0:T(8,128)(2,1)} %kern.3, f32[16,1280]{1,0:T(8,128)S(1)} %get-tuple-element.13.norm_ref), custom_call_target="tpu_custom_call" | custom-call | flops 60397977600 | bytes 58982400 | tf_op jit(solution)/shard_map/res_block_out/pallas_call | solution.py:642
  361.9 1.5 copy.17

commit v8 on v7

--- a/solution.py
+++ b/solution.py
@@ -18,11 +18,15 @@
 ROWS = 8
 STEP = 64
 CROSS_PAIRS = 5
-VMEM_LIMIT = 67_000_000
+VMEM_IN, VMEM_MID, VMEM_OUT = 53_000_000, 48_000_000, 50_000_000
 
 
 def loop(stop, **options):
     return pl.loop(0, stop, **options)
+
+
+def keep_sum(vals):
+    return jnp.sum(vals, axis=0, keepdims=True)
 
 
 def one_hot(mask):
@@ -87,10 +91,10 @@
     return pl.ds(pl.multiple_of(first + tile * TM, 32), TM)
 
 
-def members(chans, groups, offset=0):
+def members(chans, groups):
     width = chans // groups
     chan = lax.broadcasted_iota(jnp.int32, (chans, LANES), 0)
-    low = (lax.broadcasted_iota(jnp.int32, (chans, LANES), 1) - offset) * width
+    low = (lax.broadcasted_iota(jnp.int32, (chans, LANES), 1)) * width
     return one_hot((chan >= low) & (chan < low + width))
 
 
@@ -106,13 +110,13 @@
     rstd = lax.rsqrt(sums[1:2] / count - mean * mean + GN_EPS)
     back = jnp.concatenate(split3(mean) + split3(rstd) + [jnp.zeros((2, LANES), F32)], axis=0).astype(BF16)
     wide = nt(back, member)
-    scale = jnp.sum(wide[3:6], axis=0, keepdims=True) * gain
+    scale = keep_sum(wide[3:6]) * gain
     coef[0:1, :] = factor * scale
-    coef[1:2, :] = factor * (shift - jnp.sum(wide[:3], axis=0, keepdims=True) * scale)
+    coef[1:2, :] = factor * (shift - keep_sum(wide[:3]) * scale)
 
 
 def row_sums(tot, sqr):
-    return [jnp.sum(tot, axis=0, keepdims=True), jnp.sum(sqr, axis=0, keepdims=True)]
+    return [keep_sum(tot), keep_sum(sqr)]
 
 
 def eight_rows(rows):
@@ -313,7 +317,7 @@
     wide = lax.dot_general(param, spread, (((0,), (0,)), ((), ())), preferred_element_type=F32)
     place = lax.broadcasted_iota(jnp.int32, (width, chans), 0)
     inside = lax.rem(lax.broadcasted_iota(jnp.int32, (width, chans), 1), width)
-    return jnp.sum(jnp.where(place == inside, wide, 0.0), axis=0, keepdims=True)
+    return keep_sum(jnp.where(place == inside, wide, 0.0))
 
 
 def res_block_in(latent, time_emb, context, res_conv, res_time, res_norm, attn_norm, cross_kv, text, width):
@@ -329,7 +333,7 @@
     ctx_half = text_dim // 2
 
     def kernel(lat, time_hbm, ctx_hbm, kern, wtime, norm_hbm, attn_hbm, ckv, out_ref, norm_ref, bias_ref, ctx_k, ctx_v,
-               image, mid, act, wbuf, cbuf, acc, time_ref, tproj, rows, bias, mine, stats, sums, coef, norm_raw, attn_raw, ctx_mine,
+               image, mid, act, wbuf, cbuf, acc, time_ref, tproj, rows, bias, mine, stats, sums, coef, norm_raw, attn_raw, ctx_mine, landed,
                wsem, csem, tsem, own_sem, small_sem, ctx_sem, send_sem, side_sem, recv_sem, stat_send, stat_recv, swap_send, swap_recv, give_send, give_recv):
         pair = Pair(peers, band, width)
         me = pair.me
@@ -394,7 +398,7 @@
         def _(peer):
             vals = own_rows(peer)[...].astype(F32).reshape(band // ROWS, ROWS, chans)
             for part, total in enumerate((vals, vals * vals)):
-                rows[pl.ds(part * peers + peer, 1), :] = jnp.sum(jnp.sum(total, axis=0), axis=0, keepdims=True)
+                rows[pl.ds(part * peers + peer, 1), :] = keep_sum(jnp.sum(total, axis=0))
 
         found = group_sums(rows[...], member)
         for peer in range(peers):
@@ -476,24 +480,33 @@
         pair.swap_norm(mid, acc, bias, sums, member, norm_ref, row + 2, count, coef, swap_send, swap_recv)
         give = 1 - pair.side
 
+        blocks = TM // pair.sub
+
+        def image_rows(slot, index, side=None):
+            return pl.ds(pl.multiple_of(pair.block_chip(slot, index, side) * pair.sub, pair.sub), pair.sub)
+
         def emit(slot, tile, place, cols, vals):
-            blocks = TM // pair.sub
-            spots = [pl.ds(pl.multiple_of(pair.block_chip(slot, blocks * tile + index) * pair.sub, pair.sub), pair.sub) for index in range(blocks)]
-
             @pl.when(slot == give)
             def _():
                 image[slot, place, cols] = vals
-                for index, spot in enumerate(spots):
-                    remote(image.at[slot, pair.block_rows(blocks * tile + index), cols], out_ref.at[spot, cols], give_send, give_recv, pair.partner).start()
+
+                @pl.when(tile == pair.rows // TM - 1)
+                def _():
+                    remote(image.at[slot, pl.ds(width, pair.rows), cols], landed.at[:, cols], give_send, give_recv, pair.partner).start()
 
             @pl.when(slot != give)
             def _():
-                for index, spot in enumerate(spots):
-                    out_ref[spot, cols] = vals[index * pair.sub:(index + 1) * pair.sub]
+                for index in range(blocks):
+                    out_ref[image_rows(slot, blocks * tile + index), cols] = vals[index * pair.sub:(index + 1) * pair.sub]
 
         conv_columns(pair, kern, which, image, mid, act, cbuf, csem, coef, give, emit)
         for sem in (give_send, give_recv):
-            drain(out_ref.at[pl.ds(0, pair.rows)], sem)
+            drain(landed, sem)
+
+        @loop(pair.half)
+        def _(index):
+            out_ref[image_rows(pair.side, index, give), :] = landed[pl.ds(pl.multiple_of(index * pair.sub, pair.sub), pair.sub), :]
+
         drain(lat.at[pl.ds(0, peers - 2)], send_sem)
         drain(lat.at[0:2], side_sem)
 
@@ -524,9 +537,10 @@
             pltpu.VMEM(res_norm.shape, BF16),
             pltpu.VMEM(attn_norm.shape, BF16),
             pltpu.VMEM((text_rows, text_dim), BF16),
+            pltpu.VMEM((rows, chans), BF16),
             dma((2,)), dma((2,)), dma, dma, dma((3,)), dma((2,)), dma, dma, dma((chunks,)), dma, dma, dma((5,)), dma((5,)), dma, dma,
         ],
-        compiler_params=pltpu.CompilerParams(vmem_limit_bytes=53000000, collective_id=0, has_side_effects=True),
+        compiler_params=pltpu.CompilerParams(vmem_limit_bytes=VMEM_IN, collective_id=0, has_side_effects=True),
         cost_estimate=cost_of(36 * tokens * chans * chans, 36 * chans * chans),
         name='res_block_in',
     )(latent, time_emb, context, res_conv, res_time, res_norm, attn_norm, cross_kv)
@@ -567,19 +581,25 @@
             return [(image_rows(index, 0, pair.sub), pair.block_rows(index)) for index in range(pair.half)] + [
                 (image_rows(0, tokens - width, width), pl.ds(0, width)), (image_rows(pair.half, 0, width), pl.ds(width + pair.rows, width))]
 
-        await_peers(peers)
+        beside = pl.ds(0, image.shape[1])
 
         @loop(chunks)
         def _(chunk):
             cols = chunk_cols(chunk)
             for src, dst in pieces(1 - side):
-                remote(hid.at[src, cols], image.at[side, dst, cols], give_send, give_recv.at[chunk], pair.partner).start()
+                cbuf[1, chunk, dst, :] = hid[src, cols]
+
+        for src, dst in pieces(side):
+            image[side, dst, :] = hid[src, :]
+        await_peers(peers)
+
+        @loop(chunks)
+        def _(chunk):
+            remote(cbuf.at[1, chunk, beside, :], image.at[side, :, chunk_cols(chunk)], give_send, give_recv.at[chunk], pair.partner).start()
 
         owned[side] = group_sums(eight_rows(row_sums(*channel_sums(hid, tokens, chans))), member)
         tell = remote(owned.at[side], owned.at[side], tell_send, tell_recv, pair.partner)
         tell.start()
-        for src, dst in pieces(side):
-            image[side, dst, :] = hid[src, :]
         acc[...] = jnp.zeros_like(acc)
         tell.wait()
         row = 4 * which
@@ -610,6 +630,7 @@
                 pair.tiles(body, slot)
 
         start_all(fetch_cols(kern, which, 1, 0, cbuf, csem))
+        drain(cbuf.at[1, 0:chunks, beside, :], give_send)
         pair.swap_norm(mid, acc, bias_ref, sums, member, norm_ref, row + 2, count, coef, swap_send, swap_recv)
 
         def emit(slot, tile, place, cols, vals):
@@ -631,7 +652,6 @@
                         remote(src, out_ref.at[slab, :, cols], send_sem, recv_sem, peer).start()
 
         conv_columns(pair, kern, which, image, mid, act, cbuf, csem, coef, side, emit)
-        drain(image.at[0], give_send)
         others = out_ref.at[pl.ds(0, peers - 2)]
         drain(others, send_sem)
         drain(others, recv_sem)
@@ -650,7 +670,7 @@
             pltpu.VMEM((2, ROWS, chans), F32),
             dma((2,)), dma((2,)), dma, dma((chunks,)), dma, dma, dma((5,)), dma((5,)), dma, dma,
         ],
-        compiler_params=pltpu.CompilerParams(vmem_limit_bytes=48000000, collective_id=1, has_side_effects=True),
+        compiler_params=pltpu.CompilerParams(vmem_limit_bytes=VMEM_OUT, collective_id=1, has_side_effects=True),
         cost_estimate=cost_of(36 * tokens * chans * chans, 36 * chans * chans),
         name='res_block_out',
     )(hidden, bias, res_conv, norms)
@@ -801,7 +821,7 @@
                 tops.append(score_part(score_block, query, score_head, part))
                 sums.append(exp_part(exp_head, part, top))
             new_top = jnp.max(functools.reduce(jnp.maximum, tops), axis=0, keepdims=True)
-            return new_top, jnp.sum(functools.reduce(jnp.add, sums), axis=0, keepdims=True)
+            return new_top, keep_sum(functools.reduce(jnp.add, sums))
 
         def emit(block, low, high):
             hp, first = place(block)
@@ -846,7 +866,7 @@
                     vals = nn(ctx_k[:, pair_cols(hp)], query_of(hp, 0, tokens, head))
                     vals = jnp.where(text_valid, vals, -jnp.inf)
                     weights = jnp.exp(vals - jnp.max(vals, axis=0, keepdims=True))
-                    denom = jnp.sum(weights, axis=0, keepdims=True)
+                    denom = keep_sum(weights)
                     text_vals = ctx_v[pl.ds(pl.multiple_of(hp * pair + head * head_dim, head_dim), head_dim), :]
                     outs.append(nn(text_vals, weights.astype(BF16)) * (1.0 / denom))
                 aux[:, pair_cols(hp)] = jnp.concatenate(outs, axis=0).T.astype(BF16)
@@ -906,7 +926,7 @@
             pltpu.VMEM((ROWS, chans), F32),
             pltpu.SemaphoreType.DMA((2, 3)),
         ],
-        compiler_params=pltpu.CompilerParams(vmem_limit_bytes=50000000),
+        compiler_params=pltpu.CompilerParams(vmem_limit_bytes=VMEM_MID),
         cost_estimate=cost_of(flops, 50 * chans * chans),
         name='transformer',
     )(hidden, ctx_keys, ctx_vals, norms, proj_inout, qkv_t, self_out, cross_q_t, cross_out, ff_in, ff_out)

time: 365 us -> 367 us (level)
  no operation moved by 1% of the time
where the time goes in v8:
time: 367 us; the launch traced here: 365 us
  Pallas kernels  364 us (99%)
    pallas_call x1, Pallas kernels, res_block_out(): pl.pallas_call(kernel, out_shape=jax.ShapeDtypeStruct((peers, band, chans...  132 us
    pallas_call x1, Pallas kernels, res_block_in(): pl.pallas_call(kernel, out_shape=[jax.ShapeDtypeStruct((tokens, chans), B...  118 us
    pallas_call x1, Pallas kernels, transformer(): pl.pallas_call(kernel, out_shape=jax.ShapeDtypeStruct(hidden.shape, BF16)...  114 us

profile of v8, /device:TPU:30, one launch (start us, length us, event | category | flops | bytes accessed | tf_op | source)
XLA Modules:
  0.0 365.4 jit_solution(15715883817990371445)
XLA Ops:
  0.0 117.9 %res_block_in.1 = (bf16[1024,1280]{1,0:T(8,128)(2,1)S(1)}, f32[16,1280]{1,0:T(8,128)S(1)}, f32[2,1280]{1,0:T(2,128)S(1)}, bf16[80,1280]{1,0:T(8,128)(2,1)S(1)}, bf16[1280,80]{1,0:T(8,128)(2,1)S(1)}) custom-call(bf16[16,64,1280]{2,1,0:T(8,128)(2,1)} %bitcast.24, bf16[16,1280]{1,0:T(8,128)(2,1)} %time_hbm.1, bf16[1232,2048]{1,0:T(8,128)(2,1)} %bitcast.20, ...), custom_call_target="tpu_custom_call" | custom-call | flops 60397977600 | bytes 58982400 | tf_op jit(solution)/shard_map/res_block_in/pallas_call | solution.py:517
  117.9 113.5 %transformer.1.hid = bf16[1024,1280]{1,0:T(8,128)(2,1)S(1)} custom-call(bf16[1024,1280]{1,0:T(8,128)(2,1)S(1)} %get-tuple-element.10.h_ref, bf16[80,1280]{1,0:T(8,128)(2,1)S(1)} %get-tuple-element.11.ctx_k, bf16[1280,80]{1,0:T(8,128)(2,1)S(1)} %get-tuple-element.12.ctx_v, f32[16,1280]{1,0:T(8,128)S(1)} %get-tuple-element.13.norm_ref, ...), custom_call_target="tpu_custom_call" | custom-call | flops 72477573120 | bytes 81920000 | tf_op jit(solution)/shard_map/transformer/pallas_call | solution.py:914
  231.5 132.4 %res_block_out.1 = bf16[16,64,1280]{2,1,0:T(8,128)(2,1)S(1)} custom-call(bf16[1024,1280]{1,0:T(8,128)(2,1)S(1)} %transformer.1.hid, f32[2,1280]{1,0:T(2,128)S(1)} %get-tuple-element.14.bias_ref, bf16[2,2,3,3,1280,1280]{5,4,3,2,1,0:T(8,128)(2,1)} %kern.3, f32[16,1280]{1,0:T(8,128)S(1)} %get-tuple-element.13.norm_ref), custom_call_target="tpu_custom_call" | custom-call | flops 60397977600 | bytes 58982400 | tf_op jit(solution)/shard_map/res_block_out/pallas_call | solution.py:662
  363.9 1.5 copy.17

commit v9 on v6

--- a/solution.py
+++ b/solution.py
@@ -15,7 +15,19 @@
 TM = 256
 CK = 256
 CROSS_PAIRS = 5
-VMEM_LIMIT = 67_000_000
+VMEM_IN, VMEM_MID, VMEM_OUT = 53_000_000, 48_000_000, 49_000_000
+
+
+def loop(stop, **options):
+    return pl.loop(0, stop, **options)
+
+
+def one_hot(mask):
+    return mask.astype(F32).astype(BF16)
+
+
+def keep_sum(vals):
+    return jnp.sum(vals, axis=0, keepdims=True)
 
 
 def nn(lhs, rhs):
@@ -56,6 +68,11 @@
         pl.semaphore_signal(barrier, inc=1, device_id={'sp': lax.rem(me + step, peers)}, device_id_type=MESH)
 
 
+def both_ways(step, peers):
+    hop = lax.div(step + 1, 2)
+    return jnp.where(lax.rem(step, 2) == 1, hop, peers - hop)
+
+
 def await_peers(peers):
     pl.semaphore_wait(pltpu.get_barrier_semaphore(), peers - 1)
 
@@ -80,7 +97,7 @@
     width = chans // groups
     chan = lax.broadcasted_iota(jnp.int32, (chans, 128), 0)
     low = (lax.broadcasted_iota(jnp.int32, (chans, 128), 1) - offset) * width
-    return jnp.where((chan >= low) & (chan < low + width), 1.0, 0.0).astype(BF16)
+    return one_hot((chan >= low) & (chan < low + width))
 
 
 def group_sums(rows, member):
@@ -95,13 +112,13 @@
     rstd = lax.rsqrt(sums[1:2] / count - mean * mean + GN_EPS)
     back = jnp.concatenate(split3(mean) + split3(rstd) + [jnp.zeros((2, 128), F32)], axis=0).astype(BF16)
     wide = nt(back, member)
-    scale = jnp.sum(wide[3:6], axis=0, keepdims=True) * gain
+    scale = keep_sum(wide[3:6]) * gain
     coef[0:1, :] = factor * scale
-    coef[1:2, :] = factor * (shift - jnp.sum(wide[:3], axis=0, keepdims=True) * scale)
+    coef[1:2, :] = factor * (shift - keep_sum(wide[:3]) * scale)
 
 
 def two_rows(tot, sqr):
-    rows = [jnp.sum(tot, axis=0, keepdims=True), jnp.sum(sqr, axis=0, keepdims=True)]
+    rows = [keep_sum(tot), keep_sum(sqr)]
     return jnp.concatenate(rows + [jnp.zeros((6, tot.shape[1]), F32)], axis=0)
 
 
@@ -178,11 +195,11 @@
     def build(chunk, tile):
         activate(src, act, coef, pl.multiple_of(chunk * CK, CK), CK, tile * TM, TM, width)
 
-    @pl.loop(0, tokens // TM)
+    @loop(tokens // TM)
     def _(tile):
         build(0, tile)
 
-    @pl.loop(0, chunks)
+    @loop(chunks)
     def _(chunk):
         @pl.when(chunk + 1 < chunks)
         def _():
@@ -190,14 +207,14 @@
 
         wait_all(fetch(chunk))
 
-        @pl.loop(0, tokens // TM)
+        @loop(tokens // TM)
         def _(tile):
             acc[tile_rows(tile), :] += chunk_product(act, wbuf, lax.rem(chunk, 2), chunk, tile, width)
             build(lax.rem(chunk + 1, chunks), tile)
 
 
 def add_rows(dst, acc, other):
-    @pl.loop(0, acc.shape[0] // 64)
+    @loop(acc.shape[0] // 64)
     def _(idx):
         rows = pl.ds(pl.multiple_of(idx * 64, 64), 64)
         dst[rows, :] = (other[rows, :].astype(F32) + acc[rows, :]).astype(BF16)
@@ -218,11 +235,11 @@
     groups, width = param.shape
     group = lax.broadcasted_iota(jnp.int32, (groups, chans), 0) * width
     chan = lax.broadcasted_iota(jnp.int32, (groups, chans), 1)
-    spread = jnp.where((chan >= group) & (chan < group + width), 1.0, 0.0).astype(BF16)
+    spread = one_hot((chan >= group) & (chan < group + width))
     wide = lax.dot_general(param, spread, (((0,), (0,)), ((), ())), preferred_element_type=F32)
     place = lax.broadcasted_iota(jnp.int32, (width, chans), 0)
     inside = lax.rem(lax.broadcasted_iota(jnp.int32, (width, chans), 1), width)
-    return jnp.sum(jnp.where(place == inside, wide, 0.0), axis=0, keepdims=True)
+    return keep_sum(jnp.where(place == inside, wide, 0.0))
 
 
 def norm_from(src, member, norm_ref, row, count, coef):
@@ -282,17 +299,17 @@
 
             @pl.loop(1, peers)
             def _(step):
-                peer = lax.rem(me + step, peers)
+                peer = lax.rem(me + both_ways(step, peers), peers)
                 remote(lat.at[peer, :, pl.ds(first, wide)], image.at[own_rows, pl.ds(first, wide)], send_sem.at[index], recv_sem.at[index], peer).start()
 
         send(0)
         wait_all(load)
 
-        @pl.loop(0, peers)
+        @loop(peers)
         def _(peer):
             vals = own[pl.ds(pl.multiple_of(peer * band, band), band), :].astype(F32).reshape(band // 8, 8, chans)
-            rows[pl.ds(peer, 1), :] = jnp.sum(jnp.sum(vals, axis=0), axis=0, keepdims=True)
-            rows[pl.ds(peers + peer, 1), :] = jnp.sum(jnp.sum(vals * vals, axis=0), axis=0, keepdims=True)
+            rows[pl.ds(peer, 1), :] = keep_sum(jnp.sum(vals, axis=0))
+            rows[pl.ds(peers + peer, 1), :] = keep_sum(jnp.sum(vals * vals, axis=0))
 
         sums = group_sums(rows[...], member)
         for peer in range(peers):
@@ -321,12 +338,12 @@
         ctx_copies[0].wait()
         place = (text_rows, text * peers)
         wanted = lax.broadcasted_iota(jnp.int32, place, 0) * peers + me
-        pick = jnp.where(lax.broadcasted_iota(jnp.int32, place, 1) == wanted, 1.0, 0.0).astype(BF16)
+        pick = one_hot(lax.broadcasted_iota(jnp.int32, place, 1) == wanted)
         ctx_mine[...] = nn(pick, ctx_raw[...]).astype(BF16)
         ctx_copies[1].wait()
         ctx_k[...] = nt(ctx_mine[...], ckv_buf[0]).astype(BF16)
 
-        @pl.loop(0, chans // 256)
+        @loop(chans // 256)
         def _(part):
             part_rows = pl.ds(pl.multiple_of(part * 256, 256), 256)
             ctx_v[part_rows, :] = nt(ckv_buf[1, part_rows, :], ctx_mine[...]).astype(BF16)
@@ -342,7 +359,7 @@
             first, wide = pieces[index]
             return image.at[pl.ds(0, tokens - band), pl.ds(first, wide)]
 
-        @pl.loop(0, last)
+        @loop(last)
         def _(chunk):
             @pl.when(chunk + 1 < last)
             def _():
@@ -355,26 +372,26 @@
             wait_all(fetch_rows(kern, which, 0, chunk, wbuf, wsem))
             drain(image.at[pl.ds(0, tokens - band), chunk_cols(chunk)], recv_sem.at[chunk])
 
-            @pl.loop(0, tiles)
+            @loop(tiles)
             def _(tile):
                 activate(image, act, coef, pl.multiple_of(chunk * CK, CK), CK, tile * TM, TM, width)
 
-            @pl.loop(0, tiles)
+            @loop(tiles)
             def _(tile):
                 acc[tile_rows(tile), :] += chunk_product(act, wbuf, lax.rem(chunk, 2), chunk, tile, width)
 
         wait_all(fetch_halves(kern, which, 0, last, wbuf, wsem))
 
-        @pl.loop(0, 2)
+        @loop(2)
         def _(part):
             first = pl.multiple_of(last * CK + part * half, half)
             drain(image.at[pl.ds(0, tokens - band), pl.ds(first, half)], recv_sem.at[last + part])
 
-            @pl.loop(0, tiles)
+            @loop(tiles)
             def _(tile):
                 activate(image, act, coef, first, half, tile * TM, TM, width)
 
-            @pl.loop(0, tiles)
+            @loop(tiles)
             def _(tile):
                 acc[tile_rows(tile), :] += half_product(act, wbuf, last % 2, first, part, tile, width)
 
@@ -418,7 +435,7 @@
             pltpu.VMEM(cross_kv.shape, BF16),
             dma((2,)), dma, dma, dma((3,)), dma((2,)), dma((len(pieces),)), dma((len(pieces),)), dma, dma,
         ],
-        compiler_params=pltpu.CompilerParams(vmem_limit_bytes=53000000, collective_id=0, has_side_effects=True),
+        compiler_params=pltpu.CompilerParams(vmem_limit_bytes=VMEM_IN, collective_id=0, has_side_effects=True),
         cost_estimate=cost_of(36 * tokens * chans * chans, 36 * chans * chans),
         name='res_block_in',
     )(latent, time_emb, context, res_conv, res_time, res_norm, attn_norm, cross_kv)
@@ -446,7 +463,7 @@
         add_and_norm(mid, acc, bias_ref[...], member, norm_ref, row + 2, count, coef)
 
         def build(row, rows):
-            @pl.loop(0, chunks)
+            @loop(chunks)
             def _(chunk):
                 activate(mid, act, coef, pl.multiple_of(chunk * CK, CK), CK, row, rows, width)
 
@@ -466,7 +483,7 @@
 
         await_peers(peers)
 
-        @pl.loop(0, chunks)
+        @loop(chunks)
         def _(chunk):
             slot = lax.rem(chunk, 2)
             cols = chunk_cols(chunk)
@@ -477,7 +494,7 @@
 
             wait_all(fetch_cols(kern, which, 1, chunk, cbuf, csem))
 
-            @pl.loop(0, tiles)
+            @loop(tiles)
             def _(step):
                 tile = lax.rem(step + turn, tiles)
                 part = sum(nn(shifted(act, dx, tile, dy, width, slice(None)), cbuf[slot, tap]) for tap, (dy, dx) in enumerate(taps()))
@@ -521,7 +538,7 @@
             pltpu.VMEM((8, chans), F32),
             dma((2,)), dma((2,)), dma, dma,
         ],
-        compiler_params=pltpu.CompilerParams(vmem_limit_bytes=48000000, collective_id=1, has_side_effects=True),
+        compiler_params=pltpu.CompilerParams(vmem_limit_bytes=VMEM_OUT, collective_id=1, has_side_effects=True),
         cost_estimate=cost_of(36 * tokens * chans * chans, 36 * chans * chans),
         name='res_block_out',
     )(hidden, bias, res_conv, norms)
@@ -584,7 +601,7 @@
                 rows = tile_rows(tile)
                 normed_to[rows, :] = layer_norm(tok[rows, :].astype(F32))
 
-            @pl.loop(0, tiles)
+            @loop(tiles)
             def _(tile):
                 norm_tile(jnp.maximum(tile - 1, 0))
                 rows = tile_rows(tile)
@@ -597,20 +614,20 @@
         q_t, v_t = both.at[0], both.at[1]
 
         def transposed(weight, src, dst, factor):
-            @pl.loop(0, 2)
+            @loop(2)
             def _(part):
                 rows = pl.ds(pl.multiple_of(part * half, half), half)
                 dst[rows, :] = (nt(weight[rows, :], src[...]).astype(BF16) * factor).astype(BF16)
 
         w_key = take('k')
 
-        @pl.loop(0, tokens // 512)
+        @loop(tokens // 512)
         def _(part):
             rows = pl.ds(pl.multiple_of(part * 512, 512), 512)
             keys[rows, :] = nt(aux[rows, :], w_key[...]).astype(BF16)
         start('o')
 
-        @pl.loop(0, 2)
+        @loop(2)
         def _(which):
             pltpu.make_async_copy(wqkv.at[2 * which], ring.at[which, 1], rsem.at[which, 1]).wait()
             transposed(ring.at[which, 1], aux, both.at[which], jnp.where(which == 0, scale, 1.0))
@@ -668,7 +685,7 @@
                 tops.append(score_part(score_block, query, score_head, part))
                 sums.append(exp_part(exp_head, part, top))
             new_top = jnp.max(functools.reduce(jnp.maximum, tops), axis=0, keepdims=True)
-            return new_top, jnp.sum(functools.reduce(jnp.add, sums), axis=0, keepdims=True)
+            return new_top, keep_sum(functools.reduce(jnp.add, sums))
 
         def emit(block, low, high):
             hp, first = place(block)
@@ -704,7 +721,7 @@
 
         wide_step = max(count for count in (CROSS_PAIRS, 2, 1) if pairs % count == 0)
 
-        @pl.loop(0, pairs // wide_step)
+        @loop(pairs // wide_step)
         def _(step):
             for sub in range(wide_step):
                 hp = step * wide_step + sub
@@ -713,7 +730,7 @@
                     vals = nn(ctx_k[:, pair_cols(hp)], query_of(hp, 0, tokens, head))
                     vals = jnp.where(text_valid, vals, -jnp.inf)
                     weights = jnp.exp(vals - jnp.max(vals, axis=0, keepdims=True))
-                    denom = jnp.sum(weights, axis=0, keepdims=True)
+                    denom = keep_sum(weights)
                     text_vals = ctx_v[pl.ds(pl.multiple_of(hp * pair + head * head_dim, head_dim), head_dim), :]
                     outs.append(nn(text_vals, weights.astype(BF16)) * (1.0 / denom))
                 aux[:, pair_cols(hp)] = jnp.concatenate(outs, axis=0).T.astype(BF16)
@@ -723,13 +740,13 @@
             copy.start()
         acc[...] = jnp.zeros_like(acc)
 
-        @pl.loop(0, ff_steps)
+        @loop(ff_steps)
         def _(step):
             group = lax.rem(step, 2)
             for copy in ff_copies(step, group):
                 copy.wait()
 
-            @pl.loop(0, tiles, unroll=2)
+            @loop(tiles, unroll=2)
             def _(tile):
                 rows = tile_rows(tile)
                 src = keys[rows, :]
@@ -749,7 +766,7 @@
 
         w_fin = take('out')
 
-        @pl.loop(0, tiles)
+        @loop(tiles)
         def _(tile):
             rows = tile_rows(tile)
             t = (tok[rows, :].astype(F32) + acc[rows, :]).astype(BF16)
@@ -773,7 +790,7 @@
             pltpu.VMEM((8, chans), F32),
             pltpu.SemaphoreType.DMA((2, 3)),
         ],
-        compiler_params=pltpu.CompilerParams(vmem_limit_bytes=49000000),
+        compiler_params=pltpu.CompilerParams(vmem_limit_bytes=VMEM_MID),
         cost_estimate=cost_of(flops, 50 * chans * chans),
         name='transformer',
     )(hidden, ctx_keys, ctx_vals, norms, proj_inout, qkv_t, self_out, cross_q_t, cross_out, ff_in, ff_out)
@@ -791,8 +808,8 @@
         text, text_dim = context.shape[1:]
         flat_kv = jnp.transpose(cross_kv, (0, 2, 3, 1)).reshape(2, chans, text_dim)
         first, norms, bias, ctx_keys, ctx_vals = res_block_in(
-            latent.reshape(images, band, chans), time_emb, jnp.transpose(context, (1, 0, 2)).reshape(text * images, text_dim), res_conv, res_time,
-            res_norm.reshape((-1,) + res_norm.shape[3:]), attn_norm, flat_kv, text, width)
+            latent.reshape(images, band, chans), pltpu.with_memory_space_constraint(time_emb, pltpu.HBM), jnp.transpose(context, (1, 0, 2)).reshape(text * images, text_dim), res_conv, res_time,
+            pltpu.with_memory_space_constraint(res_norm.reshape((-1,) + res_norm.shape[3:]), pltpu.HBM), pltpu.with_memory_space_constraint(attn_norm, pltpu.HBM), flat_kv, text, width)
         middle = transformer(
             first, ctx_keys, ctx_vals, norms, res_norm.shape[0] * res_norm.shape[1] * res_norm.shape[2], proj_inout,
             jnp.transpose(self_qkv, (0, 2, 3, 1)).reshape(3, chans, chans),

time: 334 us -> 332 us (level)
  no operation moved by 1% of the time
where the time goes in v9:
time: 332 us; the launch traced here: 331 us
  Pallas kernels  329 us (99%)
    pallas_call x1, Pallas kernels, transformer(): pl.pallas_call(kernel, out_shape=jax.ShapeDtypeStruct(hidden.shape, BF16)...  113 us
    pallas_call x1, Pallas kernels, res_block_in(): pl.pallas_call(kernel, out_shape=[jax.ShapeDtypeStruct((tokens, chans), B...  113 us
    pallas_call x1, Pallas kernels, res_block_out(): pl.pallas_call(kernel, out_shape=jax.ShapeDtypeStruct((peers, band, chans...  103 us

profile of v9, /device:TPU:30, one launch (start us, length us, event | category | flops | bytes accessed | tf_op | source)
XLA Modules:
  0.0 330.5 jit_solution(15540760396378507748)
XLA Ops:
  0.0 113.1 %res_block_in.1 = (bf16[1024,1280]{1,0:T(8,128)(2,1)S(1)}, f32[16,1280]{1,0:T(8,128)S(1)}, f32[1,1280]{1,0:T(1,128)S(1)}, bf16[80,1280]{1,0:T(8,128)(2,1)S(1)}, bf16[1280,80]{1,0:T(8,128)(2,1)S(1)}) custom-call(bf16[16,64,1280]{2,1,0:T(8,128)(2,1)} %bitcast.24, bf16[16,1280]{1,0:T(8,128)(2,1)} %time_hbm.1, bf16[1232,2048]{1,0:T(8,128)(2,1)} %bitcast.20, ...), custom_call_target="tpu_custom_call" | custom-call | flops 60397977600 | bytes 58982400 | tf_op jit(solution)/shard_map/res_block_in/pallas_call | solution.py:408
  113.1 113.4 %transformer.1.x_ref = bf16[1024,1280]{1,0:T(8,128)(2,1)S(1)} custom-call(bf16[1024,1280]{1,0:T(8,128)(2,1)S(1)} %get-tuple-element.10.h_ref, bf16[80,1280]{1,0:T(8,128)(2,1)S(1)} %get-tuple-element.11.ctx_k, bf16[1280,80]{1,0:T(8,128)(2,1)S(1)} %get-tuple-element.12.ctx_v, f32[16,1280]{1,0:T(8,128)S(1)} %get-tuple-element.13.norm_ref, ...), custom_call_target="tpu_custom_call" | custom-call | flops 72477573120 | bytes 81920000 | tf_op jit(solution)/shard_map/transformer/pallas_call | solution.py:778
  226.5 102.5 %res_block_out.1 = bf16[16,64,1280]{2,1,0:T(8,128)(2,1)S(1)} custom-call(bf16[1024,1280]{1,0:T(8,128)(2,1)S(1)} %transformer.1.x_ref, f32[1,1280]{1,0:T(1,128)S(1)} %get-tuple-element.14.bias_ref, bf16[2,2,3,3,1280,1280]{5,4,3,2,1,0:T(8,128)(2,1)} %kern.3, f32[16,1280]{1,0:T(8,128)S(1)} %get-tuple-element.13.norm_ref), custom_call_target="tpu_custom_call" | custom-call | flops 60397977600 | bytes 58982400 | tf_op jit(solution)/shard_map/res_block_out/pallas_call | solution.py:526
  329.0 1.5 copy.17

commit v10 on v9

--- a/solution.py
+++ b/solution.py
@@ -14,6 +14,7 @@
 LN_EPS = 1e-5
 TM = 256
 CK = 256
+STEP = 64
 CROSS_PAIRS = 5
 VMEM_IN, VMEM_MID, VMEM_OUT = 53_000_000, 48_000_000, 49_000_000
 
@@ -66,11 +67,6 @@
     @pl.loop(1, peers)
     def _(step):
         pl.semaphore_signal(barrier, inc=1, device_id={'sp': lax.rem(me + step, peers)}, device_id_type=MESH)
-
-
-def both_ways(step, peers):
-    hop = lax.div(step + 1, 2)
-    return jnp.where(lax.rem(step, 2) == 1, hop, peers - hop)
 
 
 def await_peers(peers):
@@ -190,7 +186,6 @@
 def conv_rows(fetch, src, act, wbuf, coef, acc, width):
     tokens, chans = acc.shape
     chunks = chans // CK
-    acc[...] = jnp.zeros_like(acc)
 
     def build(chunk, tile):
         activate(src, act, coef, pl.multiple_of(chunk * CK, CK), CK, tile * TM, TM, width)
@@ -252,6 +247,7 @@
         rows = pl.ds(pl.multiple_of(idx * 64, 64), 64)
         rounded = (acc[rows, :] + bias).astype(BF16)
         mid[rows, :] = rounded
+        acc[rows, :] = jnp.zeros((STEP, acc.shape[1]), F32)
         vals = rounded.astype(F32).reshape(8, 8, acc.shape[1])
         return carry[0] + jnp.sum(vals, axis=0), carry[1] + jnp.sum(vals * vals, axis=0)
 
@@ -299,7 +295,7 @@
 
             @pl.loop(1, peers)
             def _(step):
-                peer = lax.rem(me + both_ways(step, peers), peers)
+                peer = lax.rem(me + step, peers)
                 remote(lat.at[peer, :, pl.ds(first, wide)], image.at[own_rows, pl.ds(first, wide)], send_sem.at[index], recv_sem.at[index], peer).start()
 
         send(0)
@@ -457,6 +453,7 @@
         clear_edges(act, width)
         member = members(chans, groups)
         row = 4 * which
+        acc[...] = jnp.zeros_like(acc)
         norm_from(x_ref, member, norm_ref, row, count, coef)
         conv_rows(lambda chunk: fetch_rows(kern, which, 0, chunk, wbuf, wsem), x_ref, act, wbuf, coef, acc, width)
         start_all(fetch_cols(kern, which, 1, 0, cbuf, csem))
@@ -596,7 +593,7 @@
         sums = group_sums(two_rows(tot, sqr), member)
         group_affine(sums, norm_ref[norm_row:norm_row + 1], norm_ref[norm_row + 1:norm_row + 2], member, count, coef, 1.0)
 
-        def project_rows(weight, src, base, normed_to):
+        def project_rows(weight, src, base, normed_to, clear=None):
             def norm_tile(tile):
                 rows = tile_rows(tile)
                 normed_to[rows, :] = layer_norm(tok[rows, :].astype(F32))
@@ -606,6 +603,8 @@
                 norm_tile(jnp.maximum(tile - 1, 0))
                 rows = tile_rows(tile)
                 tok[rows, :] = (base(rows) + nn(src(rows), weight[...])).astype(BF16)
+                if clear is not None:
+                    clear[rows, :] = jnp.zeros((TM, chans), F32)
 
             norm_tile(tiles - 1)
 
@@ -647,6 +646,7 @@
 
         halves = tokens // qw
         blocks = pairs * halves
+        unroll = next(count for count in (5, 4, 2, 1) if blocks % count == 0)
         scores = [acc.at[:, pl.ds(h * qw, qw)] for h in range(2)]
         probs = [out_ref.at[:, pl.ds(h * qw, qw)] for h in range(2)]
         parts = tokens // kb
@@ -707,11 +707,11 @@
             return top0, denom1, low
 
         def attend_blocks(step, carry):
-            for sub in range(4):
-                carry = attend_block(step * 4 + sub, carry)
+            for sub in range(unroll):
+                carry = attend_block(step * unroll + sub, carry)
             return carry
 
-        _, denom1, low = lax.fori_loop(0, blocks // 4, attend_blocks, (top_first, zero_row, zero_out))
+        _, denom1, low = lax.fori_loop(0, blocks // unroll, attend_blocks, (top_first, zero_row, zero_out))
         emit(blocks - 1, low, value_of(blocks - 1, 1, denom1))
 
         project_rows(take('o'), lambda rows: aux[rows, :], lambda rows: tok[rows, :].astype(F32), keys)
@@ -735,10 +735,9 @@
                     outs.append(nn(text_vals, weights.astype(BF16)) * (1.0 / denom))
                 aux[:, pair_cols(hp)] = jnp.concatenate(outs, axis=0).T.astype(BF16)
 
-        project_rows(take('co'), lambda rows: aux[rows, :], lambda rows: tok[rows, :].astype(F32), keys)
+        project_rows(take('co'), lambda rows: aux[rows, :], lambda rows: tok[rows, :].astype(F32), keys, acc)
         for copy in ff_copies(1, 1):
             copy.start()
-        acc[...] = jnp.zeros_like(acc)
 
         @loop(ff_steps)
         def _(step):

time: 332 us -> 330 us (level)
  no operation moved by 1% of the time
where the time goes in v10:
time: 330 us; the launch traced here: 328 us
  Pallas kernels  326 us (99%)
    pallas_call x1, Pallas kernels, transformer(): pl.pallas_call(kernel, out_shape=jax.ShapeDtypeStruct(hidden.shape, BF16)...  113 us
    pallas_call x1, Pallas kernels, res_block_in(): pl.pallas_call(kernel, out_shape=[jax.ShapeDtypeStruct((tokens, chans), B...  112 us
    pallas_call x1, Pallas kernels, res_block_out(): pl.pallas_call(kernel, out_shape=jax.ShapeDtypeStruct((peers, band, chans...  102 us

profile of v10, /device:TPU:30, one launch (start us, length us, event | category | flops | bytes accessed | tf_op | source)
XLA Modules:
  0.0 327.9 jit_solution(127359428999149231)
XLA Ops:
  0.0 111.8 %res_block_in.1 = (bf16[1024,1280]{1,0:T(8,128)(2,1)S(1)}, f32[16,1280]{1,0:T(8,128)S(1)}, f32[1,1280]{1,0:T(1,128)S(1)}, bf16[80,1280]{1,0:T(8,128)(2,1)S(1)}, bf16[1280,80]{1,0:T(8,128)(2,1)S(1)}) custom-call(bf16[16,64,1280]{2,1,0:T(8,128)(2,1)} %bitcast.24, bf16[16,1280]{1,0:T(8,128)(2,1)} %time_hbm.1, bf16[1232,2048]{1,0:T(8,128)(2,1)} %bitcast.20, ...), custom_call_target="tpu_custom_call" | custom-call | flops 60397977600 | bytes 58982400 | tf_op jit(solution)/shard_map/res_block_in/pallas_call | solution.py:404
  111.8 112.7 %transformer.1.x_ref = bf16[1024,1280]{1,0:T(8,128)(2,1)S(1)} custom-call(bf16[1024,1280]{1,0:T(8,128)(2,1)S(1)} %get-tuple-element.10.h_ref, bf16[80,1280]{1,0:T(8,128)(2,1)S(1)} %get-tuple-element.11.ctx_k, bf16[1280,80]{1,0:T(8,128)(2,1)S(1)} %get-tuple-element.12.ctx_v, f32[16,1280]{1,0:T(8,128)S(1)} %get-tuple-element.13.norm_ref, ...), custom_call_target="tpu_custom_call" | custom-call | flops 72477573120 | bytes 81920000 | tf_op jit(solution)/shard_map/transformer/pallas_call | solution.py:777
  224.6 101.8 %res_block_out.1 = bf16[16,64,1280]{2,1,0:T(8,128)(2,1)S(1)} custom-call(bf16[1024,1280]{1,0:T(8,128)(2,1)S(1)} %transformer.1.x_ref, f32[1,1280]{1,0:T(1,128)S(1)} %get-tuple-element.14.bias_ref, bf16[2,2,3,3,1280,1280]{5,4,3,2,1,0:T(8,128)(2,1)} %kern.3, f32[16,1280]{1,0:T(8,128)S(1)} %get-tuple-element.13.norm_ref), custom_call_target="tpu_custom_call" | custom-call | flops 60397977600 | bytes 58982400 | tf_op jit(solution)/shard_map/res_block_out/pallas_call | solution.py:523
  326.4 1.5 copy.17

commit v11 on v10

--- a/solution.py
+++ b/solution.py
@@ -67,6 +67,11 @@
     @pl.loop(1, peers)
     def _(step):
         pl.semaphore_signal(barrier, inc=1, device_id={'sp': lax.rem(me + step, peers)}, device_id_type=MESH)
+
+
+def far_first(step, peers):
+    hop = lax.div(step, 2)
+    return peers // 2 + jnp.where(lax.rem(step, 2) == 1, hop, -hop)
 
 
 def await_peers(peers):
@@ -295,7 +300,7 @@
 
             @pl.loop(1, peers)
             def _(step):
-                peer = lax.rem(me + step, peers)
+                peer = lax.rem(me + far_first(step, peers), peers)
                 remote(lat.at[peer, :, pl.ds(first, wide)], image.at[own_rows, pl.ds(first, wide)], send_sem.at[index], recv_sem.at[index], peer).start()
 
         send(0)

time: 330 us -> 329 us (level)
  no operation moved by 1% of the time
where the time goes in v11:
time: 329 us; the launch traced here: 327 us
  Pallas kernels  326 us (99%)
    pallas_call x1, Pallas kernels, transformer(): pl.pallas_call(kernel, out_shape=jax.ShapeDtypeStruct(hidden.shape, BF16)...  113 us
    pallas_call x1, Pallas kernels, res_block_in(): pl.pallas_call(kernel, out_shape=[jax.ShapeDtypeStruct((tokens, chans), B...  112 us
    pallas_call x1, Pallas kernels, res_block_out(): pl.pallas_call(kernel, out_shape=jax.ShapeDtypeStruct((peers, band, chans...  101 us

profile of v11, /device:TPU:30, one launch (start us, length us, event | category | flops | bytes accessed | tf_op | source)
XLA Modules:
  0.0 327.3 jit_solution(5653506433858736800)
XLA Ops:
  0.0 111.8 %res_block_in.1 = (bf16[1024,1280]{1,0:T(8,128)(2,1)S(1)}, f32[16,1280]{1,0:T(8,128)S(1)}, f32[1,1280]{1,0:T(1,128)S(1)}, bf16[80,1280]{1,0:T(8,128)(2,1)S(1)}, bf16[1280,80]{1,0:T(8,128)(2,1)S(1)}) custom-call(bf16[16,64,1280]{2,1,0:T(8,128)(2,1)} %bitcast.24, bf16[16,1280]{1,0:T(8,128)(2,1)} %time_hbm.1, bf16[1232,2048]{1,0:T(8,128)(2,1)} %bitcast.20, ...), custom_call_target="tpu_custom_call" | custom-call | flops 60397977600 | bytes 58982400 | tf_op jit(solution)/shard_map/res_block_in/pallas_call | solution.py:409
  111.8 112.7 %transformer.1.x_ref = bf16[1024,1280]{1,0:T(8,128)(2,1)S(1)} custom-call(bf16[1024,1280]{1,0:T(8,128)(2,1)S(1)} %get-tuple-element.10.h_ref, bf16[80,1280]{1,0:T(8,128)(2,1)S(1)} %get-tuple-element.11.ctx_k, bf16[1280,80]{1,0:T(8,128)(2,1)S(1)} %get-tuple-element.12.ctx_v, f32[16,1280]{1,0:T(8,128)S(1)} %get-tuple-element.13.norm_ref, ...), custom_call_target="tpu_custom_call" | custom-call | flops 72477573120 | bytes 81920000 | tf_op jit(solution)/shard_map/transformer/pallas_call | solution.py:782
  224.6 101.2 %res_block_out.1 = bf16[16,64,1280]{2,1,0:T(8,128)(2,1)S(1)} custom-call(bf16[1024,1280]{1,0:T(8,128)(2,1)S(1)} %transformer.1.x_ref, f32[1,1280]{1,0:T(1,128)S(1)} %get-tuple-element.14.bias_ref, bf16[2,2,3,3,1280,1280]{5,4,3,2,1,0:T(8,128)(2,1)} %kern.3, f32[16,1280]{1,0:T(8,128)S(1)} %get-tuple-element.13.norm_ref), custom_call_target="tpu_custom_call" | custom-call | flops 60397977600 | bytes 58982400 | tf_op jit(solution)/shard_map/res_block_out/pallas_call | solution.py:528
  325.8 1.5 copy.17
